TPU v7x, 32 devices: a whole 2x2x4 slice. The times are simulated.
32 devices in a mesh: mem: 4 (over z), lat: 8 (over y, x, core).
Axes of the slice: x: 2, y: 2, z: 4, core: 2. Of those that a mesh axis runs over, the one named last changes fastest.
Arguments:
- members: float32 [32, 2, 512, 1024], P('mem', None, 'lat'), may hold values from -0.75 to 0.75
- lat_root: float32 [512, 512], replicated, may hold values from -1 to 2
- lon_root: float32 [1024, 1024], replicated, may hold values from -1 to 2
- innovation: float32 [512, 256], P('lat', 'mem'), may hold values from -6 to 6
- obs_weight: float32 [512, 256], P('lat', 'mem'), may hold values from 0.5 to 4
- obs_mask: int32 [512, 256], P('lat', 'mem'), may hold values 0 or 1
- obs_cell: int32 [512, 256], P('lat', 'mem'), may hold values from 0 to 2047, as said below
Outputs:
- increment: float32 [2, 512, 1024], P(None, 'lat', 'mem')
- control: float32 [32, 2, 512, 1024], P('mem', None, 'lat')
Inputs may be any that keep to these rules, and one draw needn't show every extreme that they name: `obs_cell`: entry e in column c has (e % 1024) // 256 equal to c // 64.
All inputs are finite; a program needn't handle non-finite values. No bound on the sum of `obs_mask` on one device may be relied on, other than what follows from the above.
Results may differ from a plain program's by a relative error of at most 0.0003.
Values sent between devices are 32-bit elements; how exact they have to be, the bound alone decides.
No kernel may reach another device: no remote copies, remote signals or barrier semaphores. Data moves between devices by JAX's collectives and lax.ppermute only.
A program may use at most 128 MiB of HBM per device.

v0:
```python
import functools
import jax
import jax.numpy as jnp
from jax import lax
from jax.experimental import pallas as pl
from jax.experimental.pallas import tpu as pltpu
from jax.sharding import PartitionSpec as P


LANES = 128
HIGHEST = lax.Precision.HIGHEST
F32 = jnp.float32
BF16 = jnp.bfloat16
VMEM_LIMIT = 60 * 1024 * 1024


VM = pl.BlockSpec(memory_space=pltpu.VMEM)
ANY = pl.BlockSpec(memory_space=pl.ANY)


def params():
    return pltpu.CompilerParams(vmem_limit_bytes=VMEM_LIMIT)


def cost(flops, nbytes):
    return pl.CostEstimate(flops=flops, bytes_accessed=nbytes, transcendentals=0)


def take_lanes(values, index):
    numbers = lax.GatherDimensionNumbers(
        offset_dims=(),
        collapsed_slice_dims=(1,),
        start_index_map=(1,),
        operand_batching_dims=(0,),
        start_indices_batching_dims=(0,),
    )
    return lax.gather(
        values, index[..., None], numbers, slice_sizes=(1, 1), mode=lax.GatherScatterMode.PROMISE_IN_BOUNDS
    )


def split(value):
    high = value.astype(BF16)
    return high, (value - high.astype(F32)).astype(BF16)


def lane_iota(rows):
    return lax.broadcasted_iota(jnp.int32, (rows, LANES), 1)


def dot(a, b):
    return jnp.dot(a, b, preferred_element_type=F32)


def sort_kernel(cell_ref, weight_ref, mask_ref, innovation_ref, out_ref, cell, weight, value):
    rows, width = cell_ref.shape
    for scratch in (cell, weight, value):
        scratch[...] = jnp.zeros(scratch.shape, scratch.dtype)
    cell[:, :width] = cell_ref[...]
    used = weight_ref[...] * mask_ref[...].astype(F32)
    weight[:, :width] = used
    value[:, :width] = -(used * innovation_ref[...])
    lane = lane_iota(rows)
    key = cell[...] * width + lane % width
    block = 2
    while block <= width:
        hop = block // 2
        while hop:
            other = take_lanes(key, lane ^ hop)
            keep_low = ((lane & block) == 0) == ((lane & hop) == 0)
            if block == width:
                keep_low = (lane & hop) == 0
            key = jnp.where(keep_low, jnp.minimum(key, other), jnp.maximum(key, other))
            hop //= 2
        block *= 2
    slot = key % width
    per = LANES // width
    part = rows // per
    sorted_values = (
        (key // width).astype(F32),
        take_lanes(weight[...], slot),
        take_lanes(value[...], slot),
    )
    for kind, values in enumerate(sorted_values):
        values = jnp.where(lane < width, values, 0.0)
        total = values[:part]
        for side in range(1, per):
            total = total + pltpu.roll(values[side * part : (side + 1) * part], side * width, axis=1)
        out_ref[kind] = total


def run_totals(cells, values, width):
    hop = 1
    while hop < width:
        same = pltpu.roll(cells, LANES - hop, axis=1) == cells
        values = values + jnp.where(same, pltpu.roll(values, LANES - hop, axis=1), 0.0)
        hop *= 2
    return values


def pick_cells(cells, reads, width, levels, quarter, lon):
    per = LANES // width
    halves = quarter // LANES
    lane = lane_iota(cells.shape[0])
    position = cells % LANES
    kind = (cells // lon) * halves + (cells % quarter) // LANES
    outs = [jnp.zeros(cells.shape, F32) for _ in reads]
    for side in range(per):
        here = (lane // width) == side
        for level in range(levels):
            for half in range(halves):
                use = here & (kind == level * halves + half)
                outs = [
                    jnp.where(use, take_lanes(read(side, level, half), position), out)
                    for read, out in zip(reads, outs)
                ]
    return outs


def observe_kernel(width, nmem, *refs):
    block_refs, (members_ref, obs_ref, local_ref, mine_ref, other_ref, blocks) = refs[:nmem], refs[nmem:]
    _, part, _ = block_refs[0].shape
    count, levels, rows, lon = members_ref.shape
    me = lax.axis_index("mem")
    parity = lax.axis_index("lat") % 2
    per = LANES // width
    quarter = lon // nmem
    for hop, ref in enumerate(block_refs):
        blocks[lax.rem(me - hop + nmem, nmem)] = ref[...]
    lane = lane_iota(part)
    for group in range(nmem // per):
        columns = slice(group * LANES, (group + 1) * LANES)
        for kind in range(3):
            for piece in range(per):
                total = jnp.zeros((part, LANES), F32)
                for side in range(per):
                    raw = blocks[group * per + side, kind]
                    turn = ((side - piece) * width) % LANES
                    if turn:
                        raw = pltpu.roll(raw, turn, axis=1)
                    total = jnp.where(lane // width == side, raw, total)
                obs_ref[kind, piece * part : (piece + 1) * part, columns] = total
        cells = obs_ref[0, :, columns].astype(jnp.int32)
        local_ref[0, :, columns] = obs_ref[0, :, columns]
        local_ref[1, :, columns] = run_totals(cells, obs_ref[2, :, columns], width)

    step = 8
    half_count = count // 2

    def one(index, carry):
        start = pl.multiple_of(index * step, step)
        here = pl.ds(start, step)
        for group in range(nmem // per):
            columns = slice(group * LANES, (group + 1) * LANES)
            cells = obs_ref[0, here, columns].astype(jnp.int32)

            def reader(member):
                def read(side, level, half):
                    first = (group * per + side) * quarter + half * LANES
                    return members_ref[member, level, here, first : first + LANES]

                return read

            order = [parity * half_count + i for i in range(half_count)]
            order += [(1 - parity) * half_count + i for i in range(half_count)]
            outs = pick_cells(cells, [reader(member) for member in order], width, levels, quarter, lon)
            for i in range(half_count):
                mine_ref[i, here, columns] = outs[i]
                other_ref[i, here, columns] = outs[half_count + i]
        return carry

    lax.fori_loop(0, rows // step, one, 0)


def inverse_kernel(width, levels, lon, nblocks_lat, *refs):
    local_refs, (inverse_ref, value_ref, cells_all) = refs[:nblocks_lat], refs[nblocks_lat:]
    _, rows, slots = local_refs[0].shape
    nblocks = slots // width
    quarter = lon // nblocks
    per = LANES // width
    tall = 16
    for number, local_ref in enumerate(local_refs):
        value_ref[number * rows : (number + 1) * rows, :] = local_ref[1]
        cells_all[number * rows : (number + 1) * rows, :] = local_ref[0].astype(jnp.int32)

    def one(index, carry):
        here = pl.ds(pl.multiple_of(index * tall, tall), tall)
        lane = lane_iota(tall)
        for block in range(nblocks):
            group, offset = block // per, (block % per) * width
            cells = cells_all[here, group * LANES : (group + 1) * LANES]
            nothing = (offset - 1) % LANES
            for level in range(levels):
                for half in range(quarter // LANES):
                    target = lane + (level * lon + block * quarter + half * LANES)
                    place = jnp.full((tall, LANES), offset, jnp.int32)
                    hop = width // 2
                    while hop:
                        place = jnp.where(take_lanes(cells, place + (hop - 1)) < target, place + hop, place)
                        hop //= 2
                    found = take_lanes(cells, place) == target
                    inverse_ref[level * nblocks + block, here, half * LANES : (half + 1) * LANES] = jnp.where(
                        found, place, nothing
                    )
        return carry

    lax.fori_loop(0, cells_all.shape[0] // tall, one, 0)


def apply_kernel(width, levels, nlat_blocks, first, *refs):
    seen_refs = refs[:nlat_blocks]
    refs = refs[nlat_blocks:]
    if not first:
        pay_refs = refs[:nlat_blocks]
        refs = refs[nlat_blocks:]
    value_refs, inverse_refs = refs[:2], refs[2:4]
    lhs_high_ref, lhs_low_ref, local_refs, cn_high_ref, cn_low_ref = refs[4], refs[5], refs[6:8], refs[8], refs[9]
    members_ref, members_sib_ref = refs[10], refs[11]
    refs = refs[12:]
    seen_out_refs, image_refs = refs[:2], refs[2:4]
    back_high_refs, back_low_refs = refs[4:6], refs[6:8]
    refs = refs[8:]
    if not first:
        length_ref = refs[0]
        refs = refs[1:]
    (seen, value, inverse, cn_high, cn_low, members, xa_high, xa_low, xb_high, xb_low, w_high, w_low,
     back_high, back_low, sems, seen_sems, inv_sems, back_sems) = refs
    count, nlat, slots = seen.shape
    rows = nlat // nlat_blocks
    wide = 2 * rows
    nblocks = slots // width
    per = LANES // width
    nchunks = levels * nblocks
    quarter = inverse.shape[2]
    lon = quarter * nblocks
    parity = lax.axis_index("lat") % 2
    me_mem = lax.axis_index("mem")

    def rotated(block):
        return lax.rem(block - me_mem + nblocks, nblocks)

    seen_copies = [
        pltpu.make_async_copy(ref, seen.at[:, pl.ds(number * rows, rows)], seen_sems.at[number])
        for number, ref in enumerate(seen_refs)
    ]

    def inverse_copies(chunk):
        return [
            pltpu.make_async_copy(
                ref.at[chunk], inverse.at[chunk, pl.ds(side * (nlat // 2), nlat // 2)], inv_sems.at[chunk, side]
            )
            for side, ref in enumerate(inverse_refs)
        ]

    late = [
        pltpu.make_async_copy(cn_high_ref, cn_high, sems.at[0]),
        pltpu.make_async_copy(cn_low_ref, cn_low, sems.at[1]),
        pltpu.make_async_copy(members_ref.at[pl.ds(parity * count, count)], members.at[0], sems.at[2]),
        pltpu.make_async_copy(members_sib_ref.at[pl.ds(parity * count, count)], members.at[1], sems.at[3]),
    ]
    for copy in inverse_copies(0) + seen_copies:
        copy.start()
    for chunk in range(1, nchunks):
        for copy in inverse_copies(chunk):
            copy.start()
    for copy in late:
        copy.start()

    if first:
        for side, ref in enumerate(value_refs):
            value[side * (nlat // 2) : (side + 1) * (nlat // 2), :] = ref[...]
    else:
        top = jnp.zeros((1, slots), F32)
        bottom = jnp.zeros((1, slots), F32)
        for ref in pay_refs:
            top = top + ref[rows : rows + 1, :]
            bottom = bottom + ref[rows + 1 : rows + 2, :]
        length = jnp.sum(top, axis=1, keepdims=True) / jnp.sum(bottom, axis=1, keepdims=True)
        length_ref[...] = jnp.broadcast_to(length, length_ref.shape)
        per_side = nlat_blocks // 2
        for number, ref in enumerate(pay_refs):
            inside = (number % per_side) * rows
            old = value_refs[number // per_side][inside : inside + rows, :]
            value[number * rows : (number + 1) * rows, :] = old - length * (old + ref[:rows, :])

    tall = 16
    lane = lane_iota(tall)

    def build(chunk, x_high, x_low):
        block = lax.rem(chunk, nblocks)
        offset = lax.rem(block, per) * width
        columns = pl.ds(pl.multiple_of((block // per) * LANES, LANES), LANES)
        inside = (lane >= offset) & (lane < offset + width)
        for start in range(0, nlat, tall):
            part = slice(start, start + tall)
            numbers = value[part, columns]
            sources = [jnp.where(inside, seen[m, part, columns] * numbers, 0.0) for m in range(count)]
            for half in range(quarter // LANES):
                cols = slice(half * LANES, (half + 1) * LANES)
                index = inverse[chunk, part, cols]
                for m in range(count):
                    high, low = split(take_lanes(sources[m], index))
                    x_high[m, part, cols] = high
                    x_low[m, part, cols] = low

    def multiply(chunk, x_high, x_low):
        level = chunk // nblocks
        cols = pl.ds(pl.multiple_of(lax.rem(chunk, nblocks) * quarter, quarter), quarter)
        for m in range(count):
            both = (
                dot(lhs_high_ref[...], x_high[m])
                + dot(lhs_low_ref[...], x_high[m])
                + dot(lhs_high_ref[...], x_low[m])
            )
            high, low = split(both[:wide])
            where = pl.ds(pl.multiple_of((m * levels + level) * wide, wide), wide)
            w_high[where, cols] = high
            w_low[where, cols] = low
            where = pl.ds(pl.multiple_of((m * levels + level) * rows, rows), rows)
            for side in range(2):
                high, low = split(both[wide + side * rows : wide + (side + 1) * rows])
                back_high[side, where, cols] = high
                back_low[side, where, cols] = low

    for copy in inverse_copies(0) + seen_copies:
        copy.wait()
    build(0, xa_high, xa_low)

    def one(pair, carry):
        chunk = pair * 2
        for copy in inverse_copies(chunk + 1):
            copy.wait()

        @pl.when(chunk + 2 < nchunks)
        def _():
            for copy in inverse_copies(chunk + 2):
                copy.wait()

        build(chunk + 1, xb_high, xb_low)
        multiply(chunk, xa_high, xa_low)
        build(jnp.minimum(chunk + 2, nchunks - 1), xa_high, xa_low)
        multiply(chunk + 1, xb_high, xb_low)
        return carry

    lax.fori_loop(0, nchunks // 2, one, 0)

    back_copies = [
        pltpu.make_async_copy(source.at[side], refs_[side], back_sems.at[kind, side])
        for kind, (source, refs_) in enumerate(((back_high, back_high_refs), (back_low, back_low_refs)))
        for side in range(2)
    ]
    for copy in back_copies:
        copy.start()
    for copy in late:
        copy.wait()
    tile = 2 * LANES
    deep = levels * wide

    for column in range(lon // tile):
        cols = slice(column * tile, (column + 1) * tile)
        place = rotated(column * tile // quarter)
        inner = slice(column * tile % quarter, column * tile % quarter + tile)
        for member in range(count):
            part = slice(member * deep, (member + 1) * deep)
            product = (
                dot(w_high[part, :], cn_high[:, cols])
                + dot(w_low[part, :], cn_high[:, cols])
                + dot(w_high[part, :], cn_low[:, cols])
            )
            for level in range(levels):
                for side in range(2):
                    begin = level * wide + side * rows
                    term = members[side, member, level, :, cols] * product[begin : begin + rows]
                    if member == 0:
                        image_refs[side][place, level, :, inner] = term
                    else:
                        image_refs[side][place, level, :, inner] += term

    step = 8
    for side in range(2):
        for start in range(0, rows, step):
            part = slice(start, start + step)
            for group in range(nblocks // per):
                columns = slice(group * LANES, (group + 1) * LANES)
                cells = local_refs[side][0, part, columns].astype(jnp.int32)

                def read(piece, level, half):
                    return image_refs[side][
                        rotated(group * per + piece), level, part, half * LANES : (half + 1) * LANES
                    ]

                seen_out_refs[side][part, columns] = pick_cells(cells, [read], width, levels, quarter, lon)[0]
    for copy in back_copies:
        copy.wait()


def answer_kernel(width, nparts, *refs):
    parts, (obs_ref, pay_ref, seen_ref) = refs[:nparts], refs[nparts:]
    rows = obs_ref.shape[1]
    seen = parts[0][...]
    for part in parts[1:]:
        seen = seen + part[...]
    seen_ref[...] = seen
    weighted = obs_ref[1] * seen
    value = obs_ref[2]
    for group in range(seen.shape[1] // LANES):
        columns = slice(group * LANES, (group + 1) * LANES)
        cells = obs_ref[0, :, columns].astype(jnp.int32)
        pay_ref[:rows, columns] = run_totals(cells, weighted[:, columns], width)
    pay_ref[rows:, :] = jnp.zeros((8, seen.shape[1]), F32)
    pay_ref[rows : rows + 1, :] = jnp.sum(value * seen, axis=0, keepdims=True)
    pay_ref[rows + 1 : rows + 2, :] = jnp.sum(seen * (value + weighted), axis=0, keepdims=True)


def last_kernel(nparts, *refs):
    parts, (obs_ref, before_ref, length_ref, dots_ref) = refs[:nparts], refs[nparts:]
    seen = parts[0][...]
    for part in parts[1:]:
        seen = seen + part[...]
    weight, value = obs_ref[1], obs_ref[2]
    length = length_ref[:1, :1]
    value = value - length * (value + weight * before_ref[...])
    dots_ref[...] = jnp.zeros(dots_ref.shape, F32)
    dots_ref[:1, :] = jnp.sum(value * seen, axis=0, keepdims=True)
    dots_ref[1:2, :] = jnp.sum(seen * (value + weight * seen), axis=0, keepdims=True)


def lat_kernel(order, root_ref, high_ref, low_ref, turned, chip, columns, ordered):
    rows = chip.shape[0] // 2
    me = lax.axis_index("lat")
    turned[...] = root_ref[...].T
    for side in range(2):
        here = pl.ds(pl.multiple_of((me ^ side) * rows, rows), rows)
        chip[side * rows : (side + 1) * rows, :] = root_ref[here, :]
        columns[side * rows : (side + 1) * rows, :] = turned[here, :]
    covariance = lax.dot_general(
        chip[...], root_ref[...], (((1,), (1,)), ((), ())), precision=HIGHEST, preferred_element_type=F32
    )
    both = jnp.concatenate([covariance, columns[...]]).T
    turned[:, : both.shape[1]] = both
    for number, bits in enumerate(order):
        here = pl.ds(pl.multiple_of((me ^ bits) * rows, rows), rows)
        ordered[number * rows : (number + 1) * rows, :] = turned[here, : both.shape[1]]
    high_ref[...], low_ref[...] = split(ordered[...].T)


def covariance_kernel(root_ref, high_ref, low_ref, root_high_ref, root_low_ref):
    lon = root_ref.shape[0]
    root_high_ref[...], root_low_ref[...] = split(root_ref[...])
    tile = 2 * LANES
    numbers = (((1,), (1,)), ((), ()))

    def times(a, b):
        return lax.dot_general(a, b, numbers, preferred_element_type=F32)

    for column in range(lon // tile):
        cols = slice(column * tile, (column + 1) * tile)
        high, low = root_high_ref[cols, :], root_low_ref[cols, :]
        total = times(root_high_ref[...], high) + times(root_low_ref[...], high) + times(root_high_ref[...], low)
        high_ref[:, cols], low_ref[:, cols] = split(total)


def product_kernel(a_high_ref, a_low_ref, b_high_ref, b_low_ref, out_ref):
    out_ref[...] = (
        dot(a_high_ref[...], b_high_ref[...])
        + dot(a_low_ref[...], b_high_ref[...])
        + dot(a_high_ref[...], b_low_ref[...])
    )


def product(a_high, a_low, b_high, b_low):
    rows, deep = a_high.shape
    wide = b_high.shape[1]
    tile = 2 * LANES
    whole = pl.BlockSpec((rows, deep), lambda i: (0, 0))
    panel = pl.BlockSpec((deep, tile), lambda i: (0, i))
    return pl.pallas_call(
        product_kernel,
        grid=(wide // tile,),
        in_specs=[whole, whole, panel, panel],
        out_specs=pl.BlockSpec((rows, tile), lambda i: (0, i)),
        out_shape=jax.ShapeDtypeStruct((rows, wide), F32),
        compiler_params=params(),
        cost_estimate=cost(6 * rows * deep * wide, 4 * (rows * deep + deep * wide + rows * wide)),
        name="lon_product",
    )(a_high, a_low, b_high, b_low)


def final_kernel(parity_ref, dots_ref, length_ref, q0_ref, q1_ref, a0_ref, b0_ref, a1_ref, b1_ref,
                 increment_ref, control_ref, lengths):
    index = pl.program_id(0)

    @pl.when(index == 0)
    def _():
        top = jnp.sum(dots_ref[:1, :], axis=1, keepdims=True)
        bottom = jnp.sum(dots_ref[1:2, :], axis=1, keepdims=True)
        lengths[0] = length_ref[...]
        lengths[1] = jnp.broadcast_to(top / bottom, length_ref.shape)
        increment_ref[...] = -(lengths[0, :1, :1] * q0_ref[...] + lengths[1, :1, :1] * q1_ref[...])

    half = pl.num_programs(0) // 2

    @pl.when(index < half)
    def _():
        control_ref[...] = -(lengths[0, :1, :1] * a0_ref[...] + lengths[1, :1, :1] * a1_ref[...])

    @pl.when(index >= half)
    def _():
        control_ref[...] = -(lengths[0, :1, :1] * b0_ref[...] + lengths[1, :1, :1] * b1_ref[...])


def per_device(members, lat_root, lon_root, innovation, obs_weight, obs_mask, obs_cell):
    count, levels, rows, lon = members.shape
    half_count = count // 2
    nmem, nlat_dev = lax.axis_size("mem"), lax.axis_size("lat")
    nlat = lat_root.shape[0]
    width = obs_cell.shape[1]
    slots = width * nmem
    quarter = lon // nmem
    me_lat = lax.axis_index("lat")
    parity = me_lat % 2
    shape = jax.ShapeDtypeStruct
    chips = list(range(0, nlat_dev, 2))
    order = chips + [bits + 1 for bits in chips]

    def swap(value, bits):
        return lax.ppermute(value, "lat", [(i, i ^ bits) for i in range(nlat_dev)])

    def direct(value):
        return [value] + [swap(value, bits) for bits in chips[1:]]

    def around_mem(value):
        return [value] + [
            lax.ppermute(value, "mem", [(i, (i + hop) % nmem) for i in range(nmem)]) for hop in range(1, nmem)
        ]

    block = pl.pallas_call(
        sort_kernel,
        in_specs=[VM] * 4,
        out_specs=VM,
        out_shape=shape((3, rows * width // LANES, LANES), F32),
        scratch_shapes=[pltpu.VMEM((rows, LANES), jnp.int32)] + [pltpu.VMEM((rows, LANES), F32)] * 2,
        compiler_params=params(),
        name="sort_slots",
    )(obs_cell, obs_weight, obs_mask, innovation)
    blocks = around_mem(block)
    obs, local, mine, other = pl.pallas_call(
        functools.partial(observe_kernel, width, nmem),
        in_specs=[VM] * (nmem + 1),
        out_specs=[VM] * 4,
        out_shape=[
            shape((3, rows, slots), F32),
            shape((2, rows, slots), F32),
            shape((half_count, rows, slots), F32),
            shape((half_count, rows, slots), F32),
        ],
        scratch_shapes=[pltpu.VMEM((nmem, *block.shape), F32)],
        compiler_params=params(),
        cost_estimate=cost(10**8, 4 * members.size),
        name="members_at_slots",
    )(*blocks, members)

    locals_ = direct(local)
    local_sib = swap(local, 1)
    received = swap(other, 1)
    seens = direct(mine) + direct(received)
    members_sib = swap(members, 1)

    lhs_high, lhs_low = pl.pallas_call(
        functools.partial(lat_kernel, order),
        in_specs=[VM],
        out_specs=[VM] * 2,
        out_shape=[shape((4 * rows, nlat), BF16)] * 2,
        scratch_shapes=[
            pltpu.VMEM((nlat, nlat), F32),
            pltpu.VMEM((2 * rows, nlat), F32),
            pltpu.VMEM((2 * rows, nlat), F32),
            pltpu.VMEM((nlat, 4 * rows), F32),
        ],
        compiler_params=params(),
        cost_estimate=cost(3 * 10**9, 8 * nlat * nlat),
        name="lat_rows",
    )(lat_root)
    cn_high, cn_low, lon_high, lon_low = pl.pallas_call(
        covariance_kernel,
        in_specs=[VM],
        out_specs=[VM] * 4,
        out_shape=[shape((lon, lon), BF16)] * 4,
        compiler_params=params(),
        cost_estimate=cost(6 * lon**3, 12 * lon * lon),
        name="lon_covariance",
    )(lon_root)

    nchunks = levels * nmem
    inverse, value = pl.pallas_call(
        functools.partial(inverse_kernel, width, levels, lon, nlat_dev // 2),
        in_specs=[VM] * (nlat_dev // 2),
        out_specs=[VM] * 2,
        out_shape=[shape((nchunks, nlat // 2, quarter), jnp.int32), shape((nlat // 2, slots), F32)],
        scratch_shapes=[pltpu.VMEM((nlat // 2, slots), jnp.int32)],
        compiler_params=params(),
        cost_estimate=cost(10**10, 2 * nlat * lon * levels),
        name="inverse",
    )(*locals_)
    inverses, values = [inverse, swap(inverse, 1)], [value, swap(value, 1)]

    tall = half_count * levels * rows

    def apply(pays):
        first = pays is None
        outs = (
            [shape((rows, slots), F32)] * 2
            + [shape((nmem, levels, rows, quarter), F32)] * 2
            + [shape((tall, lon), BF16)] * 4
        )
        if not first:
            outs.append(shape((8, LANES), F32))
        return pl.pallas_call(
            functools.partial(apply_kernel, width, levels, nlat_dev, first),
            in_specs=[ANY] * nlat_dev
            + ([] if first else [VM] * nlat_dev)
            + [VM] * 2
            + [ANY] * 2
            + [VM] * 4
            + [ANY] * 4,
            out_specs=[VM] * 4 + [ANY] * 4 + [VM] * (len(outs) - 8),
            out_shape=outs,
            scratch_shapes=[
                pltpu.VMEM((half_count, nlat, slots), F32),
                pltpu.VMEM((nlat, slots), F32),
                pltpu.VMEM((nchunks, nlat, quarter), jnp.int32),
                pltpu.VMEM((lon, lon), BF16),
                pltpu.VMEM((lon, lon), BF16),
                pltpu.VMEM((2, half_count, levels, rows, lon), F32),
            ]
            + [pltpu.VMEM((half_count, nlat, quarter), BF16)] * 4
            + [pltpu.VMEM((2 * tall, lon), BF16)] * 2
            + [pltpu.VMEM((2, tall, lon), BF16)] * 2
            + [
                pltpu.SemaphoreType.DMA((4,)),
                pltpu.SemaphoreType.DMA((nlat_dev,)),
                pltpu.SemaphoreType.DMA((nchunks, 2)),
                pltpu.SemaphoreType.DMA((2, 2)),
            ],
            compiler_params=params(),
            cost_estimate=cost(12 * tall * lon * (nlat + lon), 30 * 2**20),
            name="apply_first" if first else "apply_next",
        )(
            *seens,
            *([] if first else pays),
            *values,
            *inverses,
            lhs_high,
            lhs_low,
            local,
            local_sib,
            cn_high,
            cn_low,
            members,
            members_sib,
        )

    def to_quarters(image):
        total = image[0]
        for hop in range(1, nmem):
            total = total + lax.ppermute(image[hop], "mem", [(i, (i + hop) % nmem) for i in range(nmem)])
        return total

    def gradient(backs):
        field = (half_count, levels, rows, lon)
        other = product(backs[1], backs[3], lon_high, lon_low)
        mine = product(backs[0], backs[2], lon_high, lon_low)
        return mine.reshape(field), other.reshape(field)

    seen_own, seen_sib, image_own, image_sib, *backs0 = apply(None)
    seen_own = seen_own + swap(seen_sib, 1)
    parts = around_mem(seen_own)
    image_sib = swap(image_sib, 1)
    pay, seen0 = pl.pallas_call(
        functools.partial(answer_kernel, width, nmem),
        in_specs=[VM] * (nmem + 1),
        out_specs=[VM] * 2,
        out_shape=[shape((rows + 8, slots), F32), shape((rows, slots), F32)],
        compiler_params=params(),
        name="answer",
    )(*parts, obs)
    pays = direct(pay)
    mine0, other0 = gradient(backs0)
    pays = pays + [swap(block, 1) for block in pays]
    other0 = swap(other0, 1)
    quarter0 = to_quarters(image_own + image_sib)

    seen_own, seen_sib, image_own, image_sib, *backs1, length0 = apply(pays)
    seen_own = seen_own + swap(seen_sib, 1)
    parts = around_mem(seen_own)
    mine1, other1 = gradient(backs1)
    image_sib = swap(image_sib, 1)
    dots = pl.pallas_call(
        functools.partial(last_kernel, nmem),
        in_specs=[VM] * (nmem + 3),
        out_specs=VM,
        out_shape=shape((8, slots), F32),
        compiler_params=params(),
        name="last_dots",
    )(*parts, obs, seen0, length0)
    other1 = swap(other1, 1)
    quarter1 = to_quarters(image_own + image_sib)
    dots_parts = direct(dots)
    dots = sum(dots_parts[1:], dots_parts[0])
    dots = dots + swap(dots, 1)

    small = pl.BlockSpec((8, slots), lambda i, par: (0, 0))
    tiny = pl.BlockSpec((8, LANES), lambda i, par: (0, 0))
    piece = pl.BlockSpec((levels, rows, quarter), lambda i, par: (0, 0, 0))
    near = pl.BlockSpec((1, levels, rows, lon), lambda i, par: (jnp.minimum(i, half_count - 1), 0, 0, 0))
    far = pl.BlockSpec((1, levels, rows, lon), lambda i, par: (jnp.maximum(i - half_count, 0), 0, 0, 0))
    put = pl.BlockSpec((1, levels, rows, lon), lambda i, par: ((i + par[0] * half_count) % count, 0, 0, 0))
    return pl.pallas_call(
        final_kernel,
        grid_spec=pltpu.PrefetchScalarGridSpec(
            num_scalar_prefetch=1,
            grid=(count,),
            in_specs=[small, tiny, piece, piece, near, far, near, far],
            out_specs=[piece, put],
            scratch_shapes=[pltpu.VMEM((2, 8, LANES), F32)],
        ),
        out_shape=[shape((levels, rows, quarter), F32), shape(members.shape, F32)],
        compiler_params=params(),
        name="final",
    )(parity[None], dots, length0, quarter0, quarter1, mine0, other0, mine1, other1)


def solution(mesh):
    return jax.shard_map(
        per_device,
        mesh=mesh,
        in_specs=(
            P("mem", None, "lat", None),
            P(),
            P(),
            P("lat", "mem"),
            P("lat", "mem"),
            P("lat", "mem"),
            P("lat", "mem"),
        ),
        out_specs=(P(None, "lat", "mem"), P("mem", None, "lat", None)),
        check_vma=False,
    )
```

profile of v0, /device:TPU:0, one launch (start us, length us, event | category | flops | bytes accessed | tf_op | source)
XLA Modules:
  0.0 246.0 jit_solution(12228380180666239754)
XLA Ops:
  1.2 3.1 %sort_slots.1.refs_0_ = f32[3,32,128]{2,1,0:T(8,128)} custom-call(s32[64,64]{1,0:T(8,128)} %cell_ref.1, f32[64,64]{1,0:T(8,128)} %weight_ref.1, s32[64,64]{1,0:T(8,128)} %mask_ref.1, f32[64,64]{1,0:T(8,128)} %innovation_ref.1), custom_call_target="tpu_custom_call" | custom-call | tf_op jit(solution)/shard_map/sort_slots/pallas_call | solution.py:537
  6.8 2.6 %collective-permute-start.1 = (f32[3,32,128]{2,1,0:T(8,128)}, f32[3,32,128]{2,1,0:T(8,128)S(1)}, u32[]{:S(2)}, u32[]{:S(2)}) collective-permute-start(f32[3,32,128]{2,1,0:T(8,128)} %sort_slots.1.refs_0_), channel_id=1, source_target_pairs={{0,16},{8,24},{16,0},{24,8},{1,17},{9,25},{17,1},{25,9},{2,18},{10... | collective-permute-start | bytes 147464 | tf_op jit(solution)/shard_map/ppermute | solution.py:534
  14.9 5.4 %members_at_slots.1 = (f32[3,64,256]{2,1,0:T(8,128)}, f32[2,64,256]{2,1,0:T(8,128)}, f32[4,64,256]{2,1,0:T(8,128)}, f32[4,64,256]{2,1,0:T(8,128)}) custom-call(f32[3,32,128]{2,1,0:T(8,128)} %sort_slots.1.refs_0_, f32[3,32,128]{2,1,0:T(8,128)} %copy-done.12, f32[3,32,128]{2,1,0:T(8,128)} %copy-done.13, f32[3,32,128]{2,1,0:T(8,128)} %copy-done.14, ...), custom_call_target="tpu_custom_call" | custom-call | flops 100000000 | bytes 4194304 | tf_op jit(solution)/shard_map/members_at_slots/pallas_call | solution.py:547
  26.3 3.6 %collective-permute-done.11.refs_2_ = f32[2,64,256]{2,1,0:T(8,128)S(1)} collective-permute-done((f32[2,64,256]{2,1,0:T(8,128)}, f32[2,64,256]{2,1,0:T(8,128)S(1)}, u32[]{:S(2)}, u32[]{:S(2)}) %collective-permute-start.11) | collective-permute-done | bytes 131104 | tf_op jit(solution)/shard_map/ppermute | solution.py:527
  31.2 13.2 %inverse.1 = (s32[8,256,256]{2,1,0:T(8,128)}, f32[256,256]{1,0:T(8,128)}) custom-call(f32[2,64,256]{2,1,0:T(8,128)} %get-tuple-element.35.refs_0_.refs_14_.refs_22_, f32[2,64,256]{2,1,0:T(8,128)} %copy-done.28, f32[2,64,256]{2,1,0:T(8,128)} %copy-done.29, f32[2,64,256]{2,1,0:T(8,128)} %copy-done.30), custom_call_target="tpu_custom_call" | custom-call | flops 10000000000 | bytes 2097152 | tf_op jit(solution)/shard_map/inverse/pallas_call | solution.py:595
  45.6 4.0 %collective-permute-done.15.refs_15_.refs_23_ = f32[2,64,256]{2,1,0:T(8,128)} collective-permute-done((f32[2,64,256]{2,1,0:T(8,128)S(1)}, f32[2,64,256]{2,1,0:T(8,128)}, u32[]{:S(2)}, u32[]{:S(2)}) %collective-permute-start.15) | collective-permute-done | bytes 131104 | tf_op jit(solution)/shard_map/ppermute | solution.py:527
  53.3 11.6 %lon_covariance.1 = (bf16[1024,1024]{1,0:T(8,128)(2,1)}, bf16[1024,1024]{1,0:T(8,128)(2,1)}, bf16[1024,1024]{1,0:T(8,128)(2,1)}, bf16[1024,1024]{1,0:T(8,128)(2,1)}) custom-call(f32[1024,1024]{1,0:T(8,128)} %root_ref.3), custom_call_target="tpu_custom_call" | custom-call | flops 6442450944 | bytes 12582912 | tf_op jit(solution)/shard_map/lon_covariance/pallas_call | solution.py:584
  68.6 3.5 %lat_rows.1 = (bf16[256,512]{1,0:T(8,128)(2,1)}, bf16[256,512]{1,0:T(8,128)(2,1)}) custom-call(f32[512,512]{1,0:T(8,128)} %root_ref.2), custom_call_target="tpu_custom_call" | custom-call | flops 3000000000 | bytes 2097152 | tf_op jit(solution)/shard_map/lat_rows/pallas_call | solution.py:569
  74.2 4.4 %collective-permute-done.8.refs_6_ = f32[4,64,256]{2,1,0:T(8,128)S(1)} collective-permute-done((f32[4,64,256]{2,1,0:T(8,128)S(1)}, f32[4,64,256]{2,1,0:T(8,128)S(1)}, u32[]{:S(2)}, u32[]{:S(2)}) %collective-permute-start.8) | collective-permute-done | bytes 262176 | tf_op jit(solution)/shard_map/ppermute | solution.py:527
  81.6 26.0 %apply_first.1 = (f32[64,256]{1,0:T(8,128)}, f32[64,256]{1,0:T(8,128)}, f32[4,2,64,256]{3,2,1,0:T(8,128)}, f32[4,2,64,256]{3,2,1,0:T(8,128)}, bf16[512,1024]{1,0...) custom-call(f32[4,64,256]{2,1,0:T(8,128)} %get-tuple-element.33.refs_0_, ...), custom_call_target="tpu_custom_call" | custom-call | flops 9663676416 | bytes 31457280 | tf_op jit(solution)/shard_map/apply_first/pallas_call | solution.py:618
  113.9 3.0 %collective-permute-done.18.refs_1_ = f32[64,256]{1,0:T(8,128)S(1)} collective-permute-done((f32[64,256]{1,0:T(8,128)S(1)}, f32[64,256]{1,0:T(8,128)S(1)}, u32[]{:S(2)}, u32[]{:S(2)}) %collective-permute-start.18) | collective-permute-done | bytes 65568 | tf_op jit(solution)/shard_map/ppermute | solution.py:534
  129.6 7.4 %lon_product.5 = f32[512,1024]{1,0:T(8,128)} custom-call(bf16[512,1024]{1,0:T(8,128)(2,1)} %get-tuple-element.58.a_high_ref, bf16[512,1024]{1,0:T(8,128)(2,1)} %get-tuple-element.59.a_low_ref, bf16[1024,1024]{1,0:T(8,128)(2,1)} %get-tuple-element.56.b_high_ref, bf16[1024,1024]{1,0:T(8,128)(2,1)} %get-tuple-element.57.b_low_ref), custom_call_target="tpu_custom_call" | custom-call | flops 3221225472 | bytes 8388608 | tf_op jit(solution)/shard_map/lon_product/pallas_call | solution.py:477
  138.7 26.7 %apply_next.1 = (f32[64,256]{1,0:T(8,128)}, f32[64,256]{1,0:T(8,128)}, f32[4,2,64,256]{3,2,1,0:T(8,128)}, f32[4,2,64,256]{3,2,1,0:T(8,128)}, bf16[512,1024]{1,0:...) custom-call(f32[4,64,256]{2,1,0:T(8,128)} %get-tuple-element.33.refs, ...), custom_call_target="tpu_custom_call" | custom-call | flops 9663676416 | bytes 31457280 | tf_op jit(solution)/shard_map/apply_next/pallas_call | solution.py:618
  165.4 7.2 %lon_product.7 = f32[512,1024]{1,0:T(8,128)} custom-call(bf16[512,1024]{1,0:T(8,128)(2,1)} %get-tuple-element.62.a_high_ref, bf16[512,1024]{1,0:T(8,128)(2,1)} %get-tuple-element.63.a_low_ref, bf16[1024,1024]{1,0:T(8,128)(2,1)} %get-tuple-element.56.b_high_ref, bf16[1024,1024]{1,0:T(8,128)(2,1)} %get-tuple-element.57.b_low_ref), custom_call_target="tpu_custom_call" | custom-call | flops 3221225472 | bytes 8388608 | tf_op jit(solution)/shard_map/lon_product/pallas_call | solution.py:477
  173.1 4.0 %collective-permute-done.28 = f32[64,256]{1,0:T(8,128)S(1)} collective-permute-done((f32[64,256]{1,0:T(8,128)S(1)}, f32[64,256]{1,0:T(8,128)S(1)}, u32[]{:S(2)}, u32[]{:S(2)}) %collective-permute-start.28) | collective-permute-done | bytes 65568 | tf_op jit(solution)/shard_map/ppermute | solution.py:527
  181.3 2.7 %collective-permute-done.29.refs_1_ = f32[64,256]{1,0:T(8,128)S(1)} collective-permute-done((f32[64,256]{1,0:T(8,128)S(1)}, f32[64,256]{1,0:T(8,128)S(1)}, u32[]{:S(2)}, u32[]{:S(2)}) %collective-permute-start.29) | collective-permute-done | bytes 65568 | tf_op jit(solution)/shard_map/ppermute | solution.py:534
  192.0 7.2 %lon_product.4 = f32[512,1024]{1,0:T(8,128)} custom-call(bf16[512,1024]{1,0:T(8,128)(2,1)} %get-tuple-element.54.a_high_ref, bf16[512,1024]{1,0:T(8,128)(2,1)} %get-tuple-element.55.a_low_ref, bf16[1024,1024]{1,0:T(8,128)(2,1)} %get-tuple-element.56.b_high_ref, bf16[1024,1024]{1,0:T(8,128)(2,1)} %get-tuple-element.57.b_low_ref), custom_call_target="tpu_custom_call" | custom-call | flops 3221225472 | bytes 8388608 | tf_op jit(solution)/shard_map/lon_product/pallas_call | solution.py:477
  199.9 7.2 %lon_product.6 = f32[512,1024]{1,0:T(8,128)} custom-call(bf16[512,1024]{1,0:T(8,128)(2,1)} %get-tuple-element.60.a_high_ref, bf16[512,1024]{1,0:T(8,128)(2,1)} %get-tuple-element.61.a_low_ref, bf16[1024,1024]{1,0:T(8,128)(2,1)} %get-tuple-element.56.b_high_ref, bf16[1024,1024]{1,0:T(8,128)(2,1)} %get-tuple-element.57.b_low_ref), custom_call_target="tpu_custom_call" | custom-call | flops 3221225472 | bytes 8388608 | tf_op jit(solution)/shard_map/lon_product/pallas_call | solution.py:477
  212.4 3.9 %collective-permute-done.37 = f32[2,64,256]{2,1,0:T(8,128)S(1)} collective-permute-done((f32[2,64,256]{2,1,0:T(8,128)S(1)}, f32[2,64,256]{2,1,0:T(8,128)S(1)}, u32[]{:S(2)}, u32[]{:S(2)}) %collective-permute-start.37) | collective-permute-done | bytes 131104 | tf_op jit(solution)/shard_map/ppermute | solution.py:666
  216.2 5.6 %collective-permute-done.38 = f32[2,64,256]{2,1,0:T(8,128)S(1)} collective-permute-done((f32[2,64,256]{2,1,0:T(8,128)S(1)}, f32[2,64,256]{2,1,0:T(8,128)S(1)}, u32[]{:S(2)}, u32[]{:S(2)}) %collective-permute-start.38) | collective-permute-done | bytes 131104 | tf_op jit(solution)/shard_map/ppermute | solution.py:666
  221.8 3.1 %collective-permute-start.43 = (f32[2,64,256]{2,1,0:T(8,128)S(1)}, f32[2,64,256]{2,1,0:T(8,128)S(1)}, u32[]{:S(2)}, u32[]{:S(2)}) collective-permute-start(f32[2,64,256]{2,1,0:T(8,128)S(1)} %get-tuple-element.65), channel_id=1, source_target_pairs={{0,24},{8,0},{16,8},{24,16},{1,25},{9,1},{17,9},{25,17},{2,26},{10... | collective-permute-start | bytes 393224 | tf_op jit(solution)/shard_map/ppermute | solution.py:666
  225.7 6.9 %collective-permute-done.42 = f32[2,64,256]{2,1,0:T(8,128)S(1)} collective-permute-done((f32[2,64,256]{2,1,0:T(8,128)S(1)}, f32[2,64,256]{2,1,0:T(8,128)S(1)}, u32[]{:S(2)}, u32[]{:S(2)}) %collective-permute-start.42) | collective-permute-done | bytes 131104 | tf_op jit(solution)/shard_map/ppermute | solution.py:666
  232.6 2.7 %collective-permute-done.43 = f32[2,64,256]{2,1,0:T(8,128)S(1)} collective-permute-done((f32[2,64,256]{2,1,0:T(8,128)S(1)}, f32[2,64,256]{2,1,0:T(8,128)S(1)}, u32[]{:S(2)}, u32[]{:S(2)}) %collective-permute-start.43) | collective-permute-done | bytes 131104 | tf_op jit(solution)/shard_map/ppermute | solution.py:666
  237.3 8.7 %final.1 = (f32[2,64,256]{2,1,0:T(8,128)}, f32[8,2,64,1024]{3,2,1,0:T(8,128)}) custom-call(s32[1]{0:T(128)} %bitcast.parity_ref, f32[8,256]{1,0:T(8,128)} %add.52.dots_ref, f32[8,128]{1,0:T(8,128)} %get-tuple-element.49.refs_6_.length_ref, f32[2,64,256]{2,1,0:T(8,128)} %fusion.5.q0_ref, f32[2,64,256]{2,1,0:T(8,128)} %fusion.2.q1_ref, ...), custom_call_target="tpu_custom_call" | custom-call | tf_op jit(solution)/shard_map/final/pallas_call | solution.py:718
  (170 shorter events, 71.3 us)
Async XLA Ops:
  0.6 79.6 %collective-permute-start.16 = (f32[8,2,64,1024]{3,2,1,0:T(8,128)}, f32[8,2,64,1024]{3,2,1,0:T(8,128)}, u32[]{:S(2)}, u32[]{:S(2)}) collective-permute-start(f32[8,2,64,1024]{3,2,1,0:T(8,128)} %refs_26_.1), channel_id=1, source_target_pairs={{0,1},{1,0},{2,3},{3,2},{4,5},{5,4},{6,7},{7,6},{8,9},{9,8},{10,11... | collective-permute-start | bytes 12582920 | tf_op jit(solution)/shard_map/ppermute | solution.py:527
  44.5 35.7 %collective-permute-start.14 = (s32[8,256,256]{2,1,0:T(8,128)}, s32[8,256,256]{2,1,0:T(8,128)S(1)}, u32[]{:S(2)}, u32[]{:S(2)}) collective-permute-start(s32[8,256,256]{2,1,0:T(8,128)} %get-tuple-element.37.refs_10_.refs_18_), channel_id=1, source_target_pairs={{0,1},{1,0},{2,3},{3,2},{4,5},{5,4},{6,7},{7,6},{8,9},{9,8},{10,11... | collective-permute-start | bytes 6291464 | tf_op jit(solution)/shard_map/ppermute | solution.py:527
  49.6 15.4 %collective-permute-start.4 = (f32[4,64,256]{2,1,0:T(8,128)S(1)}, f32[4,64,256]{2,1,0:T(8,128)S(1)}, u32[]{:S(2)}, u32[]{:S(2)}) collective-permute-start(f32[4,64,256]{2,1,0:T(8,128)S(1)} %copy-done.17), channel_id=1, source_target_pairs={{0,4},{1,5},{2,6},{3,7},{4,0},{5,1},{6,2},{7,3},{8,12},{9,13},{10,... | collective-permute-start | bytes 786440 | tf_op jit(solution)/shard_map/ppermute | solution.py:527
  51.1 14.5 %collective-permute-start.5 = (f32[4,64,256]{2,1,0:T(8,128)S(1)}, f32[4,64,256]{2,1,0:T(8,128)S(1)}, u32[]{:S(2)}, u32[]{:S(2)}) collective-permute-start(f32[4,64,256]{2,1,0:T(8,128)S(1)} %copy-done.17), channel_id=1, source_target_pairs={{0,6},{1,7},{2,4},{3,5},{4,2},{5,3},{6,0},{7,1},{8,14},{9,15},{10,... | collective-permute-start | bytes 786440 | tf_op jit(solution)/shard_map/ppermute | solution.py:527
  53.3 13.8 %collective-permute-start.13 = (f32[256,256]{1,0:T(8,128)}, f32[256,256]{1,0:T(8,128)S(1)}, u32[]{:S(2)}, u32[]{:S(2)}) collective-permute-start(f32[256,256]{1,0:T(8,128)} %get-tuple-element.36.refs_8_.refs_16_), channel_id=1, source_target_pairs={{0,1},{1,0},{2,3},{3,2},{4,5},{5,4},{6,7},{7,6},{8,9},{9,8},{10,11... | collective-permute-start | bytes 786440 | tf_op jit(solution)/shard_map/ppermute | solution.py:527
  64.9 9.2 %collective-permute-start.7 = (f32[4,64,256]{2,1,0:T(8,128)S(1)}, f32[4,64,256]{2,1,0:T(8,128)S(1)}, u32[]{:S(2)}, u32[]{:S(2)}) collective-permute-start(f32[4,64,256]{2,1,0:T(8,128)S(1)} %collective-permute-done.6.refs_4_), channel_id=1, source_target_pairs={{0,2},{1,3},{2,0},{3,1},{4,6},{5,7},{6,4},{7,5},{8,10},{9,11},{10,... | collective-permute-start | bytes 786440 | tf_op jit(solution)/shard_map/ppermute | solution.py:527
  65.6 13.0 %collective-permute-start.8 = (f32[4,64,256]{2,1,0:T(8,128)S(1)}, f32[4,64,256]{2,1,0:T(8,128)S(1)}, u32[]{:S(2)}, u32[]{:S(2)}) collective-permute-start(f32[4,64,256]{2,1,0:T(8,128)S(1)} %collective-permute-done.6.refs_4_), channel_id=1, source_target_pairs={{0,4},{1,5},{2,6},{3,7},{4,0},{5,1},{6,2},{7,3},{8,12},{9,13},{10,... | collective-permute-start | bytes 786440 | tf_op jit(solution)/shard_map/ppermute | solution.py:527
  67.1 13.1 %collective-permute-start.9 = (f32[4,64,256]{2,1,0:T(8,128)S(1)}, f32[4,64,256]{2,1,0:T(8,128)S(1)}, u32[]{:S(2)}, u32[]{:S(2)}) collective-permute-start(f32[4,64,256]{2,1,0:T(8,128)S(1)} %collective-permute-done.6.refs_4_), channel_id=1, source_target_pairs={{0,6},{1,7},{2,4},{3,5},{4,2},{5,3},{6,0},{7,1},{8,14},{9,15},{10,... | collective-permute-start | bytes 786440 | tf_op jit(solution)/shard_map/ppermute | solution.py:527
  125.2 12.1 %collective-permute-start.24 = (f32[72,256]{1,0:T(8,128)}, f32[72,256]{1,0:T(8,128)S(1)}, u32[]{:S(2)}, u32[]{:S(2)}) collective-permute-start(f32[72,256]{1,0:T(8,128)} %get-tuple-element.45.refs_8_), channel_id=1, source_target_pairs={{0,1},{1,0},{2,3},{3,2},{4,5},{5,4},{6,7},{7,6},{8,9},{9,8},{10,11... | collective-permute-start | bytes 221192 | tf_op jit(solution)/shard_map/ppermute | solution.py:527
  126.7 10.7 %collective-permute-start.25 = (f32[72,256]{1,0:T(8,128)S(1)}, f32[72,256]{1,0:T(8,128)S(1)}, u32[]{:S(2)}, u32[]{:S(2)}) collective-permute-start(f32[72,256]{1,0:T(8,128)S(1)} %collective-permute-done.21.refs_9_), channel_id=1, source_target_pairs={{0,1},{1,0},{2,3},{3,2},{4,5},{5,4},{6,7},{7,6},{8,9},{9,8},{10,11... | collective-permute-start | bytes 221192 | tf_op jit(solution)/shard_map/ppermute | solution.py:527
  128.0 9.4 %collective-permute-start.26 = (f32[72,256]{1,0:T(8,128)S(1)}, f32[72,256]{1,0:T(8,128)S(1)}, u32[]{:S(2)}, u32[]{:S(2)}) collective-permute-start(f32[72,256]{1,0:T(8,128)S(1)} %collective-permute-done.22.refs_10_), channel_id=1, source_target_pairs={{0,1},{1,0},{2,3},{3,2},{4,5},{5,4},{6,7},{7,6},{8,9},{9,8},{10,11... | collective-permute-start | bytes 221192 | tf_op jit(solution)/shard_map/ppermute | solution.py:527
  137.0 98.9 %collective-permute-start.44 = (f32[4,2,64,1024]{3,2,1,0:T(8,128)}, f32[4,2,64,1024]{3,2,1,0:T(8,128)S(1)}, u32[]{:S(2)}, u32[]{:S(2)}) collective-permute-start(f32[4,2,64,1024]{3,2,1,0:T(8,128)} %bitcast.35), channel_id=1, source_target_pairs={{0,1},{1,0},{2,3},{3,2},{4,5},{5,4},{6,7},{7,6},{8,9},{9,8},{10,11... | collective-permute-start | bytes 6291464 | tf_op jit(solution)/shard_map/ppermute | solution.py:527
  172.6 63.4 %collective-permute-start.45 = (f32[4,2,64,1024]{3,2,1,0:T(8,128)}, f32[4,2,64,1024]{3,2,1,0:T(8,128)}, u32[]{:S(2)}, u32[]{:S(2)}) collective-permute-start(f32[4,2,64,1024]{3,2,1,0:T(8,128)} %bitcast.36), channel_id=1, source_target_pairs={{0,1},{1,0},{2,3},{3,2},{4,5},{5,4},{6,7},{7,6},{8,9},{9,8},{10,11... | collective-permute-start | bytes 6291464 | tf_op jit(solution)/shard_map/ppermute | solution.py:527
  188.5 10.7 %collective-permute-start.32 = (f32[8,256]{1,0:T(8,128)}, f32[8,256]{1,0:T(8,128)S(1)}, u32[]{:S(2)}, u32[]{:S(2)}) collective-permute-start(f32[8,256]{1,0:T(8,128)} %last_dots.1), channel_id=1, source_target_pairs={{0,2},{1,3},{2,0},{3,1},{4,6},{5,7},{6,4},{7,5},{8,10},{9,11},{10,... | collective-permute-start | bytes 24584 | tf_op jit(solution)/shard_map/ppermute | solution.py:527
  189.1 10.1 %collective-permute-start.33 = (f32[8,256]{1,0:T(8,128)}, f32[8,256]{1,0:T(8,128)S(1)}, u32[]{:S(2)}, u32[]{:S(2)}) collective-permute-start(f32[8,256]{1,0:T(8,128)} %last_dots.1), channel_id=1, source_target_pairs={{0,4},{1,5},{2,6},{3,7},{4,0},{5,1},{6,2},{7,3},{8,12},{9,13},{10,... | collective-permute-start | bytes 24584 | tf_op jit(solution)/shard_map/ppermute | solution.py:527
  190.2 9.5 %collective-permute-start.34 = (f32[8,256]{1,0:T(8,128)}, f32[8,256]{1,0:T(8,128)S(1)}, u32[]{:S(2)}, u32[]{:S(2)}) collective-permute-start(f32[8,256]{1,0:T(8,128)} %last_dots.1), channel_id=1, source_target_pairs={{0,6},{1,7},{2,4},{3,5},{4,2},{5,3},{6,0},{7,1},{8,14},{9,15},{10,... | collective-permute-start | bytes 24584 | tf_op jit(solution)/shard_map/ppermute | solution.py:527
  199.2 8.5 %collective-permute-start.36 = (f32[4,2,64,256]{3,2,1,0:T(8,128)}, f32[4,2,64,256]{3,2,1,0:T(8,128)S(1)}, u32[]{:S(2)}, u32[]{:S(2)}) collective-permute-start(f32[4,2,64,256]{3,2,1,0:T(8,128)} %get-tuple-element.51), channel_id=1, source_target_pairs={{0,1},{1,0},{2,3},{3,2},{4,5},{5,4},{6,7},{7,6},{8,9},{9,8},{10,11... | collective-permute-start | bytes 1572872 | tf_op jit(solution)/shard_map/ppermute | solution.py:527
  199.2 11.8 %collective-permute-start.40 = (f32[4,2,64,256]{3,2,1,0:T(8,128)}, f32[4,2,64,256]{3,2,1,0:T(8,128)S(1)}, u32[]{:S(2)}, u32[]{:S(2)}) collective-permute-start(f32[4,2,64,256]{3,2,1,0:T(8,128)} %get-tuple-element.53), channel_id=1, source_target_pairs={{0,1},{1,0},{2,3},{3,2},{4,5},{5,4},{6,7},{7,6},{8,9},{9,8},{10,11... | collective-permute-start | bytes 1572872 | tf_op jit(solution)/shard_map/ppermute | solution.py:527
  207.9 8.3 %collective-permute-start.37 = (f32[2,64,256]{2,1,0:T(8,128)S(1)}, f32[2,64,256]{2,1,0:T(8,128)S(1)}, u32[]{:S(2)}, u32[]{:S(2)}) collective-permute-start(f32[2,64,256]{2,1,0:T(8,128)S(1)} %get-tuple-element.67), channel_id=1, source_target_pairs={{0,8},{8,16},{16,24},{24,0},{1,9},{9,17},{17,25},{25,1},{2,10},{10... | collective-permute-start | bytes 393224 | tf_op jit(solution)/shard_map/ppermute | solution.py:666
  209.8 12.0 %collective-permute-start.38 = (f32[2,64,256]{2,1,0:T(8,128)S(1)}, f32[2,64,256]{2,1,0:T(8,128)S(1)}, u32[]{:S(2)}, u32[]{:S(2)}) collective-permute-start(f32[2,64,256]{2,1,0:T(8,128)S(1)} %get-tuple-element.69), channel_id=1, source_target_pairs={{0,16},{8,24},{16,0},{24,8},{1,17},{9,25},{17,1},{25,9},{2,18},{10... | collective-permute-start | bytes 393224 | tf_op jit(solution)/shard_map/ppermute | solution.py:666
  211.1 10.8 %collective-permute-start.39 = (f32[2,64,256]{2,1,0:T(8,128)S(1)}, f32[2,64,256]{2,1,0:T(8,128)S(1)}, u32[]{:S(2)}, u32[]{:S(2)}) collective-permute-start(f32[2,64,256]{2,1,0:T(8,128)S(1)} %get-tuple-element.68), channel_id=1, source_target_pairs={{0,24},{8,0},{16,8},{24,16},{1,25},{9,1},{17,9},{25,17},{2,26},{10... | collective-permute-start | bytes 393224 | tf_op jit(solution)/shard_map/ppermute | solution.py:666
  216.2 9.4 %collective-permute-start.41 = (f32[2,64,256]{2,1,0:T(8,128)S(1)}, f32[2,64,256]{2,1,0:T(8,128)S(1)}, u32[]{:S(2)}, u32[]{:S(2)}) collective-permute-start(f32[2,64,256]{2,1,0:T(8,128)S(1)} %get-tuple-element.64), channel_id=1, source_target_pairs={{0,8},{8,16},{16,24},{24,0},{1,9},{9,17},{17,25},{25,1},{2,10},{10... | collective-permute-start | bytes 393224 | tf_op jit(solution)/shard_map/ppermute | solution.py:666
  221.8 10.7 %collective-permute-start.42 = (f32[2,64,256]{2,1,0:T(8,128)S(1)}, f32[2,64,256]{2,1,0:T(8,128)S(1)}, u32[]{:S(2)}, u32[]{:S(2)}) collective-permute-start(f32[2,64,256]{2,1,0:T(8,128)S(1)} %get-tuple-element.66), channel_id=1, source_target_pairs={{0,16},{8,24},{16,0},{24,8},{1,17},{9,25},{17,1},{25,9},{2,18},{10... | collective-permute-start | bytes 393224 | tf_op jit(solution)/shard_map/ppermute | solution.py:666
  221.8 13.4 %collective-permute-start.43 = (f32[2,64,256]{2,1,0:T(8,128)S(1)}, f32[2,64,256]{2,1,0:T(8,128)S(1)}, u32[]{:S(2)}, u32[]{:S(2)}) collective-permute-start(f32[2,64,256]{2,1,0:T(8,128)S(1)} %get-tuple-element.65), channel_id=1, source_target_pairs={{0,24},{8,0},{16,8},{24,16},{1,25},{9,1},{17,9},{25,17},{2,26},{10... | collective-permute-start | bytes 393224 | tf_op jit(solution)/shard_map/ppermute | solution.py:666
  (61 other events, 370.5 us)
where the time goes:
time: 247 us; the launch traced here: 246 us
  Pallas kernels  131 us (53%)
  waiting for transfers between devices  61.8 us (25%)
  starting transfers between devices  41.5 us (17%)
  local copies, waits for them, and re-layouts  7.58 us (3%)
  other arithmetic  3 us (1%)
    pallas_call x2, Pallas kernels, apply(): pl.pallas_call(functools.partial(apply_kernel, width, levels, nlat_dev, f...  52.7 us
    ppermute x31, waiting for transfers between devices, swap(): return lax.ppermute(value, 'lat', [(i, i ^ bits) for i in range(nlat_dev)])  29.7 us
    pallas_call x4, Pallas kernels, product(): pl.pallas_call(product_kernel, grid=(wide // tile,), in_specs=[whole, who...  29 us
    ppermute x31, starting transfers between devices, swap(): return lax.ppermute(value, 'lat', [(i, i ^ bits) for i in range(nlat_dev)])  19.4 us
    ppermute x6, waiting for transfers between devices, to_quarters(): lax.ppermute(image[hop], 'mem', [(i, (i + hop) % nmem) for i in range(nme...  19.1 us
    ppermute x9, starting transfers between devices, around_mem(): lax.ppermute(value, 'mem', [(i, (i + hop) % nmem) for i in range(nmem)])  14.6 us
    pallas_call x1, Pallas kernels, per_device(): pl.pallas_call(functools.partial(inverse_kernel, width, levels, lon, nlat...  13.2 us
    ppermute x9, waiting for transfers between devices, around_mem(): lax.ppermute(value, 'mem', [(i, (i + hop) % nmem) for i in range(nmem)])  13 us
  transfers between devices with their start and end apart: 46, of which 23 were waited for; matrix products, arithmetic and copies ran while one was open for 1% of the time, Pallas kernels for 38%

commit v1 on v0

--- a/solution.py
+++ b/solution.py
@@ -118,7 +118,7 @@
 
 
 def observe_kernel(width, nmem, *refs):
-    block_refs, (members_ref, obs_ref, local_ref, mine_ref, other_ref, blocks) = refs[:nmem], refs[nmem:]
+    block_refs, (members_ref, obs_ref, joint_ref, other_ref, blocks) = refs[:nmem], refs[nmem:]
     _, part, _ = block_refs[0].shape
     count, levels, rows, lon = members_ref.shape
     me = lax.axis_index("mem")
@@ -141,8 +141,8 @@
                     total = jnp.where(lane // width == side, raw, total)
                 obs_ref[kind, piece * part : (piece + 1) * part, columns] = total
         cells = obs_ref[0, :, columns].astype(jnp.int32)
-        local_ref[0, :, columns] = obs_ref[0, :, columns]
-        local_ref[1, :, columns] = run_totals(cells, obs_ref[2, :, columns], width)
+        joint_ref[0, :, columns] = obs_ref[0, :, columns]
+        joint_ref[1, :, columns] = run_totals(cells, obs_ref[2, :, columns], width)
 
     step = 8
     half_count = count // 2
@@ -165,7 +165,7 @@
             order += [(1 - parity) * half_count + i for i in range(half_count)]
             outs = pick_cells(cells, [reader(member) for member in order], width, levels, quarter, lon)
             for i in range(half_count):
-                mine_ref[i, here, columns] = outs[i]
+                joint_ref[2 + i, here, columns] = outs[i]
                 other_ref[i, here, columns] = outs[half_count + i]
         return carry
 
@@ -173,15 +173,23 @@
 
 
 def inverse_kernel(width, levels, lon, nblocks_lat, *refs):
-    local_refs, (inverse_ref, value_ref, cells_all) = refs[:nblocks_lat], refs[nblocks_lat:]
-    _, rows, slots = local_refs[0].shape
+    local_refs, (inverse_ref, value_ref, cells_all, local, sems) = refs[:nblocks_lat], refs[nblocks_lat:]
+    _, _, rows, slots = local.shape
+    copies = [
+        pltpu.make_async_copy(ref.at[pl.ds(0, 2)], local.at[number], sems.at[number])
+        for number, ref in enumerate(local_refs)
+    ]
+    for copy in copies:
+        copy.start()
+    for copy in copies:
+        copy.wait()
     nblocks = slots // width
     quarter = lon // nblocks
     per = LANES // width
     tall = 16
-    for number, local_ref in enumerate(local_refs):
-        value_ref[number * rows : (number + 1) * rows, :] = local_ref[1]
-        cells_all[number * rows : (number + 1) * rows, :] = local_ref[0].astype(jnp.int32)
+    for number in range(nblocks_lat):
+        value_ref[number * rows : (number + 1) * rows, :] = local[number, 1]
+        cells_all[number * rows : (number + 1) * rows, :] = local[number, 0].astype(jnp.int32)
 
     def one(index, carry):
         here = pl.ds(pl.multiple_of(index * tall, tall), tall)
@@ -239,8 +247,13 @@
     def rotated(block):
         return lax.rem(block - me_mem + nblocks, nblocks)
 
+    half_blocks = nlat_blocks // 2
     seen_copies = [
-        pltpu.make_async_copy(ref, seen.at[:, pl.ds(number * rows, rows)], seen_sems.at[number])
+        pltpu.make_async_copy(
+            ref.at[pl.ds(2, count)] if number < half_blocks else ref,
+            seen.at[:, pl.ds(number * rows, rows)],
+            seen_sems.at[number],
+        )
         for number, ref in enumerate(seen_refs)
     ]
 
@@ -258,12 +271,7 @@
         pltpu.make_async_copy(members_ref.at[pl.ds(parity * count, count)], members.at[0], sems.at[2]),
         pltpu.make_async_copy(members_sib_ref.at[pl.ds(parity * count, count)], members.at[1], sems.at[3]),
     ]
-    for copy in inverse_copies(0) + seen_copies:
-        copy.start()
-    for chunk in range(1, nchunks):
-        for copy in inverse_copies(chunk):
-            copy.start()
-    for copy in late:
+    for copy in inverse_copies(0) + seen_copies + inverse_copies(1):
         copy.start()
 
     if first:
@@ -324,6 +332,8 @@
 
     for copy in inverse_copies(0) + seen_copies:
         copy.wait()
+    for copy in inverse_copies(2):
+        copy.start()
     build(0, xa_high, xa_low)
 
     def one(pair, carry):
@@ -335,6 +345,18 @@
         def _():
             for copy in inverse_copies(chunk + 2):
                 copy.wait()
+            for copy in inverse_copies(chunk + 3):
+                copy.start()
+
+        @pl.when(chunk + 4 < nchunks)
+        def _():
+            for copy in inverse_copies(chunk + 4):
+                copy.start()
+
+        @pl.when(pair == 0)
+        def _():
+            for copy in late:
+                copy.start()
 
         build(chunk + 1, xb_high, xb_low)
         multiply(chunk, xa_high, xa_low)
@@ -356,10 +378,12 @@
     tile = 2 * LANES
     deep = levels * wide
 
-    for column in range(lon // tile):
-        cols = slice(column * tile, (column + 1) * tile)
-        place = rotated(column * tile // quarter)
-        inner = slice(column * tile % quarter, column * tile % quarter + tile)
+    def panel(column, carry):
+        begin = column * tile
+        cols = pl.ds(pl.multiple_of(begin, tile), tile)
+        place = rotated(begin // quarter)
+        inner = pl.ds(pl.multiple_of(lax.rem(begin, quarter), tile), tile)
+        totals = [[None] * levels for _ in range(2)]
         for member in range(count):
             part = slice(member * deep, (member + 1) * deep)
             product = (
@@ -369,12 +393,16 @@
             )
             for level in range(levels):
                 for side in range(2):
-                    begin = level * wide + side * rows
-                    term = members[side, member, level, :, cols] * product[begin : begin + rows]
-                    if member == 0:
-                        image_refs[side][place, level, :, inner] = term
-                    else:
-                        image_refs[side][place, level, :, inner] += term
+                    top = level * wide + side * rows
+                    term = members[side, member, level, :, cols] * product[top : top + rows]
+                    old = totals[side][level]
+                    totals[side][level] = term if old is None else old + term
+        for side in range(2):
+            for level in range(levels):
+                image_refs[side][place, level, :, inner] = totals[side][level]
+        return carry
+
+    lax.fori_loop(0, lon // tile, panel, 0)
 
     step = 8
     for side in range(2):
@@ -444,20 +472,22 @@
     high_ref[...], low_ref[...] = split(ordered[...].T)
 
 
-def covariance_kernel(root_ref, high_ref, low_ref, root_high_ref, root_low_ref):
-    lon = root_ref.shape[0]
-    root_high_ref[...], root_low_ref[...] = split(root_ref[...])
-    tile = 2 * LANES
+def covariance_kernel(root_ref, high_ref, low_ref, root_high_ref, root_low_ref, root_high, root_low):
+    tile = high_ref.shape[1]
     numbers = (((1,), (1,)), ((), ()))
+
+    @pl.when(pl.program_id(0) == 0)
+    def _():
+        root_high[...], root_low[...] = split(root_ref[...])
 
     def times(a, b):
         return lax.dot_general(a, b, numbers, preferred_element_type=F32)
 
-    for column in range(lon // tile):
-        cols = slice(column * tile, (column + 1) * tile)
-        high, low = root_high_ref[cols, :], root_low_ref[cols, :]
-        total = times(root_high_ref[...], high) + times(root_low_ref[...], high) + times(root_high_ref[...], low)
-        high_ref[:, cols], low_ref[:, cols] = split(total)
+    here = pl.ds(pl.multiple_of(pl.program_id(0) * tile, tile), tile)
+    high, low = root_high[here, :], root_low[here, :]
+    root_high_ref[...], root_low_ref[...] = high, low
+    total = times(root_high[...], high) + times(root_low[...], high) + times(root_high[...], low)
+    high_ref[...], low_ref[...] = split(total)
 
 
 def product_kernel(a_high_ref, a_low_ref, b_high_ref, b_low_ref, out_ref):
@@ -544,14 +574,13 @@
         name="sort_slots",
     )(obs_cell, obs_weight, obs_mask, innovation)
     blocks = around_mem(block)
-    obs, local, mine, other = pl.pallas_call(
+    obs, joint, other = pl.pallas_call(
         functools.partial(observe_kernel, width, nmem),
         in_specs=[VM] * (nmem + 1),
-        out_specs=[VM] * 4,
+        out_specs=[VM] * 3,
         out_shape=[
             shape((3, rows, slots), F32),
-            shape((2, rows, slots), F32),
-            shape((half_count, rows, slots), F32),
+            shape((2 + half_count, rows, slots), F32),
             shape((half_count, rows, slots), F32),
         ],
         scratch_shapes=[pltpu.VMEM((nmem, *block.shape), F32)],
@@ -560,10 +589,10 @@
         name="members_at_slots",
     )(*blocks, members)
 
-    locals_ = direct(local)
-    local_sib = swap(local, 1)
     received = swap(other, 1)
-    seens = direct(mine) + direct(received)
+    joints = direct(joint)
+    seens = joints + direct(received)
+    obs_sib = swap(obs, 1)
     members_sib = swap(members, 1)
 
     lhs_high, lhs_low = pl.pallas_call(
@@ -583,9 +612,12 @@
     )(lat_root)
     cn_high, cn_low, lon_high, lon_low = pl.pallas_call(
         covariance_kernel,
-        in_specs=[VM],
-        out_specs=[VM] * 4,
+        grid=(lon // (2 * LANES),),
+        in_specs=[pl.BlockSpec((lon, lon), lambda i: (0, 0))],
+        out_specs=[pl.BlockSpec((lon, 2 * LANES), lambda i: (0, i))] * 2
+        + [pl.BlockSpec((2 * LANES, lon), lambda i: (i, 0))] * 2,
         out_shape=[shape((lon, lon), BF16)] * 4,
+        scratch_shapes=[pltpu.VMEM((lon, lon), BF16)] * 2,
         compiler_params=params(),
         cost_estimate=cost(6 * lon**3, 12 * lon * lon),
         name="lon_covariance",
@@ -594,14 +626,18 @@
     nchunks = levels * nmem
     inverse, value = pl.pallas_call(
         functools.partial(inverse_kernel, width, levels, lon, nlat_dev // 2),
-        in_specs=[VM] * (nlat_dev // 2),
+        in_specs=[ANY] * (nlat_dev // 2),
         out_specs=[VM] * 2,
         out_shape=[shape((nchunks, nlat // 2, quarter), jnp.int32), shape((nlat // 2, slots), F32)],
-        scratch_shapes=[pltpu.VMEM((nlat // 2, slots), jnp.int32)],
+        scratch_shapes=[
+            pltpu.VMEM((nlat // 2, slots), jnp.int32),
+            pltpu.VMEM((nlat_dev // 2, 2, rows, slots), F32),
+            pltpu.SemaphoreType.DMA((nlat_dev // 2,)),
+        ],
         compiler_params=params(),
         cost_estimate=cost(10**10, 2 * nlat * lon * levels),
         name="inverse",
-    )(*locals_)
+    )(*joints)
     inverses, values = [inverse, swap(inverse, 1)], [value, swap(value, 1)]
 
     tall = half_count * levels * rows
@@ -652,8 +688,8 @@
             *inverses,
             lhs_high,
             lhs_low,
-            local,
-            local_sib,
+            obs,
+            obs_sib,
             cn_high,
             cn_low,
             members,

time: 247 us -> 251 us (1.016)
  waiting for transfers between devices: 61.8 us -> 71.4 us
  starting transfers between devices: 41.5 us -> 38.6 us
    ppermute x31 -> x28, waiting for transfers between devices: 29.7 us -> 39 us  [swap(): return lax.ppermute(value, 'lat', [(i, i ^ bits) for i in range(nlat_dev)])]
    ppermute x31 -> x28, starting transfers between devices: 19.4 us -> 17.1 us  [swap(): return lax.ppermute(value, 'lat', [(i, i ^ bits) for i in range(nlat_dev)])]
    unnamed x78 -> x72, local copies, waits for them, and re-layouts: 7.53 us -> 7.83 us
  transfers between devices with their start and end apart: 46 -> 43, of which waited for: 23 -> 20; matrix products, arithmetic and copies ran while one was open for 1% -> 1% of each run, Pallas kernels for 38% -> 37%
where the time goes in v1:
time: 251 us
  Pallas kernels  129 us (51%)
  waiting for transfers between devices  71.4 us (28%)
  starting transfers between devices  38.6 us (15%)
  local copies, waits for them, and re-layouts  7.88 us (3%)
  other arithmetic  2.97 us (1%)
    pallas_call x2, Pallas kernels, apply(): pl.pallas_call(functools.partial(apply_kernel, width, levels, nlat_dev, f...  50.4 us
    ppermute x28, waiting for transfers between devices, swap(): return lax.ppermute(value, 'lat', [(i, i ^ bits) for i in range(nlat_dev)])  39 us
    pallas_call x4, Pallas kernels, product(): pl.pallas_call(product_kernel, grid=(wide // tile,), in_specs=[whole, who...  28.8 us
    ppermute x6, waiting for transfers between devices, to_quarters(): lax.ppermute(image[hop], 'mem', [(i, (i + hop) % nmem) for i in range(nme...  19.3 us
    ppermute x28, starting transfers between devices, swap(): return lax.ppermute(value, 'lat', [(i, i ^ bits) for i in range(nlat_dev)])  17.1 us
    ppermute x9, starting transfers between devices, around_mem(): lax.ppermute(value, 'mem', [(i, (i + hop) % nmem) for i in range(nmem)])  14.3 us
    pallas_call x1, Pallas kernels, per_device(): pl.pallas_call(functools.partial(inverse_kernel, width, levels, lon, nlat...  13.3 us
    ppermute x9, waiting for transfers between devices, around_mem(): lax.ppermute(value, 'mem', [(i, (i + hop) % nmem) for i in range(nmem)])  13.2 us
  transfers between devices with their start and end apart: 43, of which 20 were waited for; matrix products, arithmetic and copies ran while one was open for 1% of the time, Pallas kernels for 37%

profile of v1, /device:TPU:0, one launch (start us, length us, event | category | flops | bytes accessed | tf_op | source)
XLA Modules:
  0.0 250.6 jit_solution(12049947487103793993)
XLA Ops:
  1.2 3.1 %sort_slots.1.refs_0_ = f32[3,32,128]{2,1,0:T(8,128)} custom-call(s32[64,64]{1,0:T(8,128)} %cell_ref.1, f32[64,64]{1,0:T(8,128)} %weight_ref.1, s32[64,64]{1,0:T(8,128)} %mask_ref.1, f32[64,64]{1,0:T(8,128)} %innovation_ref.1), custom_call_target="tpu_custom_call" | custom-call | tf_op jit(solution)/shard_map/sort_slots/pallas_call | solution.py:567
  14.9 5.5 %members_at_slots.1 = (f32[3,64,256]{2,1,0:T(8,128)}, f32[6,64,256]{2,1,0:T(8,128)}, f32[4,64,256]{2,1,0:T(8,128)}) custom-call(f32[3,32,128]{2,1,0:T(8,128)} %sort_slots.1.refs_0_, f32[3,32,128]{2,1,0:T(8,128)} %copy-done.13, f32[3,32,128]{2,1,0:T(8,128)} %copy-done.14, f32[3,32,128]{2,1,0:T(8,128)} %copy-done.15, f32[8,2,64,1024]{3,2,1,0:T(8,128)} %refs_26_.1), custom_call_target="tpu_custom_call" | custom-call | flops 100000000 | bytes 4194304 | tf_op jit(solution)/shard_map/members_at_slots/pallas_call | solution.py:577
  23.8 8.7 %collective-permute-done.3.refs_1_ = f32[6,64,256]{2,1,0:T(8,128)S(1)} collective-permute-done((f32[6,64,256]{2,1,0:T(8,128)}, f32[6,64,256]{2,1,0:T(8,128)S(1)}, u32[]{:S(2)}, u32[]{:S(2)}) %collective-permute-start.3) | collective-permute-done | bytes 393248 | tf_op jit(solution)/shard_map/ppermute | solution.py:557
  32.5 8.6 %collective-permute-done.4.refs_2_ = f32[6,64,256]{2,1,0:T(8,128)S(1)} collective-permute-done((f32[6,64,256]{2,1,0:T(8,128)}, f32[6,64,256]{2,1,0:T(8,128)S(1)}, u32[]{:S(2)}, u32[]{:S(2)}) %collective-permute-start.4) | collective-permute-done | bytes 393248 | tf_op jit(solution)/shard_map/ppermute | solution.py:557
  42.7 13.3 %inverse.1 = (s32[8,256,256]{2,1,0:T(8,128)}, f32[256,256]{1,0:T(8,128)}) custom-call(f32[6,64,256]{2,1,0:T(8,128)} %get-tuple-element.32.refs_0_, f32[6,64,256]{2,1,0:T(8,128)} %copy-done.17, f32[6,64,256]{2,1,0:T(8,128)} %copy-done.18, f32[6,64,256]{2,1,0:T(8,128)} %copy-done.19), custom_call_target="tpu_custom_call" | custom-call | flops 10000000000 | bytes 2097152 | tf_op jit(solution)/shard_map/inverse/pallas_call | solution.py:627
  56.7 4.1 %collective-permute-done.6.refs_4_ = f32[4,64,256]{2,1,0:T(8,128)S(1)} collective-permute-done((f32[4,64,256]{2,1,0:T(8,128)S(1)}, f32[4,64,256]{2,1,0:T(8,128)S(1)}, u32[]{:S(2)}, u32[]{:S(2)}) %collective-permute-start.6) | collective-permute-done | bytes 262176 | tf_op jit(solution)/shard_map/ppermute | solution.py:557
  61.3 11.5 %lon_covariance.1 = (bf16[1024,1024]{1,0:T(8,128)(2,1)}, bf16[1024,1024]{1,0:T(8,128)(2,1)}, bf16[1024,1024]{1,0:T(8,128)(2,1)}, bf16[1024,1024]{1,0:T(8,128)(2,1)}) custom-call(f32[1024,1024]{1,0:T(8,128)} %root_ref.3), custom_call_target="tpu_custom_call" | custom-call | flops 6442450944 | bytes 12582912 | tf_op jit(solution)/shard_map/lon_covariance/pallas_call | solution.py:613
  76.0 3.6 %lat_rows.1 = (bf16[256,512]{1,0:T(8,128)(2,1)}, bf16[256,512]{1,0:T(8,128)(2,1)}) custom-call(f32[512,512]{1,0:T(8,128)} %root_ref.2), custom_call_target="tpu_custom_call" | custom-call | flops 3000000000 | bytes 2097152 | tf_op jit(solution)/shard_map/lat_rows/pallas_call | solution.py:598
  79.5 6.9 %collective-permute-done.8.refs_6_ = f32[4,64,256]{2,1,0:T(8,128)S(1)} collective-permute-done((f32[4,64,256]{2,1,0:T(8,128)S(1)}, f32[4,64,256]{2,1,0:T(8,128)S(1)}, u32[]{:S(2)}, u32[]{:S(2)}) %collective-permute-start.8) | collective-permute-done | bytes 262176 | tf_op jit(solution)/shard_map/ppermute | solution.py:557
  87.4 25.1 %apply_first.1 = (f32[64,256]{1,0:T(8,128)}, f32[64,256]{1,0:T(8,128)}, f32[4,2,64,256]{3,2,1,0:T(8,128)}, f32[4,2,64,256]{3,2,1,0:T(8,128)}, bf16[512,1024]{1,0...) custom-call(f32[6,64,256]{2,1,0:T(8,128)} %get-tuple-element.32.refs_0_, ...), custom_call_target="tpu_custom_call" | custom-call | flops 9663676416 | bytes 31457280 | tf_op jit(solution)/shard_map/apply_first/pallas_call | solution.py:654
  118.7 3.0 %collective-permute-done.15.refs_1_ = f32[64,256]{1,0:T(8,128)S(1)} collective-permute-done((f32[64,256]{1,0:T(8,128)S(1)}, f32[64,256]{1,0:T(8,128)S(1)}, u32[]{:S(2)}, u32[]{:S(2)}) %collective-permute-start.15) | collective-permute-done | bytes 65568 | tf_op jit(solution)/shard_map/ppermute | solution.py:564
  135.7 7.2 %lon_product.5 = f32[512,1024]{1,0:T(8,128)} custom-call(bf16[512,1024]{1,0:T(8,128)(2,1)} %get-tuple-element.56.a_high_ref, bf16[512,1024]{1,0:T(8,128)(2,1)} %get-tuple-element.57.a_low_ref, bf16[1024,1024]{1,0:T(8,128)(2,1)} %get-tuple-element.54.b_high_ref, bf16[1024,1024]{1,0:T(8,128)(2,1)} %get-tuple-element.55.b_low_ref), custom_call_target="tpu_custom_call" | custom-call | flops 3221225472 | bytes 8388608 | tf_op jit(solution)/shard_map/lon_product/pallas_call | solution.py:507
  144.8 25.3 %apply_next.1 = (f32[64,256]{1,0:T(8,128)}, f32[64,256]{1,0:T(8,128)}, f32[4,2,64,256]{3,2,1,0:T(8,128)}, f32[4,2,64,256]{3,2,1,0:T(8,128)}, bf16[512,1024]{1,0:...) custom-call(f32[6,64,256]{2,1,0:T(8,128)} %get-tuple-element.32.refs, ...), custom_call_target="tpu_custom_call" | custom-call | flops 9663676416 | bytes 31457280 | tf_op jit(solution)/shard_map/apply_next/pallas_call | solution.py:654
  170.1 7.2 %lon_product.7 = f32[512,1024]{1,0:T(8,128)} custom-call(bf16[512,1024]{1,0:T(8,128)(2,1)} %get-tuple-element.60.a_high_ref, bf16[512,1024]{1,0:T(8,128)(2,1)} %get-tuple-element.61.a_low_ref, bf16[1024,1024]{1,0:T(8,128)(2,1)} %get-tuple-element.54.b_high_ref, bf16[1024,1024]{1,0:T(8,128)(2,1)} %get-tuple-element.55.b_low_ref), custom_call_target="tpu_custom_call" | custom-call | flops 3221225472 | bytes 8388608 | tf_op jit(solution)/shard_map/lon_product/pallas_call | solution.py:507
  177.8 4.0 %collective-permute-done.25 = f32[64,256]{1,0:T(8,128)S(1)} collective-permute-done((f32[64,256]{1,0:T(8,128)S(1)}, f32[64,256]{1,0:T(8,128)S(1)}, u32[]{:S(2)}, u32[]{:S(2)}) %collective-permute-start.25) | collective-permute-done | bytes 65568 | tf_op jit(solution)/shard_map/ppermute | solution.py:557
  185.7 3.0 %collective-permute-done.26.refs_1_ = f32[64,256]{1,0:T(8,128)S(1)} collective-permute-done((f32[64,256]{1,0:T(8,128)S(1)}, f32[64,256]{1,0:T(8,128)S(1)}, u32[]{:S(2)}, u32[]{:S(2)}) %collective-permute-start.26) | collective-permute-done | bytes 65568 | tf_op jit(solution)/shard_map/ppermute | solution.py:564
  196.6 7.2 %lon_product.4 = f32[512,1024]{1,0:T(8,128)} custom-call(bf16[512,1024]{1,0:T(8,128)(2,1)} %get-tuple-element.52.a_high_ref, bf16[512,1024]{1,0:T(8,128)(2,1)} %get-tuple-element.53.a_low_ref, bf16[1024,1024]{1,0:T(8,128)(2,1)} %get-tuple-element.54.b_high_ref, bf16[1024,1024]{1,0:T(8,128)(2,1)} %get-tuple-element.55.b_low_ref), custom_call_target="tpu_custom_call" | custom-call | flops 3221225472 | bytes 8388608 | tf_op jit(solution)/shard_map/lon_product/pallas_call | solution.py:507
  204.5 7.2 %lon_product.6 = f32[512,1024]{1,0:T(8,128)} custom-call(bf16[512,1024]{1,0:T(8,128)(2,1)} %get-tuple-element.58.a_high_ref, bf16[512,1024]{1,0:T(8,128)(2,1)} %get-tuple-element.59.a_low_ref, bf16[1024,1024]{1,0:T(8,128)(2,1)} %get-tuple-element.54.b_high_ref, bf16[1024,1024]{1,0:T(8,128)(2,1)} %get-tuple-element.55.b_low_ref), custom_call_target="tpu_custom_call" | custom-call | flops 3221225472 | bytes 8388608 | tf_op jit(solution)/shard_map/lon_product/pallas_call | solution.py:507
  216.8 4.0 %collective-permute-done.34 = f32[2,64,256]{2,1,0:T(8,128)S(1)} collective-permute-done((f32[2,64,256]{2,1,0:T(8,128)S(1)}, f32[2,64,256]{2,1,0:T(8,128)S(1)}, u32[]{:S(2)}, u32[]{:S(2)}) %collective-permute-start.34) | collective-permute-done | bytes 131104 | tf_op jit(solution)/shard_map/ppermute | solution.py:702
  220.8 5.6 %collective-permute-done.35 = f32[2,64,256]{2,1,0:T(8,128)S(1)} collective-permute-done((f32[2,64,256]{2,1,0:T(8,128)S(1)}, f32[2,64,256]{2,1,0:T(8,128)S(1)}, u32[]{:S(2)}, u32[]{:S(2)}) %collective-permute-start.35) | collective-permute-done | bytes 131104 | tf_op jit(solution)/shard_map/ppermute | solution.py:702
  226.4 3.1 %collective-permute-start.40 = (f32[2,64,256]{2,1,0:T(8,128)S(1)}, f32[2,64,256]{2,1,0:T(8,128)S(1)}, u32[]{:S(2)}, u32[]{:S(2)}) collective-permute-start(f32[2,64,256]{2,1,0:T(8,128)S(1)} %get-tuple-element.63), channel_id=1, source_target_pairs={{0,24},{8,0},{16,8},{24,16},{1,25},{9,1},{17,9},{25,17},{2,26},{10... | collective-permute-start | bytes 393224 | tf_op jit(solution)/shard_map/ppermute | solution.py:702
  230.2 7.0 %collective-permute-done.39 = f32[2,64,256]{2,1,0:T(8,128)S(1)} collective-permute-done((f32[2,64,256]{2,1,0:T(8,128)S(1)}, f32[2,64,256]{2,1,0:T(8,128)S(1)}, u32[]{:S(2)}, u32[]{:S(2)}) %collective-permute-start.39) | collective-permute-done | bytes 131104 | tf_op jit(solution)/shard_map/ppermute | solution.py:702
  237.1 2.7 %collective-permute-done.40 = f32[2,64,256]{2,1,0:T(8,128)S(1)} collective-permute-done((f32[2,64,256]{2,1,0:T(8,128)S(1)}, f32[2,64,256]{2,1,0:T(8,128)S(1)}, u32[]{:S(2)}, u32[]{:S(2)}) %collective-permute-start.40) | collective-permute-done | bytes 131104 | tf_op jit(solution)/shard_map/ppermute | solution.py:702
  241.8 8.7 %final.1 = (f32[2,64,256]{2,1,0:T(8,128)}, f32[8,2,64,1024]{3,2,1,0:T(8,128)}) custom-call(s32[1]{0:T(128)} %bitcast.parity_ref, f32[8,256]{1,0:T(8,128)} %add.52.dots_ref, f32[8,128]{1,0:T(8,128)} %get-tuple-element.47.refs_6_.length_ref, f32[2,64,256]{2,1,0:T(8,128)} %fusion.5.q0_ref, f32[2,64,256]{2,1,0:T(8,128)} %fusion.2.q1_ref, ...), custom_call_target="tpu_custom_call" | custom-call | tf_op jit(solution)/shard_map/final/pallas_call | solution.py:754
  (158 shorter events, 64.1 us)
Async XLA Ops:
  0.6 85.9 %collective-permute-start.13 = (f32[8,2,64,1024]{3,2,1,0:T(8,128)}, f32[8,2,64,1024]{3,2,1,0:T(8,128)}, u32[]{:S(2)}, u32[]{:S(2)}) collective-permute-start(f32[8,2,64,1024]{3,2,1,0:T(8,128)} %refs_26_.1), channel_id=1, source_target_pairs={{0,1},{1,0},{2,3},{3,2},{4,5},{5,4},{6,7},{7,6},{8,9},{9,8},{10,11... | collective-permute-start | bytes 12582920 | tf_op jit(solution)/shard_map/ppermute | solution.py:557
  20.3 12.2 %collective-permute-start.3 = (f32[6,64,256]{2,1,0:T(8,128)}, f32[6,64,256]{2,1,0:T(8,128)S(1)}, u32[]{:S(2)}, u32[]{:S(2)}) collective-permute-start(f32[6,64,256]{2,1,0:T(8,128)} %get-tuple-element.32.refs_0_), channel_id=1, source_target_pairs={{0,2},{1,3},{2,0},{3,1},{4,6},{5,7},{6,4},{7,5},{8,10},{9,11},{10,... | collective-permute-start | bytes 1179656 | tf_op jit(solution)/shard_map/ppermute | solution.py:557
  21.8 19.4 %collective-permute-start.4 = (f32[6,64,256]{2,1,0:T(8,128)}, f32[6,64,256]{2,1,0:T(8,128)S(1)}, u32[]{:S(2)}, u32[]{:S(2)}) collective-permute-start(f32[6,64,256]{2,1,0:T(8,128)} %get-tuple-element.32.refs_0_), channel_id=1, source_target_pairs={{0,4},{1,5},{2,6},{3,7},{4,0},{5,1},{6,2},{7,3},{8,12},{9,13},{10,... | collective-permute-start | bytes 1179656 | tf_op jit(solution)/shard_map/ppermute | solution.py:557
  23.3 17.8 %collective-permute-start.5 = (f32[6,64,256]{2,1,0:T(8,128)}, f32[6,64,256]{2,1,0:T(8,128)S(1)}, u32[]{:S(2)}, u32[]{:S(2)}) collective-permute-start(f32[6,64,256]{2,1,0:T(8,128)} %get-tuple-element.32.refs_0_), channel_id=1, source_target_pairs={{0,6},{1,7},{2,4},{3,5},{4,2},{5,3},{6,0},{7,1},{8,14},{9,15},{10,... | collective-permute-start | bytes 1179656 | tf_op jit(solution)/shard_map/ppermute | solution.py:557
  56.0 30.5 %collective-permute-start.11 = (s32[8,256,256]{2,1,0:T(8,128)}, s32[8,256,256]{2,1,0:T(8,128)}, u32[]{:S(2)}, u32[]{:S(2)}) collective-permute-start(s32[8,256,256]{2,1,0:T(8,128)} %get-tuple-element.35.refs_10_.refs_18_), channel_id=1, source_target_pairs={{0,1},{1,0},{2,3},{3,2},{4,5},{5,4},{6,7},{7,6},{8,9},{9,8},{10,11... | collective-permute-start | bytes 6291464 | tf_op jit(solution)/shard_map/ppermute | solution.py:557
  56.6 17.8 %collective-permute-start.12 = (f32[3,64,256]{2,1,0:T(8,128)S(1)}, f32[3,64,256]{2,1,0:T(8,128)S(1)}, u32[]{:S(2)}, u32[]{:S(2)}) collective-permute-start(f32[3,64,256]{2,1,0:T(8,128)S(1)} %copy-done.1), channel_id=1, source_target_pairs={{0,1},{1,0},{2,3},{3,2},{4,5},{5,4},{6,7},{7,6},{8,9},{9,8},{10,11... | collective-permute-start | bytes 589832 | tf_op jit(solution)/shard_map/ppermute | solution.py:557
  60.8 15.1 %collective-permute-start.7 = (f32[4,64,256]{2,1,0:T(8,128)S(1)}, f32[4,64,256]{2,1,0:T(8,128)S(1)}, u32[]{:S(2)}, u32[]{:S(2)}) collective-permute-start(f32[4,64,256]{2,1,0:T(8,128)S(1)} %collective-permute-done.6.refs_4_), channel_id=1, source_target_pairs={{0,2},{1,3},{2,0},{3,1},{4,6},{5,7},{6,4},{7,5},{8,10},{9,11},{10,... | collective-permute-start | bytes 786440 | tf_op jit(solution)/shard_map/ppermute | solution.py:557
  72.8 13.7 %collective-permute-start.8 = (f32[4,64,256]{2,1,0:T(8,128)S(1)}, f32[4,64,256]{2,1,0:T(8,128)S(1)}, u32[]{:S(2)}, u32[]{:S(2)}) collective-permute-start(f32[4,64,256]{2,1,0:T(8,128)S(1)} %collective-permute-done.6.refs_4_), channel_id=1, source_target_pairs={{0,4},{1,5},{2,6},{3,7},{4,0},{5,1},{6,2},{7,3},{8,12},{9,13},{10,... | collective-permute-start | bytes 786440 | tf_op jit(solution)/shard_map/ppermute | solution.py:557
  74.4 12.1 %collective-permute-start.9 = (f32[4,64,256]{2,1,0:T(8,128)S(1)}, f32[4,64,256]{2,1,0:T(8,128)S(1)}, u32[]{:S(2)}, u32[]{:S(2)}) collective-permute-start(f32[4,64,256]{2,1,0:T(8,128)S(1)} %collective-permute-done.6.refs_4_), channel_id=1, source_target_pairs={{0,6},{1,7},{2,4},{3,5},{4,2},{5,3},{6,0},{7,1},{8,14},{9,15},{10,... | collective-permute-start | bytes 786440 | tf_op jit(solution)/shard_map/ppermute | solution.py:557
  75.9 10.6 %collective-permute-start.10 = (f32[256,256]{1,0:T(8,128)S(1)}, f32[256,256]{1,0:T(8,128)S(1)}, u32[]{:S(2)}, u32[]{:S(2)}) collective-permute-start(f32[256,256]{1,0:T(8,128)S(1)} %copy-done.20), channel_id=1, source_target_pairs={{0,1},{1,0},{2,3},{3,2},{4,5},{5,4},{6,7},{7,6},{8,9},{9,8},{10,11... | collective-permute-start | bytes 786440 | tf_op jit(solution)/shard_map/ppermute | solution.py:557
  130.6 12.8 %collective-permute-start.21 = (f32[72,256]{1,0:T(8,128)}, f32[72,256]{1,0:T(8,128)S(1)}, u32[]{:S(2)}, u32[]{:S(2)}) collective-permute-start(f32[72,256]{1,0:T(8,128)} %get-tuple-element.43.refs_8_), channel_id=1, source_target_pairs={{0,1},{1,0},{2,3},{3,2},{4,5},{5,4},{6,7},{7,6},{8,9},{9,8},{10,11... | collective-permute-start | bytes 221192 | tf_op jit(solution)/shard_map/ppermute | solution.py:557
  131.7 11.7 %collective-permute-start.22 = (f32[72,256]{1,0:T(8,128)S(1)}, f32[72,256]{1,0:T(8,128)S(1)}, u32[]{:S(2)}, u32[]{:S(2)}) collective-permute-start(f32[72,256]{1,0:T(8,128)S(1)} %collective-permute-done.18.refs_9_), channel_id=1, source_target_pairs={{0,1},{1,0},{2,3},{3,2},{4,5},{5,4},{6,7},{7,6},{8,9},{9,8},{10,11... | collective-permute-start | bytes 221192 | tf_op jit(solution)/shard_map/ppermute | solution.py:557
  134.0 9.4 %collective-permute-start.23 = (f32[72,256]{1,0:T(8,128)S(1)}, f32[72,256]{1,0:T(8,128)S(1)}, u32[]{:S(2)}, u32[]{:S(2)}) collective-permute-start(f32[72,256]{1,0:T(8,128)S(1)} %collective-permute-done.19.refs_10_), channel_id=1, source_target_pairs={{0,1},{1,0},{2,3},{3,2},{4,5},{5,4},{6,7},{7,6},{8,9},{9,8},{10,11... | collective-permute-start | bytes 221192 | tf_op jit(solution)/shard_map/ppermute | solution.py:557
  142.9 97.6 %collective-permute-start.41 = (f32[4,2,64,1024]{3,2,1,0:T(8,128)}, f32[4,2,64,1024]{3,2,1,0:T(8,128)S(1)}, u32[]{:S(2)}, u32[]{:S(2)}) collective-permute-start(f32[4,2,64,1024]{3,2,1,0:T(8,128)} %bitcast.35), channel_id=1, source_target_pairs={{0,1},{1,0},{2,3},{3,2},{4,5},{5,4},{6,7},{7,6},{8,9},{9,8},{10,11... | collective-permute-start | bytes 6291464 | tf_op jit(solution)/shard_map/ppermute | solution.py:557
  177.3 63.2 %collective-permute-start.42 = (f32[4,2,64,1024]{3,2,1,0:T(8,128)}, f32[4,2,64,1024]{3,2,1,0:T(8,128)}, u32[]{:S(2)}, u32[]{:S(2)}) collective-permute-start(f32[4,2,64,1024]{3,2,1,0:T(8,128)} %bitcast.36), channel_id=1, source_target_pairs={{0,1},{1,0},{2,3},{3,2},{4,5},{5,4},{6,7},{7,6},{8,9},{9,8},{10,11... | collective-permute-start | bytes 6291464 | tf_op jit(solution)/shard_map/ppermute | solution.py:557
  193.1 10.7 %collective-permute-start.29 = (f32[8,256]{1,0:T(8,128)}, f32[8,256]{1,0:T(8,128)S(1)}, u32[]{:S(2)}, u32[]{:S(2)}) collective-permute-start(f32[8,256]{1,0:T(8,128)} %last_dots.1), channel_id=1, source_target_pairs={{0,2},{1,3},{2,0},{3,1},{4,6},{5,7},{6,4},{7,5},{8,10},{9,11},{10,... | collective-permute-start | bytes 24584 | tf_op jit(solution)/shard_map/ppermute | solution.py:557
  193.7 10.2 %collective-permute-start.30 = (f32[8,256]{1,0:T(8,128)}, f32[8,256]{1,0:T(8,128)S(1)}, u32[]{:S(2)}, u32[]{:S(2)}) collective-permute-start(f32[8,256]{1,0:T(8,128)} %last_dots.1), channel_id=1, source_target_pairs={{0,4},{1,5},{2,6},{3,7},{4,0},{5,1},{6,2},{7,3},{8,12},{9,13},{10,... | collective-permute-start | bytes 24584 | tf_op jit(solution)/shard_map/ppermute | solution.py:557
  194.1 10.2 %collective-permute-start.31 = (f32[8,256]{1,0:T(8,128)}, f32[8,256]{1,0:T(8,128)S(1)}, u32[]{:S(2)}, u32[]{:S(2)}) collective-permute-start(f32[8,256]{1,0:T(8,128)} %last_dots.1), channel_id=1, source_target_pairs={{0,6},{1,7},{2,4},{3,5},{4,2},{5,3},{6,0},{7,1},{8,14},{9,15},{10,... | collective-permute-start | bytes 24584 | tf_op jit(solution)/shard_map/ppermute | solution.py:557
  203.8 11.7 %collective-permute-start.37 = (f32[4,2,64,256]{3,2,1,0:T(8,128)}, f32[4,2,64,256]{3,2,1,0:T(8,128)S(1)}, u32[]{:S(2)}, u32[]{:S(2)}) collective-permute-start(f32[4,2,64,256]{3,2,1,0:T(8,128)} %get-tuple-element.51), channel_id=1, source_target_pairs={{0,1},{1,0},{2,3},{3,2},{4,5},{5,4},{6,7},{7,6},{8,9},{9,8},{10,11... | collective-permute-start | bytes 1572872 | tf_op jit(solution)/shard_map/ppermute | solution.py:557
  214.3 12.1 %collective-permute-start.35 = (f32[2,64,256]{2,1,0:T(8,128)S(1)}, f32[2,64,256]{2,1,0:T(8,128)S(1)}, u32[]{:S(2)}, u32[]{:S(2)}) collective-permute-start(f32[2,64,256]{2,1,0:T(8,128)S(1)} %get-tuple-element.67), channel_id=1, source_target_pairs={{0,16},{8,24},{16,0},{24,8},{1,17},{9,25},{17,1},{25,9},{2,18},{10... | collective-permute-start | bytes 393224 | tf_op jit(solution)/shard_map/ppermute | solution.py:702
  215.6 10.9 %collective-permute-start.36 = (f32[2,64,256]{2,1,0:T(8,128)S(1)}, f32[2,64,256]{2,1,0:T(8,128)S(1)}, u32[]{:S(2)}, u32[]{:S(2)}) collective-permute-start(f32[2,64,256]{2,1,0:T(8,128)S(1)} %get-tuple-element.66), channel_id=1, source_target_pairs={{0,24},{8,0},{16,8},{24,16},{1,25},{9,1},{17,9},{25,17},{2,26},{10... | collective-permute-start | bytes 393224 | tf_op jit(solution)/shard_map/ppermute | solution.py:702
  220.8 9.3 %collective-permute-start.38 = (f32[2,64,256]{2,1,0:T(8,128)S(1)}, f32[2,64,256]{2,1,0:T(8,128)S(1)}, u32[]{:S(2)}, u32[]{:S(2)}) collective-permute-start(f32[2,64,256]{2,1,0:T(8,128)S(1)} %get-tuple-element.62), channel_id=1, source_target_pairs={{0,8},{8,16},{16,24},{24,0},{1,9},{9,17},{17,25},{25,1},{2,10},{10... | collective-permute-start | bytes 393224 | tf_op jit(solution)/shard_map/ppermute | solution.py:702
  226.4 10.7 %collective-permute-start.39 = (f32[2,64,256]{2,1,0:T(8,128)S(1)}, f32[2,64,256]{2,1,0:T(8,128)S(1)}, u32[]{:S(2)}, u32[]{:S(2)}) collective-permute-start(f32[2,64,256]{2,1,0:T(8,128)S(1)} %get-tuple-element.64), channel_id=1, source_target_pairs={{0,16},{8,24},{16,0},{24,8},{1,17},{9,25},{17,1},{25,9},{2,18},{10... | collective-permute-start | bytes 393224 | tf_op jit(solution)/shard_map/ppermute | solution.py:702
  226.4 13.4 %collective-permute-start.40 = (f32[2,64,256]{2,1,0:T(8,128)S(1)}, f32[2,64,256]{2,1,0:T(8,128)S(1)}, u32[]{:S(2)}, u32[]{:S(2)}) collective-permute-start(f32[2,64,256]{2,1,0:T(8,128)S(1)} %get-tuple-element.63), channel_id=1, source_target_pairs={{0,24},{8,0},{16,8},{24,16},{1,25},{9,1},{17,9},{25,17},{2,26},{10... | collective-permute-start | bytes 393224 | tf_op jit(solution)/shard_map/ppermute | solution.py:702
  (55 other events, 343.9 us)

commit v2 on v1

--- a/solution.py
+++ b/solution.py
@@ -11,15 +11,16 @@
 HIGHEST = lax.Precision.HIGHEST
 F32 = jnp.float32
 BF16 = jnp.bfloat16
-VMEM_LIMIT = 60 * 1024 * 1024
+MIB = 1024 * 1024
+APPLY_LIMIT = 16
 
 
 VM = pl.BlockSpec(memory_space=pltpu.VMEM)
 ANY = pl.BlockSpec(memory_space=pl.ANY)
 
 
-def params():
-    return pltpu.CompilerParams(vmem_limit_bytes=VMEM_LIMIT)
+def params(limit=4):
+    return pltpu.CompilerParams(vmem_limit_bytes=limit * MIB)
 
 
 def cost(flops, nbytes):
@@ -118,7 +119,8 @@
 
 
 def observe_kernel(width, nmem, *refs):
-    block_refs, (members_ref, obs_ref, joint_ref, other_ref, blocks) = refs[:nmem], refs[nmem:]
+    block_refs = refs[:nmem]
+    members_ref, obs_ref, joint_ref, other_ref, members_mine_ref, members_other_ref, blocks = refs[nmem:]
     _, part, _ = block_refs[0].shape
     count, levels, rows, lon = members_ref.shape
     me = lax.axis_index("mem")
@@ -146,6 +148,9 @@
 
     step = 8
     half_count = count // 2
+    for i in range(half_count):
+        members_mine_ref[i] = members_ref[parity * half_count + i]
+        members_other_ref[i] = members_ref[(1 - parity) * half_count + i]
 
     def one(index, carry):
         start = pl.multiple_of(index * step, step)
@@ -231,49 +236,25 @@
     if not first:
         length_ref = refs[0]
         refs = refs[1:]
-    (seen, value, inverse, cn_high, cn_low, members, xa_high, xa_low, xb_high, xb_low, w_high, w_low,
-     back_high, back_low, sems, seen_sems, inv_sems, back_sems) = refs
+    seen, value, xa_high, xa_low, xb_high, xb_low, w_high, w_low = refs
     count, nlat, slots = seen.shape
     rows = nlat // nlat_blocks
     wide = 2 * rows
     nblocks = slots // width
     per = LANES // width
     nchunks = levels * nblocks
-    quarter = inverse.shape[2]
+    quarter = inverse_refs[0].shape[2]
     lon = quarter * nblocks
-    parity = lax.axis_index("lat") % 2
     me_mem = lax.axis_index("mem")
+    members_refs = (members_ref, members_sib_ref)
 
     def rotated(block):
         return lax.rem(block - me_mem + nblocks, nblocks)
 
     half_blocks = nlat_blocks // 2
-    seen_copies = [
-        pltpu.make_async_copy(
-            ref.at[pl.ds(2, count)] if number < half_blocks else ref,
-            seen.at[:, pl.ds(number * rows, rows)],
-            seen_sems.at[number],
-        )
-        for number, ref in enumerate(seen_refs)
-    ]
-
-    def inverse_copies(chunk):
-        return [
-            pltpu.make_async_copy(
-                ref.at[chunk], inverse.at[chunk, pl.ds(side * (nlat // 2), nlat // 2)], inv_sems.at[chunk, side]
-            )
-            for side, ref in enumerate(inverse_refs)
-        ]
-
-    late = [
-        pltpu.make_async_copy(cn_high_ref, cn_high, sems.at[0]),
-        pltpu.make_async_copy(cn_low_ref, cn_low, sems.at[1]),
-        pltpu.make_async_copy(members_ref.at[pl.ds(parity * count, count)], members.at[0], sems.at[2]),
-        pltpu.make_async_copy(members_sib_ref.at[pl.ds(parity * count, count)], members.at[1], sems.at[3]),
-    ]
-    for copy in inverse_copies(0) + seen_copies + inverse_copies(1):
-        copy.start()
-
+    for number, ref in enumerate(seen_refs):
+        for m in range(count):
+            seen[m, number * rows : (number + 1) * rows, :] = ref[m + 2 if number < half_blocks else m]
     if first:
         for side, ref in enumerate(value_refs):
             value[side * (nlat // 2) : (side + 1) * (nlat // 2), :] = ref[...]
@@ -305,7 +286,8 @@
             sources = [jnp.where(inside, seen[m, part, columns] * numbers, 0.0) for m in range(count)]
             for half in range(quarter // LANES):
                 cols = slice(half * LANES, (half + 1) * LANES)
-                index = inverse[chunk, part, cols]
+                inner = start % (nlat // 2)
+                index = inverse_refs[start // (nlat // 2)][chunk, inner : inner + tall, cols]
                 for m in range(count):
                     high, low = split(take_lanes(sources[m], index))
                     x_high[m, part, cols] = high
@@ -327,37 +309,13 @@
             where = pl.ds(pl.multiple_of((m * levels + level) * rows, rows), rows)
             for side in range(2):
                 high, low = split(both[wide + side * rows : wide + (side + 1) * rows])
-                back_high[side, where, cols] = high
-                back_low[side, where, cols] = low
-
-    for copy in inverse_copies(0) + seen_copies:
-        copy.wait()
-    for copy in inverse_copies(2):
-        copy.start()
+                back_high_refs[side][where, cols] = high
+                back_low_refs[side][where, cols] = low
+
     build(0, xa_high, xa_low)
 
     def one(pair, carry):
         chunk = pair * 2
-        for copy in inverse_copies(chunk + 1):
-            copy.wait()
-
-        @pl.when(chunk + 2 < nchunks)
-        def _():
-            for copy in inverse_copies(chunk + 2):
-                copy.wait()
-            for copy in inverse_copies(chunk + 3):
-                copy.start()
-
-        @pl.when(chunk + 4 < nchunks)
-        def _():
-            for copy in inverse_copies(chunk + 4):
-                copy.start()
-
-        @pl.when(pair == 0)
-        def _():
-            for copy in late:
-                copy.start()
-
         build(chunk + 1, xb_high, xb_low)
         multiply(chunk, xa_high, xa_low)
         build(jnp.minimum(chunk + 2, nchunks - 1), xa_high, xa_low)
@@ -366,15 +324,6 @@
 
     lax.fori_loop(0, nchunks // 2, one, 0)
 
-    back_copies = [
-        pltpu.make_async_copy(source.at[side], refs_[side], back_sems.at[kind, side])
-        for kind, (source, refs_) in enumerate(((back_high, back_high_refs), (back_low, back_low_refs)))
-        for side in range(2)
-    ]
-    for copy in back_copies:
-        copy.start()
-    for copy in late:
-        copy.wait()
     tile = 2 * LANES
     deep = levels * wide
 
@@ -387,14 +336,14 @@
         for member in range(count):
             part = slice(member * deep, (member + 1) * deep)
             product = (
-                dot(w_high[part, :], cn_high[:, cols])
-                + dot(w_low[part, :], cn_high[:, cols])
-                + dot(w_high[part, :], cn_low[:, cols])
+                dot(w_high[part, :], cn_high_ref[:, cols])
+                + dot(w_low[part, :], cn_high_ref[:, cols])
+                + dot(w_high[part, :], cn_low_ref[:, cols])
             )
             for level in range(levels):
                 for side in range(2):
                     top = level * wide + side * rows
-                    term = members[side, member, level, :, cols] * product[top : top + rows]
+                    term = members_refs[side][member, level, :, cols] * product[top : top + rows]
                     old = totals[side][level]
                     totals[side][level] = term if old is None else old + term
         for side in range(2):
@@ -418,8 +367,6 @@
                     ]
 
                 seen_out_refs[side][part, columns] = pick_cells(cells, [read], width, levels, quarter, lon)[0]
-    for copy in back_copies:
-        copy.wait()
 
 
 def answer_kernel(width, nparts, *refs):
@@ -472,71 +419,70 @@
     high_ref[...], low_ref[...] = split(ordered[...].T)
 
 
-def covariance_kernel(root_ref, high_ref, low_ref, root_high_ref, root_low_ref, root_high, root_low):
-    tile = high_ref.shape[1]
+def covariance_kernel(root_ref, high_ref, low_ref, root_high_ref, root_low_ref):
+    tile = 2 * LANES
     numbers = (((1,), (1,)), ((), ()))
-
-    @pl.when(pl.program_id(0) == 0)
-    def _():
-        root_high[...], root_low[...] = split(root_ref[...])
+    root_high_ref[...], root_low_ref[...] = split(root_ref[...])
 
     def times(a, b):
         return lax.dot_general(a, b, numbers, preferred_element_type=F32)
 
-    here = pl.ds(pl.multiple_of(pl.program_id(0) * tile, tile), tile)
-    high, low = root_high[here, :], root_low[here, :]
-    root_high_ref[...], root_low_ref[...] = high, low
-    total = times(root_high[...], high) + times(root_low[...], high) + times(root_high[...], low)
-    high_ref[...], low_ref[...] = split(total)
+    def panel(column, carry):
+        here = pl.ds(pl.multiple_of(column * tile, tile), tile)
+        high, low = root_high_ref[here, :], root_low_ref[here, :]
+        total = times(root_high_ref[...], high) + times(root_low_ref[...], high) + times(root_high_ref[...], low)
+        high_ref[:, here], low_ref[:, here] = split(total)
+        return carry
+
+    lax.fori_loop(0, root_ref.shape[0] // tile, panel, 0)
 
 
 def product_kernel(a_high_ref, a_low_ref, b_high_ref, b_low_ref, out_ref):
-    out_ref[...] = (
-        dot(a_high_ref[...], b_high_ref[...])
-        + dot(a_low_ref[...], b_high_ref[...])
-        + dot(a_high_ref[...], b_low_ref[...])
-    )
+    tile = 2 * LANES
+
+    def panel(column, carry):
+        here = pl.ds(pl.multiple_of(column * tile, tile), tile)
+        out_ref[:, here] = (
+            dot(a_high_ref[...], b_high_ref[:, here])
+            + dot(a_low_ref[...], b_high_ref[:, here])
+            + dot(a_high_ref[...], b_low_ref[:, here])
+        )
+        return carry
+
+    lax.fori_loop(0, b_high_ref.shape[1] // tile, panel, 0)
 
 
 def product(a_high, a_low, b_high, b_low):
     rows, deep = a_high.shape
     wide = b_high.shape[1]
-    tile = 2 * LANES
-    whole = pl.BlockSpec((rows, deep), lambda i: (0, 0))
-    panel = pl.BlockSpec((deep, tile), lambda i: (0, i))
     return pl.pallas_call(
         product_kernel,
-        grid=(wide // tile,),
-        in_specs=[whole, whole, panel, panel],
-        out_specs=pl.BlockSpec((rows, tile), lambda i: (0, i)),
+        in_specs=[VM] * 4,
+        out_specs=VM,
         out_shape=jax.ShapeDtypeStruct((rows, wide), F32),
-        compiler_params=params(),
+        compiler_params=params(6),
         cost_estimate=cost(6 * rows * deep * wide, 4 * (rows * deep + deep * wide + rows * wide)),
         name="lon_product",
     )(a_high, a_low, b_high, b_low)
 
 
-def final_kernel(parity_ref, dots_ref, length_ref, q0_ref, q1_ref, a0_ref, b0_ref, a1_ref, b1_ref,
-                 increment_ref, control_ref, lengths):
-    index = pl.program_id(0)
-
-    @pl.when(index == 0)
-    def _():
-        top = jnp.sum(dots_ref[:1, :], axis=1, keepdims=True)
-        bottom = jnp.sum(dots_ref[1:2, :], axis=1, keepdims=True)
-        lengths[0] = length_ref[...]
-        lengths[1] = jnp.broadcast_to(top / bottom, length_ref.shape)
-        increment_ref[...] = -(lengths[0, :1, :1] * q0_ref[...] + lengths[1, :1, :1] * q1_ref[...])
-
-    half = pl.num_programs(0) // 2
-
-    @pl.when(index < half)
-    def _():
-        control_ref[...] = -(lengths[0, :1, :1] * a0_ref[...] + lengths[1, :1, :1] * a1_ref[...])
-
-    @pl.when(index >= half)
-    def _():
-        control_ref[...] = -(lengths[0, :1, :1] * b0_ref[...] + lengths[1, :1, :1] * b1_ref[...])
+def final_kernel(dots_ref, length_ref, q0_ref, q1_ref, a0_ref, b0_ref, a1_ref, b1_ref,
+                 increment_ref, control_ref, control, sems):
+    parity = lax.axis_index("lat") % 2
+    half = a0_ref.shape[0]
+    length0 = length_ref[:1, :1]
+    length1 = jnp.sum(dots_ref[:1, :], axis=1, keepdims=True) / jnp.sum(dots_ref[1:2, :], axis=1, keepdims=True)
+    copies = []
+    for side, (first_ref, second_ref) in enumerate(((a0_ref, a1_ref), (b0_ref, b1_ref))):
+        for i in range(half):
+            number = side * half + i
+            member = (parity ^ side) * half + i
+            control[number] = -(length0 * first_ref[i] + length1 * second_ref[i])
+            copies.append(pltpu.make_async_copy(control.at[number], control_ref.at[member], sems.at[number]))
+            copies[-1].start()
+    increment_ref[...] = -(length0 * q0_ref[...] + length1 * q1_ref[...])
+    for copy in copies:
+        copy.wait()
 
 
 def per_device(members, lat_root, lon_root, innovation, obs_weight, obs_mask, obs_cell):
@@ -547,8 +493,6 @@
     width = obs_cell.shape[1]
     slots = width * nmem
     quarter = lon // nmem
-    me_lat = lax.axis_index("lat")
-    parity = me_lat % 2
     shape = jax.ShapeDtypeStruct
     chips = list(range(0, nlat_dev, 2))
     order = chips + [bits + 1 for bits in chips]
@@ -570,18 +514,20 @@
         out_specs=VM,
         out_shape=shape((3, rows * width // LANES, LANES), F32),
         scratch_shapes=[pltpu.VMEM((rows, LANES), jnp.int32)] + [pltpu.VMEM((rows, LANES), F32)] * 2,
-        compiler_params=params(),
+        compiler_params=params(2),
         name="sort_slots",
     )(obs_cell, obs_weight, obs_mask, innovation)
     blocks = around_mem(block)
-    obs, joint, other = pl.pallas_call(
+    obs, joint, other, members_mine, members_sib = pl.pallas_call(
         functools.partial(observe_kernel, width, nmem),
         in_specs=[VM] * (nmem + 1),
-        out_specs=[VM] * 3,
+        out_specs=[VM] * 5,
         out_shape=[
             shape((3, rows, slots), F32),
             shape((2 + half_count, rows, slots), F32),
             shape((half_count, rows, slots), F32),
+            shape((half_count, levels, rows, lon), F32),
+            shape((half_count, levels, rows, lon), F32),
         ],
         scratch_shapes=[pltpu.VMEM((nmem, *block.shape), F32)],
         compiler_params=params(),
@@ -593,7 +539,7 @@
     joints = direct(joint)
     seens = joints + direct(received)
     obs_sib = swap(obs, 1)
-    members_sib = swap(members, 1)
+    members_sib = swap(members_sib, 1)
 
     lhs_high, lhs_low = pl.pallas_call(
         functools.partial(lat_kernel, order),
@@ -612,13 +558,10 @@
     )(lat_root)
     cn_high, cn_low, lon_high, lon_low = pl.pallas_call(
         covariance_kernel,
-        grid=(lon // (2 * LANES),),
-        in_specs=[pl.BlockSpec((lon, lon), lambda i: (0, 0))],
-        out_specs=[pl.BlockSpec((lon, 2 * LANES), lambda i: (0, i))] * 2
-        + [pl.BlockSpec((2 * LANES, lon), lambda i: (i, 0))] * 2,
+        in_specs=[VM],
+        out_specs=[VM] * 4,
         out_shape=[shape((lon, lon), BF16)] * 4,
-        scratch_shapes=[pltpu.VMEM((lon, lon), BF16)] * 2,
-        compiler_params=params(),
+        compiler_params=params(6),
         cost_estimate=cost(6 * lon**3, 12 * lon * lon),
         name="lon_covariance",
     )(lon_root)
@@ -653,32 +596,13 @@
             outs.append(shape((8, LANES), F32))
         return pl.pallas_call(
             functools.partial(apply_kernel, width, levels, nlat_dev, first),
-            in_specs=[ANY] * nlat_dev
-            + ([] if first else [VM] * nlat_dev)
-            + [VM] * 2
-            + [ANY] * 2
-            + [VM] * 4
-            + [ANY] * 4,
-            out_specs=[VM] * 4 + [ANY] * 4 + [VM] * (len(outs) - 8),
+            in_specs=[VM] * (nlat_dev * (1 if first else 2) + 12),
+            out_specs=[VM] * len(outs),
             out_shape=outs,
-            scratch_shapes=[
-                pltpu.VMEM((half_count, nlat, slots), F32),
-                pltpu.VMEM((nlat, slots), F32),
-                pltpu.VMEM((nchunks, nlat, quarter), jnp.int32),
-                pltpu.VMEM((lon, lon), BF16),
-                pltpu.VMEM((lon, lon), BF16),
-                pltpu.VMEM((2, half_count, levels, rows, lon), F32),
-            ]
+            scratch_shapes=[pltpu.VMEM((half_count, nlat, slots), F32), pltpu.VMEM((nlat, slots), F32)]
             + [pltpu.VMEM((half_count, nlat, quarter), BF16)] * 4
-            + [pltpu.VMEM((2 * tall, lon), BF16)] * 2
-            + [pltpu.VMEM((2, tall, lon), BF16)] * 2
-            + [
-                pltpu.SemaphoreType.DMA((4,)),
-                pltpu.SemaphoreType.DMA((nlat_dev,)),
-                pltpu.SemaphoreType.DMA((nchunks, 2)),
-                pltpu.SemaphoreType.DMA((2, 2)),
-            ],
-            compiler_params=params(),
+            + [pltpu.VMEM((2 * tall, lon), BF16)] * 2,
+            compiler_params=params(APPLY_LIMIT),
             cost_estimate=cost(12 * tall * lon * (nlat + lon), 30 * 2**20),
             name="apply_first" if first else "apply_next",
         )(
@@ -692,7 +616,7 @@
             obs_sib,
             cn_high,
             cn_low,
-            members,
+            members_mine,
             members_sib,
         )
 
@@ -745,25 +669,15 @@
     dots = sum(dots_parts[1:], dots_parts[0])
     dots = dots + swap(dots, 1)
 
-    small = pl.BlockSpec((8, slots), lambda i, par: (0, 0))
-    tiny = pl.BlockSpec((8, LANES), lambda i, par: (0, 0))
-    piece = pl.BlockSpec((levels, rows, quarter), lambda i, par: (0, 0, 0))
-    near = pl.BlockSpec((1, levels, rows, lon), lambda i, par: (jnp.minimum(i, half_count - 1), 0, 0, 0))
-    far = pl.BlockSpec((1, levels, rows, lon), lambda i, par: (jnp.maximum(i - half_count, 0), 0, 0, 0))
-    put = pl.BlockSpec((1, levels, rows, lon), lambda i, par: ((i + par[0] * half_count) % count, 0, 0, 0))
     return pl.pallas_call(
         final_kernel,
-        grid_spec=pltpu.PrefetchScalarGridSpec(
-            num_scalar_prefetch=1,
-            grid=(count,),
-            in_specs=[small, tiny, piece, piece, near, far, near, far],
-            out_specs=[piece, put],
-            scratch_shapes=[pltpu.VMEM((2, 8, LANES), F32)],
-        ),
+        in_specs=[VM] * 8,
+        out_specs=[VM, ANY],
         out_shape=[shape((levels, rows, quarter), F32), shape(members.shape, F32)],
-        compiler_params=params(),
+        scratch_shapes=[pltpu.VMEM(members.shape, F32), pltpu.SemaphoreType.DMA((count,))],
+        compiler_params=params(8),
         name="final",
-    )(parity[None], dots, length0, quarter0, quarter1, mine0, other0, mine1, other1)
+    )(dots, length0, quarter0, quarter1, mine0, other0, mine1, other1)
 
 
 def solution(mesh):

time: 251 us -> 197 us (0.78)
  Pallas kernels: 129 us -> 84.3 us
  waiting for transfers between devices: 71.4 us -> 66.9 us
  other arithmetic: 2.97 us -> 0.25 us
  local copies, waits for them, and re-layouts: 7.88 us -> 5.27 us
    pallas_call x6, Pallas kernels: 49.1 us -> 27 us  [the longest x4 16.1 us: product(): pl.pallas_call(product_kernel, in_specs=[VM] * 4, out_specs=VM, out_shape...]
    pallas_call x2, Pallas kernels: 50.4 us -> 39.6 us  [apply(): pl.pallas_call(functools.partial(apply_kernel, width, levels, nlat_dev, f...]
    ppermute x28, waiting for transfers between devices: 39 us -> 33 us  [swap(): return lax.ppermute(value, 'lat', [(i, i ^ bits) for i in range(nlat_dev)])]
    pallas_call x1, Pallas kernels: 5.45 us -> 2.57 us  [per_device(): pl.pallas_call(functools.partial(observe_kernel, width, nmem), in_specs=[...]
    unnamed x72 -> x14, local copies, waits for them, and re-layouts: 7.83 us -> 5.22 us
  transfers between devices with their start and end apart: 43 -> 43, of which waited for: 20 -> 21; matrix products, arithmetic and copies ran while one was open for 1% -> 0% of each run, Pallas kernels for 37% -> 29%
where the time goes in v2:
time: 197 us
  Pallas kernels  84.3 us (43%)
  waiting for transfers between devices  66.9 us (34%)
  starting transfers between devices  39 us (20%)
  local copies, waits for them, and re-layouts  5.27 us (3%)
    pallas_call x2, Pallas kernels, apply(): pl.pallas_call(functools.partial(apply_kernel, width, levels, nlat_dev, f...  39.6 us
    ppermute x28, waiting for transfers between devices, swap(): return lax.ppermute(value, 'lat', [(i, i ^ bits) for i in range(nlat_dev)])  33 us
    ppermute x6, waiting for transfers between devices, to_quarters(): lax.ppermute(image[hop], 'mem', [(i, (i + hop) % nmem) for i in range(nme...  19.1 us
    ppermute x28, starting transfers between devices, swap(): return lax.ppermute(value, 'lat', [(i, i ^ bits) for i in range(nlat_dev)])  16.8 us
    pallas_call x4, Pallas kernels, product(): pl.pallas_call(product_kernel, in_specs=[VM] * 4, out_specs=VM, out_shape...  16.1 us
    ppermute x9, waiting for transfers between devices, around_mem(): lax.ppermute(value, 'mem', [(i, (i + hop) % nmem) for i in range(nmem)])  14.9 us
    ppermute x9, starting transfers between devices, around_mem(): lax.ppermute(value, 'mem', [(i, (i + hop) % nmem) for i in range(nmem)])  14.5 us
    pallas_call x1, Pallas kernels, per_device(): pl.pallas_call(functools.partial(inverse_kernel, width, levels, lon, nlat...  11.5 us
  transfers between devices with their start and end apart: 43, of which 21 were waited for; matrix products, arithmetic and copies ran while one was open for 0% of the time, Pallas kernels for 29%

profile of v2, /device:TPU:0, one launch (start us, length us, event | category | flops | bytes accessed | tf_op | source)
XLA Modules:
  0.0 196.8 jit_solution(4872225806338001995)
XLA Ops:
  5.3 5.1 %collective-permute-start.2 = (f32[3,32,128]{2,1,0:T(8,128)S(1)}, f32[3,32,128]{2,1,0:T(8,128)S(1)}, u32[]{:S(2)}, u32[]{:S(2)}) collective-permute-start(f32[3,32,128]{2,1,0:T(8,128)S(1)} %sort_slots.1.refs_0_), channel_id=1, source_target_pairs={{0,24},{8,0},{16,8},{24,16},{1,25},{9,1},{17,9},{25,17},{2,26},{10... | collective-permute-start | bytes 147464 | tf_op jit(solution)/shard_map/ppermute | solution.py:508
  12.5 2.9 %collective-permute-done.1.refs_2_ = f32[3,32,128]{2,1,0:T(8,128)S(1)} collective-permute-done((f32[3,32,128]{2,1,0:T(8,128)S(1)}, f32[3,32,128]{2,1,0:T(8,128)S(1)}, u32[]{:S(2)}, u32[]{:S(2)}) %collective-permute-start.1) | collective-permute-done | bytes 49184 | tf_op jit(solution)/shard_map/ppermute | solution.py:508
  18.5 2.6 %members_at_slots.1 = (f32[3,64,256]{2,1,0:T(8,128)S(1)}, f32[6,64,256]{2,1,0:T(8,128)S(1)}, f32[4,64,256]{2,1,0:T(8,128)S(1)}, f32[4,2,64,1024]{3,2,1,0:T(8,128)S(1)}, f32[4,2,64,1024]{3,2,1,0:T(8,128)S(1)}) custom-call(f32[3,32,128]{2,1,0:T(8,128)S(1)} %sort_slots.1.refs_0_, f32[3,32,128]{2,1,0:T(8,128)S(1)} %collective-permute-done.refs_1_, ...), custom_call_target="tpu_custom_call" | custom-call | flops 100000000 | bytes 4194304 | tf_op jit(solution)/shard_map/members_at_slots/pallas_call | solution.py:521
  24.6 9.4 %collective-permute-done.5.refs_3_ = f32[6,64,256]{2,1,0:T(8,128)S(1)} collective-permute-done((f32[6,64,256]{2,1,0:T(8,128)S(1)}, f32[6,64,256]{2,1,0:T(8,128)S(1)}, u32[]{:S(2)}, u32[]{:S(2)}) %collective-permute-start.5) | collective-permute-done | bytes 393248 | tf_op jit(solution)/shard_map/ppermute | solution.py:501
  34.1 5.8 %collective-permute-done.4.refs_2_ = f32[6,64,256]{2,1,0:T(8,128)S(1)} collective-permute-done((f32[6,64,256]{2,1,0:T(8,128)S(1)}, f32[6,64,256]{2,1,0:T(8,128)S(1)}, u32[]{:S(2)}, u32[]{:S(2)}) %collective-permute-start.4) | collective-permute-done | bytes 393248 | tf_op jit(solution)/shard_map/ppermute | solution.py:501
  40.0 11.5 %inverse.1 = (s32[8,256,256]{2,1,0:T(8,128)S(1)}, f32[256,256]{1,0:T(8,128)S(1)}) custom-call(f32[6,64,256]{2,1,0:T(8,128)S(1)} %get-tuple-element.34.refs_0_, f32[6,64,256]{2,1,0:T(8,128)S(1)} %collective-permute-done.3.refs_1_, f32[6,64,256]{2,1,0:T(8,128)S(1)} %collective-permute-done.4.refs_2_, f32[6,64,256]{2,1,0:T(8,128)S(1)} %collective-permute-done.5.refs_3_), custom_call_target="tpu_custom_call" | custom-call | flops 10000000000 | bytes 2097152 | tf_op jit(solution)/shard_map/inverse/pallas_call | solution.py:570
  52.2 3.9 %collective-permute-done.6.refs_4_ = f32[4,64,256]{2,1,0:T(8,128)S(1)} collective-permute-done((f32[4,64,256]{2,1,0:T(8,128)S(1)}, f32[4,64,256]{2,1,0:T(8,128)S(1)}, u32[]{:S(2)}, u32[]{:S(2)}) %collective-permute-start.6) | collective-permute-done | bytes 262176 | tf_op jit(solution)/shard_map/ppermute | solution.py:501
  57.8 8.0 %lon_covariance.1 = (bf16[1024,1024]{1,0:T(8,128)(2,1)S(1)}, bf16[1024,1024]{1,0:T(8,128)(2,1)S(1)}, bf16[1024,1024]{1,0:T(8,128)(2,1)S(1)}, bf16[1024,1024]{1,0:T(8,128)(2,1)S(1)}) custom-call(f32[1024,1024]{1,0:T(8,128)S(1)} %copy-done.5), custom_call_target="tpu_custom_call" | custom-call | flops 6442450944 | bytes 12582912 | tf_op jit(solution)/shard_map/lon_covariance/pallas_call | solution.py:559
  69.2 4.8 %collective-permute-done.8.refs_6_ = f32[4,64,256]{2,1,0:T(8,128)S(1)} collective-permute-done((f32[4,64,256]{2,1,0:T(8,128)S(1)}, f32[4,64,256]{2,1,0:T(8,128)S(1)}, u32[]{:S(2)}, u32[]{:S(2)}) %collective-permute-start.8) | collective-permute-done | bytes 262176 | tf_op jit(solution)/shard_map/ppermute | solution.py:501
  75.0 19.7 %apply_first.1 = (f32[64,256]{1,0:T(8,128)S(1)}, f32[64,256]{1,0:T(8,128)S(1)}, f32[4,2,64,256]{3,2,1,0:T(8,128)S(1)}, f32[4,2,64,256]{3,2,1,0:T(8,128)S(1)}, bf...) custom-call(f32[6,64,256]{2,1,0:T(8,128)S(1)} %get-tuple-element.34., ...), custom_call_target="tpu_custom_call" | custom-call | flops 9663676416 | bytes 31457280 | tf_op jit(solution)/shard_map/apply_first/pallas_call | solution.py:597
  100.3 4.5 %collective-permute-done.16.refs_2_ = f32[64,256]{1,0:T(8,128)S(1)} collective-permute-done((f32[64,256]{1,0:T(8,128)S(1)}, f32[64,256]{1,0:T(8,128)S(1)}, u32[]{:S(2)}, u32[]{:S(2)}) %collective-permute-start.16) | collective-permute-done | bytes 65568 | tf_op jit(solution)/shard_map/ppermute | solution.py:508
  112.1 4.0 %lon_product.5 = f32[512,1024]{1,0:T(8,128)S(1)} custom-call(bf16[512,1024]{1,0:T(8,128)(2,1)S(1)} %get-tuple-element.60.a_high_ref, bf16[512,1024]{1,0:T(8,128)(2,1)S(1)} %get-tuple-element.61.a_low_ref, bf16[1024,1024]{1,0:T(8,128)(2,1)S(1)} %get-tuple-element.58.b_high_ref, bf16[1024,1024]{1,0:T(8,128)(2,1)S(1)} %get-tuple-element.59.b_low_ref), custom_call_target="tpu_custom_call" | custom-call | flops 3221225472 | bytes 8388608 | tf_op jit(solution)/shard_map/lon_product/pallas_call | solution.py:458
  116.3 19.9 %apply_next.1 = (f32[64,256]{1,0:T(8,128)S(1)}, f32[64,256]{1,0:T(8,128)S(1)}, f32[4,2,64,256]{3,2,1,0:T(8,128)S(1)}, f32[4,2,64,256]{3,2,1,0:T(8,128)S(1)}, bf1...) custom-call(f32[6,64,256]{2,1,0:T(8,128)S(1)} %get-tuple-element.34., ...), custom_call_target="tpu_custom_call" | custom-call | flops 9663676416 | bytes 31457280 | tf_op jit(solution)/shard_map/apply_next/pallas_call | solution.py:597
  136.2 4.0 %lon_product.7 = f32[512,1024]{1,0:T(8,128)S(1)} custom-call(bf16[512,1024]{1,0:T(8,128)(2,1)S(1)} %get-tuple-element.64.a_high_ref, bf16[512,1024]{1,0:T(8,128)(2,1)S(1)} %get-tuple-element.65.a_low_ref, bf16[1024,1024]{1,0:T(8,128)(2,1)S(1)} %get-tuple-element.58.b_high_ref, bf16[1024,1024]{1,0:T(8,128)(2,1)S(1)} %get-tuple-element.59.b_low_ref), custom_call_target="tpu_custom_call" | custom-call | flops 3221225472 | bytes 8388608 | tf_op jit(solution)/shard_map/lon_product/pallas_call | solution.py:458
  140.8 3.8 %collective-permute-done.25 = f32[64,256]{1,0:T(8,128)S(1)} collective-permute-done((f32[64,256]{1,0:T(8,128)S(1)}, f32[64,256]{1,0:T(8,128)S(1)}, u32[]{:S(2)}, u32[]{:S(2)}) %collective-permute-start.25) | collective-permute-done | bytes 65568 | tf_op jit(solution)/shard_map/ppermute | solution.py:501
  149.0 5.1 %collective-permute-done.27.refs_2_ = f32[64,256]{1,0:T(8,128)S(1)} collective-permute-done((f32[64,256]{1,0:T(8,128)S(1)}, f32[64,256]{1,0:T(8,128)S(1)}, u32[]{:S(2)}, u32[]{:S(2)}) %collective-permute-start.27) | collective-permute-done | bytes 65568 | tf_op jit(solution)/shard_map/ppermute | solution.py:508
  157.8 4.0 %lon_product.4 = f32[512,1024]{1,0:T(8,128)S(1)} custom-call(bf16[512,1024]{1,0:T(8,128)(2,1)S(1)} %get-tuple-element.56.a_high_ref, bf16[512,1024]{1,0:T(8,128)(2,1)S(1)} %get-tuple-element.57.a_low_ref, bf16[1024,1024]{1,0:T(8,128)(2,1)S(1)} %get-tuple-element.58.b_high_ref, bf16[1024,1024]{1,0:T(8,128)(2,1)S(1)} %get-tuple-element.59.b_low_ref), custom_call_target="tpu_custom_call" | custom-call | flops 3221225472 | bytes 8388608 | tf_op jit(solution)/shard_map/lon_product/pallas_call | solution.py:458
  162.5 4.0 %lon_product.6 = f32[512,1024]{1,0:T(8,128)S(1)} custom-call(bf16[512,1024]{1,0:T(8,128)(2,1)S(1)} %get-tuple-element.62.a_high_ref, bf16[512,1024]{1,0:T(8,128)(2,1)S(1)} %get-tuple-element.63.a_low_ref, bf16[1024,1024]{1,0:T(8,128)(2,1)S(1)} %get-tuple-element.58.b_high_ref, bf16[1024,1024]{1,0:T(8,128)(2,1)S(1)} %get-tuple-element.59.b_low_ref), custom_call_target="tpu_custom_call" | custom-call | flops 3221225472 | bytes 8388608 | tf_op jit(solution)/shard_map/lon_product/pallas_call | solution.py:458
  166.8 3.8 %collective-permute-start.36 = (f32[2,64,256]{2,1,0:T(8,128)S(1)}, f32[2,64,256]{2,1,0:T(8,128)S(1)}, u32[]{:S(2)}, u32[]{:S(2)}) collective-permute-start(f32[2,64,256]{2,1,0:T(8,128)S(1)} %get-tuple-element.70), channel_id=1, source_target_pairs={{0,24},{8,0},{16,8},{24,16},{1,25},{9,1},{17,9},{25,17},{2,26},{10... | collective-permute-start | bytes 393224 | tf_op jit(solution)/shard_map/ppermute | solution.py:626
  170.7 4.3 %collective-permute-done.34 = f32[2,64,256]{2,1,0:T(8,128)S(1)} collective-permute-done((f32[2,64,256]{2,1,0:T(8,128)S(1)}, f32[2,64,256]{2,1,0:T(8,128)S(1)}, u32[]{:S(2)}, u32[]{:S(2)}) %collective-permute-start.34) | collective-permute-done | bytes 131104 | tf_op jit(solution)/shard_map/ppermute | solution.py:626
  175.0 2.8 %collective-permute-start.38 = (f32[2,64,256]{2,1,0:T(8,128)S(1)}, f32[2,64,256]{2,1,0:T(8,128)S(1)}, u32[]{:S(2)}, u32[]{:S(2)}) collective-permute-start(f32[2,64,256]{2,1,0:T(8,128)S(1)} %get-tuple-element.66), channel_id=1, source_target_pairs={{0,8},{8,16},{16,24},{24,0},{1,9},{9,17},{17,25},{25,1},{2,10},{10... | collective-permute-start | bytes 393224 | tf_op jit(solution)/shard_map/ppermute | solution.py:626
  178.8 7.2 %collective-permute-done.35 = f32[2,64,256]{2,1,0:T(8,128)S(1)} collective-permute-done((f32[2,64,256]{2,1,0:T(8,128)S(1)}, f32[2,64,256]{2,1,0:T(8,128)S(1)}, u32[]{:S(2)}, u32[]{:S(2)}) %collective-permute-start.35) | collective-permute-done | bytes 131104 | tf_op jit(solution)/shard_map/ppermute | solution.py:626
  186.6 7.1 %collective-permute-done.39 = f32[2,64,256]{2,1,0:T(8,128)S(1)} collective-permute-done((f32[2,64,256]{2,1,0:T(8,128)S(1)}, f32[2,64,256]{2,1,0:T(8,128)S(1)}, u32[]{:S(2)}, u32[]{:S(2)}) %collective-permute-start.39) | collective-permute-done | bytes 131104 | tf_op jit(solution)/shard_map/ppermute | solution.py:626
  193.7 2.9 %final.1 = (f32[2,64,256]{2,1,0:T(8,128)}, f32[8,2,64,1024]{3,2,1,0:T(8,128)}) custom-call(f32[8,256]{1,0:T(8,128)S(1)} %add.47.dots_ref, f32[8,128]{1,0:T(8,128)S(1)} %get-tuple-element.51.refs_6_.length_ref, f32[2,64,256]{2,1,0:T(8,128)S(1)} %fusion.5.q0_ref, f32[2,64,256]{2,1,0:T(8,128)S(1)} %fusion.2.q1_ref, f32[4,2,64,1024]{3,2,1,0:T(8,128)S(1)} %bitcast.32, ...), custom_call_target="tpu_custom_call" | custom-call | tf_op jit(solution)/shard_map/final/pallas_call | solution.py:672
  (100 shorter events, 44.5 us)
Async XLA Ops:
  21.1 13.0 %collective-permute-start.5 = (f32[6,64,256]{2,1,0:T(8,128)S(1)}, f32[6,64,256]{2,1,0:T(8,128)S(1)}, u32[]{:S(2)}, u32[]{:S(2)}) collective-permute-start(f32[6,64,256]{2,1,0:T(8,128)S(1)} %get-tuple-element.34.refs_0_), channel_id=1, source_target_pairs={{0,6},{1,7},{2,4},{3,5},{4,2},{5,3},{6,0},{7,1},{8,14},{9,15},{10,... | collective-permute-start | bytes 1179656 | tf_op jit(solution)/shard_map/ppermute | solution.py:501
  23.6 16.3 %collective-permute-start.4 = (f32[6,64,256]{2,1,0:T(8,128)S(1)}, f32[6,64,256]{2,1,0:T(8,128)S(1)}, u32[]{:S(2)}, u32[]{:S(2)}) collective-permute-start(f32[6,64,256]{2,1,0:T(8,128)S(1)} %get-tuple-element.34.refs_0_), channel_id=1, source_target_pairs={{0,4},{1,5},{2,6},{3,7},{4,0},{5,1},{6,2},{7,3},{8,12},{9,13},{10,... | collective-permute-start | bytes 1179656 | tf_op jit(solution)/shard_map/ppermute | solution.py:501
  24.1 15.9 %collective-permute-start.3 = (f32[6,64,256]{2,1,0:T(8,128)S(1)}, f32[6,64,256]{2,1,0:T(8,128)S(1)}, u32[]{:S(2)}, u32[]{:S(2)}) collective-permute-start(f32[6,64,256]{2,1,0:T(8,128)S(1)} %get-tuple-element.34.refs_0_), channel_id=1, source_target_pairs={{0,2},{1,3},{2,0},{3,1},{4,6},{5,7},{6,4},{7,5},{8,10},{9,11},{10,... | collective-permute-start | bytes 1179656 | tf_op jit(solution)/shard_map/ppermute | solution.py:501
  24.6 50.3 %collective-permute-start.13 = (f32[4,2,64,1024]{3,2,1,0:T(8,128)S(1)}, f32[4,2,64,1024]{3,2,1,0:T(8,128)S(1)}, u32[]{:S(2)}, u32[]{:S(2)}) collective-permute-start(f32[4,2,64,1024]{3,2,1,0:T(8,128)S(1)} %get-tuple-element.44), channel_id=1, source_target_pairs={{0,1},{1,0},{2,3},{3,2},{4,5},{5,4},{6,7},{7,6},{8,9},{9,8},{10,11... | collective-permute-start | bytes 6291464 | tf_op jit(solution)/shard_map/ppermute | solution.py:501
  51.5 23.5 %collective-permute-start.11 = (s32[8,256,256]{2,1,0:T(8,128)S(1)}, s32[8,256,256]{2,1,0:T(8,128)S(1)}, u32[]{:S(2)}, u32[]{:S(2)}) collective-permute-start(s32[8,256,256]{2,1,0:T(8,128)S(1)} %get-tuple-element.37.refs_10_.refs_18_), channel_id=1, source_target_pairs={{0,1},{1,0},{2,3},{3,2},{4,5},{5,4},{6,7},{7,6},{8,9},{9,8},{10,11... | collective-permute-start | bytes 6291464 | tf_op jit(solution)/shard_map/ppermute | solution.py:501
  52.1 15.1 %collective-permute-start.12 = (f32[3,64,256]{2,1,0:T(8,128)S(1)}, f32[3,64,256]{2,1,0:T(8,128)S(1)}, u32[]{:S(2)}, u32[]{:S(2)}) collective-permute-start(f32[3,64,256]{2,1,0:T(8,128)S(1)} %get-tuple-element.40.refs_14_.refs_4_.refs_22_), channel_id=1, source_target_pairs={{0,1},{1,0},{2,3},{3,2},{4,5},{5,4},{6,7},{7,6},{8,9},{9,8},{10,11... | collective-permute-start | bytes 589832 | tf_op jit(solution)/shard_map/ppermute | solution.py:501
  56.1 11.6 %collective-permute-start.9 = (f32[4,64,256]{2,1,0:T(8,128)S(1)}, f32[4,64,256]{2,1,0:T(8,128)S(1)}, u32[]{:S(2)}, u32[]{:S(2)}) collective-permute-start(f32[4,64,256]{2,1,0:T(8,128)S(1)} %collective-permute-done.6.refs_4_), channel_id=1, source_target_pairs={{0,6},{1,7},{2,4},{3,5},{4,2},{5,3},{6,0},{7,1},{8,14},{9,15},{10,... | collective-permute-start | bytes 786440 | tf_op jit(solution)/shard_map/ppermute | solution.py:501
  65.8 8.1 %collective-permute-start.8 = (f32[4,64,256]{2,1,0:T(8,128)S(1)}, f32[4,64,256]{2,1,0:T(8,128)S(1)}, u32[]{:S(2)}, u32[]{:S(2)}) collective-permute-start(f32[4,64,256]{2,1,0:T(8,128)S(1)} %collective-permute-done.6.refs_4_), channel_id=1, source_target_pairs={{0,4},{1,5},{2,6},{3,7},{4,0},{5,1},{6,2},{7,3},{8,12},{9,13},{10,... | collective-permute-start | bytes 786440 | tf_op jit(solution)/shard_map/ppermute | solution.py:501
  67.2 7.8 %collective-permute-start.7 = (f32[4,64,256]{2,1,0:T(8,128)S(1)}, f32[4,64,256]{2,1,0:T(8,128)S(1)}, u32[]{:S(2)}, u32[]{:S(2)}) collective-permute-start(f32[4,64,256]{2,1,0:T(8,128)S(1)} %collective-permute-done.6.refs_4_), channel_id=1, source_target_pairs={{0,2},{1,3},{2,0},{3,1},{4,6},{5,7},{6,4},{7,5},{8,10},{9,11},{10,... | collective-permute-start | bytes 786440 | tf_op jit(solution)/shard_map/ppermute | solution.py:501
  67.7 7.3 %collective-permute-start.10 = (f32[256,256]{1,0:T(8,128)S(1)}, f32[256,256]{1,0:T(8,128)S(1)}, u32[]{:S(2)}, u32[]{:S(2)}) collective-permute-start(f32[256,256]{1,0:T(8,128)S(1)} %get-tuple-element.36.refs_8_.refs_16_), channel_id=1, source_target_pairs={{0,1},{1,0},{2,3},{3,2},{4,5},{5,4},{6,7},{7,6},{8,9},{9,8},{10,11... | collective-permute-start | bytes 786440 | tf_op jit(solution)/shard_map/ppermute | solution.py:501
  97.2 7.6 %collective-permute-start.16 = (f32[64,256]{1,0:T(8,128)S(1)}, f32[64,256]{1,0:T(8,128)S(1)}, u32[]{:S(2)}, u32[]{:S(2)}) collective-permute-start(f32[64,256]{1,0:T(8,128)S(1)} %add.42.refs_0_), channel_id=1, source_target_pairs={{0,16},{8,24},{16,0},{24,8},{1,17},{9,25},{17,1},{25,9},{2,18},{10... | collective-permute-start | bytes 196616 | tf_op jit(solution)/shard_map/ppermute | solution.py:508
  108.8 7.5 %collective-permute-start.21 = (f32[72,256]{1,0:T(8,128)S(1)}, f32[72,256]{1,0:T(8,128)S(1)}, u32[]{:S(2)}, u32[]{:S(2)}) collective-permute-start(f32[72,256]{1,0:T(8,128)S(1)} %get-tuple-element.47.refs_8_), channel_id=1, source_target_pairs={{0,1},{1,0},{2,3},{3,2},{4,5},{5,4},{6,7},{7,6},{8,9},{9,8},{10,11... | collective-permute-start | bytes 221192 | tf_op jit(solution)/shard_map/ppermute | solution.py:501
  116.2 77.6 %collective-permute-start.41 = (f32[4,2,64,1024]{3,2,1,0:T(8,128)S(1)}, f32[4,2,64,1024]{3,2,1,0:T(8,128)S(1)}, u32[]{:S(2)}, u32[]{:S(2)}) collective-permute-start(f32[4,2,64,1024]{3,2,1,0:T(8,128)S(1)} %bitcast.34), channel_id=1, source_target_pairs={{0,1},{1,0},{2,3},{3,2},{4,5},{5,4},{6,7},{7,6},{8,9},{9,8},{10,11... | collective-permute-start | bytes 6291464 | tf_op jit(solution)/shard_map/ppermute | solution.py:501
  140.2 53.5 %collective-permute-start.42 = (f32[4,2,64,1024]{3,2,1,0:T(8,128)S(1)}, f32[4,2,64,1024]{3,2,1,0:T(8,128)S(1)}, u32[]{:S(2)}, u32[]{:S(2)}) collective-permute-start(f32[4,2,64,1024]{3,2,1,0:T(8,128)S(1)} %bitcast.35), channel_id=1, source_target_pairs={{0,1},{1,0},{2,3},{3,2},{4,5},{5,4},{6,7},{7,6},{8,9},{9,8},{10,11... | collective-permute-start | bytes 6291464 | tf_op jit(solution)/shard_map/ppermute | solution.py:501
  146.3 7.8 %collective-permute-start.27 = (f32[64,256]{1,0:T(8,128)S(1)}, f32[64,256]{1,0:T(8,128)S(1)}, u32[]{:S(2)}, u32[]{:S(2)}) collective-permute-start(f32[64,256]{1,0:T(8,128)S(1)} %add.43.refs_0_), channel_id=1, source_target_pairs={{0,16},{8,24},{16,0},{24,8},{1,17},{9,25},{17,1},{25,9},{2,18},{10... | collective-permute-start | bytes 196616 | tf_op jit(solution)/shard_map/ppermute | solution.py:508
  146.9 7.2 %collective-permute-start.26 = (f32[64,256]{1,0:T(8,128)S(1)}, f32[64,256]{1,0:T(8,128)S(1)}, u32[]{:S(2)}, u32[]{:S(2)}) collective-permute-start(f32[64,256]{1,0:T(8,128)S(1)} %add.43.refs_0_), channel_id=1, source_target_pairs={{0,8},{8,16},{16,24},{24,0},{1,9},{9,17},{17,25},{25,1},{2,10},{10... | collective-permute-start | bytes 196616 | tf_op jit(solution)/shard_map/ppermute | solution.py:508
  154.2 7.6 %collective-permute-start.31 = (f32[8,256]{1,0:T(8,128)S(1)}, f32[8,256]{1,0:T(8,128)S(1)}, u32[]{:S(2)}, u32[]{:S(2)}) collective-permute-start(f32[8,256]{1,0:T(8,128)S(1)} %last_dots.1), channel_id=1, source_target_pairs={{0,6},{1,7},{2,4},{3,5},{4,2},{5,3},{6,0},{7,1},{8,14},{9,15},{10,... | collective-permute-start | bytes 24584 | tf_op jit(solution)/shard_map/ppermute | solution.py:501
  161.9 8.7 %collective-permute-start.37 = (f32[4,2,64,256]{3,2,1,0:T(8,128)S(1)}, f32[4,2,64,256]{3,2,1,0:T(8,128)S(1)}, u32[]{:S(2)}, u32[]{:S(2)}) collective-permute-start(f32[4,2,64,256]{3,2,1,0:T(8,128)S(1)} %get-tuple-element.55), channel_id=1, source_target_pairs={{0,1},{1,0},{2,3},{3,2},{4,5},{5,4},{6,7},{7,6},{8,9},{9,8},{10,11... | collective-permute-start | bytes 1572872 | tf_op jit(solution)/shard_map/ppermute | solution.py:501
  166.7 8.3 %collective-permute-start.34 = (f32[2,64,256]{2,1,0:T(8,128)S(1)}, f32[2,64,256]{2,1,0:T(8,128)S(1)}, u32[]{:S(2)}, u32[]{:S(2)}) collective-permute-start(f32[2,64,256]{2,1,0:T(8,128)S(1)} %get-tuple-element.69), channel_id=1, source_target_pairs={{0,8},{8,16},{16,24},{24,0},{1,9},{9,17},{17,25},{25,1},{2,10},{10... | collective-permute-start | bytes 393224 | tf_op jit(solution)/shard_map/ppermute | solution.py:626
  166.8 11.0 %collective-permute-start.36 = (f32[2,64,256]{2,1,0:T(8,128)S(1)}, f32[2,64,256]{2,1,0:T(8,128)S(1)}, u32[]{:S(2)}, u32[]{:S(2)}) collective-permute-start(f32[2,64,256]{2,1,0:T(8,128)S(1)} %get-tuple-element.70), channel_id=1, source_target_pairs={{0,24},{8,0},{16,8},{24,16},{1,25},{9,1},{17,9},{25,17},{2,26},{10... | collective-permute-start | bytes 393224 | tf_op jit(solution)/shard_map/ppermute | solution.py:626
  170.6 15.5 %collective-permute-start.35 = (f32[2,64,256]{2,1,0:T(8,128)S(1)}, f32[2,64,256]{2,1,0:T(8,128)S(1)}, u32[]{:S(2)}, u32[]{:S(2)}) collective-permute-start(f32[2,64,256]{2,1,0:T(8,128)S(1)} %get-tuple-element.71), channel_id=1, source_target_pairs={{0,16},{8,24},{16,0},{24,8},{1,17},{9,25},{17,1},{25,9},{2,18},{10... | collective-permute-start | bytes 393224 | tf_op jit(solution)/shard_map/ppermute | solution.py:626
  175.0 11.1 %collective-permute-start.38 = (f32[2,64,256]{2,1,0:T(8,128)S(1)}, f32[2,64,256]{2,1,0:T(8,128)S(1)}, u32[]{:S(2)}, u32[]{:S(2)}) collective-permute-start(f32[2,64,256]{2,1,0:T(8,128)S(1)} %get-tuple-element.66), channel_id=1, source_target_pairs={{0,8},{8,16},{16,24},{24,0},{1,9},{9,17},{17,25},{25,1},{2,10},{10... | collective-permute-start | bytes 393224 | tf_op jit(solution)/shard_map/ppermute | solution.py:626
  177.7 8.9 %collective-permute-start.40 = (f32[2,64,256]{2,1,0:T(8,128)S(1)}, f32[2,64,256]{2,1,0:T(8,128)S(1)}, u32[]{:S(2)}, u32[]{:S(2)}) collective-permute-start(f32[2,64,256]{2,1,0:T(8,128)S(1)} %get-tuple-element.67), channel_id=1, source_target_pairs={{0,24},{8,0},{16,8},{24,16},{1,25},{9,1},{17,9},{25,17},{2,26},{10... | collective-permute-start | bytes 393224 | tf_op jit(solution)/shard_map/ppermute | solution.py:626
  186.1 7.6 %collective-permute-start.39 = (f32[2,64,256]{2,1,0:T(8,128)S(1)}, f32[2,64,256]{2,1,0:T(8,128)S(1)}, u32[]{:S(2)}, u32[]{:S(2)}) collective-permute-start(f32[2,64,256]{2,1,0:T(8,128)S(1)} %get-tuple-element.68), channel_id=1, source_target_pairs={{0,16},{8,24},{16,0},{24,8},{1,17},{9,25},{17,1},{25,9},{2,18},{10... | collective-permute-start | bytes 393224 | tf_op jit(solution)/shard_map/ppermute | solution.py:626
  (26 other events, 147.6 us)

commit v3 on v2

--- a/solution.py
+++ b/solution.py
@@ -53,10 +53,20 @@
     return jnp.dot(a, b, preferred_element_type=F32)
 
 
-def sort_kernel(cell_ref, weight_ref, mask_ref, innovation_ref, out_ref, cell, weight, value):
+def sort_kernel(*refs):
+    sources, (out_ref, cell, weight, value), scratch, sems = refs[:4], refs[4:8], refs[8:12], refs[12]
+    copies = [
+        pltpu.make_async_copy(source, target, sems.at[i])
+        for i, (source, target) in enumerate(zip(sources, scratch))
+    ]
+    for copy in copies:
+        copy.start()
+    for copy in copies:
+        copy.wait()
+    cell_ref, weight_ref, mask_ref, innovation_ref = scratch
     rows, width = cell_ref.shape
-    for scratch in (cell, weight, value):
-        scratch[...] = jnp.zeros(scratch.shape, scratch.dtype)
+    for padded in (cell, weight, value):
+        padded[...] = jnp.zeros(padded.shape, padded.dtype)
     cell[:, :width] = cell_ref[...]
     used = weight_ref[...] * mask_ref[...].astype(F32)
     weight[:, :width] = used
@@ -120,7 +130,7 @@
 
 def observe_kernel(width, nmem, *refs):
     block_refs = refs[:nmem]
-    members_ref, obs_ref, joint_ref, other_ref, members_mine_ref, members_other_ref, blocks = refs[nmem:]
+    members_ref, obs_ref, local_ref, mine_ref, other_ref, members_mine_ref, members_other_ref, blocks = refs[nmem:]
     _, part, _ = block_refs[0].shape
     count, levels, rows, lon = members_ref.shape
     me = lax.axis_index("mem")
@@ -143,8 +153,8 @@
                     total = jnp.where(lane // width == side, raw, total)
                 obs_ref[kind, piece * part : (piece + 1) * part, columns] = total
         cells = obs_ref[0, :, columns].astype(jnp.int32)
-        joint_ref[0, :, columns] = obs_ref[0, :, columns]
-        joint_ref[1, :, columns] = run_totals(cells, obs_ref[2, :, columns], width)
+        local_ref[0, :, columns] = obs_ref[0, :, columns]
+        local_ref[1, :, columns] = run_totals(cells, obs_ref[2, :, columns], width)
 
     step = 8
     half_count = count // 2
@@ -170,7 +180,7 @@
             order += [(1 - parity) * half_count + i for i in range(half_count)]
             outs = pick_cells(cells, [reader(member) for member in order], width, levels, quarter, lon)
             for i in range(half_count):
-                joint_ref[2 + i, here, columns] = outs[i]
+                mine_ref[i, here, columns] = outs[i]
                 other_ref[i, here, columns] = outs[half_count + i]
         return carry
 
@@ -178,23 +188,15 @@
 
 
 def inverse_kernel(width, levels, lon, nblocks_lat, *refs):
-    local_refs, (inverse_ref, value_ref, cells_all, local, sems) = refs[:nblocks_lat], refs[nblocks_lat:]
-    _, _, rows, slots = local.shape
-    copies = [
-        pltpu.make_async_copy(ref.at[pl.ds(0, 2)], local.at[number], sems.at[number])
-        for number, ref in enumerate(local_refs)
-    ]
-    for copy in copies:
-        copy.start()
-    for copy in copies:
-        copy.wait()
+    local_refs, (inverse_ref, value_ref, cells_all) = refs[:nblocks_lat], refs[nblocks_lat:]
+    _, rows, slots = local_refs[0].shape
     nblocks = slots // width
     quarter = lon // nblocks
     per = LANES // width
     tall = 16
     for number in range(nblocks_lat):
-        value_ref[number * rows : (number + 1) * rows, :] = local[number, 1]
-        cells_all[number * rows : (number + 1) * rows, :] = local[number, 0].astype(jnp.int32)
+        value_ref[number * rows : (number + 1) * rows, :] = local_refs[number][1]
+        cells_all[number * rows : (number + 1) * rows, :] = local_refs[number][0].astype(jnp.int32)
 
     def one(index, carry):
         here = pl.ds(pl.multiple_of(index * tall, tall), tall)
@@ -251,10 +253,8 @@
     def rotated(block):
         return lax.rem(block - me_mem + nblocks, nblocks)
 
-    half_blocks = nlat_blocks // 2
     for number, ref in enumerate(seen_refs):
-        for m in range(count):
-            seen[m, number * rows : (number + 1) * rows, :] = ref[m + 2 if number < half_blocks else m]
+        seen[:, number * rows : (number + 1) * rows, :] = ref[...]
     if first:
         for side, ref in enumerate(value_refs):
             value[side * (nlat // 2) : (side + 1) * (nlat // 2), :] = ref[...]
@@ -510,21 +510,25 @@
 
     block = pl.pallas_call(
         sort_kernel,
-        in_specs=[VM] * 4,
+        in_specs=[ANY] * 4,
         out_specs=VM,
         out_shape=shape((3, rows * width // LANES, LANES), F32),
-        scratch_shapes=[pltpu.VMEM((rows, LANES), jnp.int32)] + [pltpu.VMEM((rows, LANES), F32)] * 2,
+        scratch_shapes=[pltpu.VMEM((rows, LANES), jnp.int32)]
+        + [pltpu.VMEM((rows, LANES), F32)] * 2
+        + [pltpu.VMEM(value.shape, value.dtype) for value in (obs_cell, obs_weight, obs_mask, innovation)]
+        + [pltpu.SemaphoreType.DMA((4,))],
         compiler_params=params(2),
         name="sort_slots",
     )(obs_cell, obs_weight, obs_mask, innovation)
     blocks = around_mem(block)
-    obs, joint, other, members_mine, members_sib = pl.pallas_call(
+    obs, local, mine, other, members_mine, members_sib = pl.pallas_call(
         functools.partial(observe_kernel, width, nmem),
         in_specs=[VM] * (nmem + 1),
-        out_specs=[VM] * 5,
+        out_specs=[VM] * 6,
         out_shape=[
             shape((3, rows, slots), F32),
-            shape((2 + half_count, rows, slots), F32),
+            shape((2, rows, slots), F32),
+            shape((half_count, rows, slots), F32),
             shape((half_count, rows, slots), F32),
             shape((half_count, levels, rows, lon), F32),
             shape((half_count, levels, rows, lon), F32),
@@ -535,9 +539,10 @@
         name="members_at_slots",
     )(*blocks, members)
 
+    locals_ = direct(local)
     received = swap(other, 1)
-    joints = direct(joint)
-    seens = joints + direct(received)
+    seens = direct(mine)
+    seens = seens + direct(received)
     obs_sib = swap(obs, 1)
     members_sib = swap(members_sib, 1)
 
@@ -569,18 +574,14 @@
     nchunks = levels * nmem
     inverse, value = pl.pallas_call(
         functools.partial(inverse_kernel, width, levels, lon, nlat_dev // 2),
-        in_specs=[ANY] * (nlat_dev // 2),
+        in_specs=[VM] * (nlat_dev // 2),
         out_specs=[VM] * 2,
         out_shape=[shape((nchunks, nlat // 2, quarter), jnp.int32), shape((nlat // 2, slots), F32)],
-        scratch_shapes=[
-            pltpu.VMEM((nlat // 2, slots), jnp.int32),
-            pltpu.VMEM((nlat_dev // 2, 2, rows, slots), F32),
-            pltpu.SemaphoreType.DMA((nlat_dev // 2,)),
-        ],
+        scratch_shapes=[pltpu.VMEM((nlat // 2, slots), jnp.int32)],
         compiler_params=params(),
         cost_estimate=cost(10**10, 2 * nlat * lon * levels),
         name="inverse",
-    )(*joints)
+    )(*locals_)
     inverses, values = [inverse, swap(inverse, 1)], [value, swap(value, 1)]
 
     tall = half_count * levels * rows

time: 197 us -> 197 us (level)
  waiting for transfers between devices: 66.9 us -> 64.2 us
  starting transfers between devices: 39 us -> 41.5 us
    ppermute x28 -> x31, starting transfers between devices: 16.8 us -> 20.1 us  [swap(): return lax.ppermute(value, 'lat', [(i, i ^ bits) for i in range(nlat_dev)])]
    ppermute x28 -> x31, waiting for transfers between devices: 33 us -> 29.9 us  [swap(): return lax.ppermute(value, 'lat', [(i, i ^ bits) for i in range(nlat_dev)])]
  transfers between devices with their start and end apart: 43 -> 46, of which waited for: 21 -> 22; matrix products, arithmetic and copies ran while one was open for 0% -> 0% of each run, Pallas kernels for 29% -> 29%
where the time goes in v3:
time: 197 us; the launch traced here: 196 us
  Pallas kernels  83.9 us (43%)
  waiting for transfers between devices  64.2 us (33%)
  starting transfers between devices  41.5 us (21%)
  local copies, waits for them, and re-layouts  5.27 us (3%)
    pallas_call x2, Pallas kernels, apply(): pl.pallas_call(functools.partial(apply_kernel, width, levels, nlat_dev, f...  39.7 us
    ppermute x31, waiting for transfers between devices, swap(): return lax.ppermute(value, 'lat', [(i, i ^ bits) for i in range(nlat_dev)])  29.9 us
    ppermute x31, starting transfers between devices, swap(): return lax.ppermute(value, 'lat', [(i, i ^ bits) for i in range(nlat_dev)])  20.1 us
    ppermute x6, waiting for transfers between devices, to_quarters(): lax.ppermute(image[hop], 'mem', [(i, (i + hop) % nmem) for i in range(nme...  19.1 us
    pallas_call x4, Pallas kernels, product(): pl.pallas_call(product_kernel, in_specs=[VM] * 4, out_specs=VM, out_shape...  16 us
    ppermute x9, waiting for transfers between devices, around_mem(): lax.ppermute(value, 'mem', [(i, (i + hop) % nmem) for i in range(nmem)])  15.2 us
    ppermute x9, starting transfers between devices, around_mem(): lax.ppermute(value, 'mem', [(i, (i + hop) % nmem) for i in range(nmem)])  13.7 us
    pallas_call x1, Pallas kernels, per_device(): pl.pallas_call(functools.partial(inverse_kernel, width, levels, lon, nlat...  10.8 us
  transfers between devices with their start and end apart: 46, of which 22 were waited for; matrix products, arithmetic and copies ran while one was open for 0% of the time, Pallas kernels for 29%

profile of v3, /device:TPU:0, one launch (start us, length us, event | category | flops | bytes accessed | tf_op | source)
XLA Modules:
  0.0 196.2 jit_solution(14492883777031335105)
XLA Ops:
  5.5 5.1 %collective-permute-start.2 = (f32[3,32,128]{2,1,0:T(8,128)S(1)}, f32[3,32,128]{2,1,0:T(8,128)S(1)}, u32[]{:S(2)}, u32[]{:S(2)}) collective-permute-start(f32[3,32,128]{2,1,0:T(8,128)S(1)} %sort_slots.1.refs_0_), channel_id=1, source_target_pairs={{0,24},{8,0},{16,8},{24,16},{1,25},{9,1},{17,9},{25,17},{2,26},{10... | collective-permute-start | bytes 147464 | tf_op jit(solution)/shard_map/ppermute | solution.py:508
  12.7 2.9 %collective-permute-done.1.refs_2_ = f32[3,32,128]{2,1,0:T(8,128)S(1)} collective-permute-done((f32[3,32,128]{2,1,0:T(8,128)S(1)}, f32[3,32,128]{2,1,0:T(8,128)S(1)}, u32[]{:S(2)}, u32[]{:S(2)}) %collective-permute-start.1) | collective-permute-done | bytes 49184 | tf_op jit(solution)/shard_map/ppermute | solution.py:508
  24.8 3.8 %collective-permute-done.12.refs_3_ = f32[2,64,256]{2,1,0:T(8,128)S(1)} collective-permute-done((f32[2,64,256]{2,1,0:T(8,128)S(1)}, f32[2,64,256]{2,1,0:T(8,128)S(1)}, u32[]{:S(2)}, u32[]{:S(2)}) %collective-permute-start.12) | collective-permute-done | bytes 131104 | tf_op jit(solution)/shard_map/ppermute | solution.py:501
  29.4 10.8 %inverse.1 = (s32[8,256,256]{2,1,0:T(8,128)S(1)}, f32[256,256]{1,0:T(8,128)S(1)}) custom-call(f32[2,64,256]{2,1,0:T(8,128)S(1)} %get-tuple-element.37.refs_0_, f32[2,64,256]{2,1,0:T(8,128)S(1)} %collective-permute-done.10.refs_1_, f32[2,64,256]{2,1,0:T(8,128)S(1)} %collective-permute-done.11.refs_2_, f32[2,64,256]{2,1,0:T(8,128)S(1)} %collective-permute-done.12.refs_3_), custom_call_target="tpu_custom_call" | custom-call | flops 10000000000 | bytes 2097152 | tf_op jit(solution)/shard_map/inverse/pallas_call | solution.py:575
  42.2 2.9 %collective-permute-done.15.refs_15_.refs_23_ = f32[3,64,256]{2,1,0:T(8,128)S(1)} collective-permute-done((f32[3,64,256]{2,1,0:T(8,128)S(1)}, f32[3,64,256]{2,1,0:T(8,128)S(1)}, u32[]{:S(2)}, u32[]{:S(2)}) %collective-permute-start.15) | collective-permute-done | bytes 196640 | tf_op jit(solution)/shard_map/ppermute | solution.py:501
  47.0 3.8 %collective-permute-done.5.refs_3_ = f32[4,64,256]{2,1,0:T(8,128)S(1)} collective-permute-done((f32[4,64,256]{2,1,0:T(8,128)S(1)}, f32[4,64,256]{2,1,0:T(8,128)S(1)}, u32[]{:S(2)}, u32[]{:S(2)}) %collective-permute-start.5) | collective-permute-done | bytes 262176 | tf_op jit(solution)/shard_map/ppermute | solution.py:501
  50.9 8.0 %lon_covariance.1 = (bf16[1024,1024]{1,0:T(8,128)(2,1)S(1)}, bf16[1024,1024]{1,0:T(8,128)(2,1)S(1)}, bf16[1024,1024]{1,0:T(8,128)(2,1)S(1)}, bf16[1024,1024]{1,0:T(8,128)(2,1)S(1)}) custom-call(f32[1024,1024]{1,0:T(8,128)S(1)} %copy-done.5), custom_call_target="tpu_custom_call" | custom-call | flops 6442450944 | bytes 12582912 | tf_op jit(solution)/shard_map/lon_covariance/pallas_call | solution.py:564
  64.0 5.2 %collective-permute-done.9.refs_7_ = f32[4,64,256]{2,1,0:T(8,128)S(1)} collective-permute-done((f32[4,64,256]{2,1,0:T(8,128)S(1)}, f32[4,64,256]{2,1,0:T(8,128)S(1)}, u32[]{:S(2)}, u32[]{:S(2)}) %collective-permute-start.9) | collective-permute-done | bytes 262176 | tf_op jit(solution)/shard_map/ppermute | solution.py:501
  69.1 5.1 %collective-permute-done.8.refs_6_ = f32[4,64,256]{2,1,0:T(8,128)S(1)} collective-permute-done((f32[4,64,256]{2,1,0:T(8,128)S(1)}, f32[4,64,256]{2,1,0:T(8,128)S(1)}, u32[]{:S(2)}, u32[]{:S(2)}) %collective-permute-start.8) | collective-permute-done | bytes 262176 | tf_op jit(solution)/shard_map/ppermute | solution.py:501
  74.2 19.7 %apply_first.1 = (f32[64,256]{1,0:T(8,128)S(1)}, f32[64,256]{1,0:T(8,128)S(1)}, f32[4,2,64,256]{3,2,1,0:T(8,128)S(1)}, f32[4,2,64,256]{3,2,1,0:T(8,128)S(1)}, bf...) custom-call(f32[4,64,256]{2,1,0:T(8,128)S(1)} %get-tuple-element.35., ...), custom_call_target="tpu_custom_call" | custom-call | flops 9663676416 | bytes 31457280 | tf_op jit(solution)/shard_map/apply_first/pallas_call | solution.py:598
  99.6 4.6 %collective-permute-done.19.refs_2_ = f32[64,256]{1,0:T(8,128)S(1)} collective-permute-done((f32[64,256]{1,0:T(8,128)S(1)}, f32[64,256]{1,0:T(8,128)S(1)}, u32[]{:S(2)}, u32[]{:S(2)}) %collective-permute-start.19) | collective-permute-done | bytes 65568 | tf_op jit(solution)/shard_map/ppermute | solution.py:508
  111.6 4.0 %lon_product.5 = f32[512,1024]{1,0:T(8,128)S(1)} custom-call(bf16[512,1024]{1,0:T(8,128)(2,1)S(1)} %get-tuple-element.62.a_high_ref, bf16[512,1024]{1,0:T(8,128)(2,1)S(1)} %get-tuple-element.63.a_low_ref, bf16[1024,1024]{1,0:T(8,128)(2,1)S(1)} %get-tuple-element.60.b_high_ref, bf16[1024,1024]{1,0:T(8,128)(2,1)S(1)} %get-tuple-element.61.b_low_ref), custom_call_target="tpu_custom_call" | custom-call | flops 3221225472 | bytes 8388608 | tf_op jit(solution)/shard_map/lon_product/pallas_call | solution.py:458
  116.2 20.0 %apply_next.1 = (f32[64,256]{1,0:T(8,128)S(1)}, f32[64,256]{1,0:T(8,128)S(1)}, f32[4,2,64,256]{3,2,1,0:T(8,128)S(1)}, f32[4,2,64,256]{3,2,1,0:T(8,128)S(1)}, bf1...) custom-call(f32[4,64,256]{2,1,0:T(8,128)S(1)} %get-tuple-element.35., ...), custom_call_target="tpu_custom_call" | custom-call | flops 9663676416 | bytes 31457280 | tf_op jit(solution)/shard_map/apply_next/pallas_call | solution.py:598
  136.1 4.0 %lon_product.7 = f32[512,1024]{1,0:T(8,128)S(1)} custom-call(bf16[512,1024]{1,0:T(8,128)(2,1)S(1)} %get-tuple-element.66.a_high_ref, bf16[512,1024]{1,0:T(8,128)(2,1)S(1)} %get-tuple-element.67.a_low_ref, bf16[1024,1024]{1,0:T(8,128)(2,1)S(1)} %get-tuple-element.60.b_high_ref, bf16[1024,1024]{1,0:T(8,128)(2,1)S(1)} %get-tuple-element.61.b_low_ref), custom_call_target="tpu_custom_call" | custom-call | flops 3221225472 | bytes 8388608 | tf_op jit(solution)/shard_map/lon_product/pallas_call | solution.py:458
  140.7 3.7 %collective-permute-done.28 = f32[64,256]{1,0:T(8,128)S(1)} collective-permute-done((f32[64,256]{1,0:T(8,128)S(1)}, f32[64,256]{1,0:T(8,128)S(1)}, u32[]{:S(2)}, u32[]{:S(2)}) %collective-permute-start.28) | collective-permute-done | bytes 65568 | tf_op jit(solution)/shard_map/ppermute | solution.py:501
  148.8 4.7 %collective-permute-done.30.refs_2_ = f32[64,256]{1,0:T(8,128)S(1)} collective-permute-done((f32[64,256]{1,0:T(8,128)S(1)}, f32[64,256]{1,0:T(8,128)S(1)}, u32[]{:S(2)}, u32[]{:S(2)}) %collective-permute-start.30) | collective-permute-done | bytes 65568 | tf_op jit(solution)/shard_map/ppermute | solution.py:508
  157.1 4.0 %lon_product.4 = f32[512,1024]{1,0:T(8,128)S(1)} custom-call(bf16[512,1024]{1,0:T(8,128)(2,1)S(1)} %get-tuple-element.58.a_high_ref, bf16[512,1024]{1,0:T(8,128)(2,1)S(1)} %get-tuple-element.59.a_low_ref, bf16[1024,1024]{1,0:T(8,128)(2,1)S(1)} %get-tuple-element.60.b_high_ref, bf16[1024,1024]{1,0:T(8,128)(2,1)S(1)} %get-tuple-element.61.b_low_ref), custom_call_target="tpu_custom_call" | custom-call | flops 3221225472 | bytes 8388608 | tf_op jit(solution)/shard_map/lon_product/pallas_call | solution.py:458
  161.9 4.0 %lon_product.6 = f32[512,1024]{1,0:T(8,128)S(1)} custom-call(bf16[512,1024]{1,0:T(8,128)(2,1)S(1)} %get-tuple-element.64.a_high_ref, bf16[512,1024]{1,0:T(8,128)(2,1)S(1)} %get-tuple-element.65.a_low_ref, bf16[1024,1024]{1,0:T(8,128)(2,1)S(1)} %get-tuple-element.60.b_high_ref, bf16[1024,1024]{1,0:T(8,128)(2,1)S(1)} %get-tuple-element.61.b_low_ref), custom_call_target="tpu_custom_call" | custom-call | flops 3221225472 | bytes 8388608 | tf_op jit(solution)/shard_map/lon_product/pallas_call | solution.py:458
  166.1 3.8 %collective-permute-start.39 = (f32[2,64,256]{2,1,0:T(8,128)S(1)}, f32[2,64,256]{2,1,0:T(8,128)S(1)}, u32[]{:S(2)}, u32[]{:S(2)}) collective-permute-start(f32[2,64,256]{2,1,0:T(8,128)S(1)} %get-tuple-element.72), channel_id=1, source_target_pairs={{0,24},{8,0},{16,8},{24,16},{1,25},{9,1},{17,9},{25,17},{2,26},{10... | collective-permute-start | bytes 393224 | tf_op jit(solution)/shard_map/ppermute | solution.py:627
  170.0 4.3 %collective-permute-done.37 = f32[2,64,256]{2,1,0:T(8,128)S(1)} collective-permute-done((f32[2,64,256]{2,1,0:T(8,128)S(1)}, f32[2,64,256]{2,1,0:T(8,128)S(1)}, u32[]{:S(2)}, u32[]{:S(2)}) %collective-permute-start.37) | collective-permute-done | bytes 131104 | tf_op jit(solution)/shard_map/ppermute | solution.py:627
  174.3 2.8 %collective-permute-start.41 = (f32[2,64,256]{2,1,0:T(8,128)S(1)}, f32[2,64,256]{2,1,0:T(8,128)S(1)}, u32[]{:S(2)}, u32[]{:S(2)}) collective-permute-start(f32[2,64,256]{2,1,0:T(8,128)S(1)} %get-tuple-element.68), channel_id=1, source_target_pairs={{0,8},{8,16},{16,24},{24,0},{1,9},{9,17},{17,25},{25,1},{2,10},{10... | collective-permute-start | bytes 393224 | tf_op jit(solution)/shard_map/ppermute | solution.py:627
  178.2 7.2 %collective-permute-done.38 = f32[2,64,256]{2,1,0:T(8,128)S(1)} collective-permute-done((f32[2,64,256]{2,1,0:T(8,128)S(1)}, f32[2,64,256]{2,1,0:T(8,128)S(1)}, u32[]{:S(2)}, u32[]{:S(2)}) %collective-permute-start.38) | collective-permute-done | bytes 131104 | tf_op jit(solution)/shard_map/ppermute | solution.py:627
  186.0 7.1 %collective-permute-done.42 = f32[2,64,256]{2,1,0:T(8,128)S(1)} collective-permute-done((f32[2,64,256]{2,1,0:T(8,128)S(1)}, f32[2,64,256]{2,1,0:T(8,128)S(1)}, u32[]{:S(2)}, u32[]{:S(2)}) %collective-permute-start.42) | collective-permute-done | bytes 131104 | tf_op jit(solution)/shard_map/ppermute | solution.py:627
  193.1 2.9 %final.1 = (f32[2,64,256]{2,1,0:T(8,128)}, f32[8,2,64,1024]{3,2,1,0:T(8,128)}) custom-call(f32[8,256]{1,0:T(8,128)S(1)} %add.47.dots_ref, f32[8,128]{1,0:T(8,128)S(1)} %get-tuple-element.53.refs_6_.length_ref, f32[2,64,256]{2,1,0:T(8,128)S(1)} %fusion.5.q0_ref, f32[2,64,256]{2,1,0:T(8,128)S(1)} %fusion.2.q1_ref, f32[4,2,64,1024]{3,2,1,0:T(8,128)S(1)} %bitcast.32, ...), custom_call_target="tpu_custom_call" | custom-call | tf_op jit(solution)/shard_map/final/pallas_call | solution.py:673
  (106 shorter events, 50.6 us)
Async XLA Ops:
  5.5 7.2 %collective-permute-start.2 = (f32[3,32,128]{2,1,0:T(8,128)S(1)}, f32[3,32,128]{2,1,0:T(8,128)S(1)}, u32[]{:S(2)}, u32[]{:S(2)}) collective-permute-start(f32[3,32,128]{2,1,0:T(8,128)S(1)} %sort_slots.1.refs_0_), channel_id=1, source_target_pairs={{0,24},{8,0},{16,8},{24,16},{1,25},{9,1},{17,9},{25,17},{2,26},{10... | collective-permute-start | bytes 147464 | tf_op jit(solution)/shard_map/ppermute | solution.py:508
  21.3 7.3 %collective-permute-start.12 = (f32[2,64,256]{2,1,0:T(8,128)S(1)}, f32[2,64,256]{2,1,0:T(8,128)S(1)}, u32[]{:S(2)}, u32[]{:S(2)}) collective-permute-start(f32[2,64,256]{2,1,0:T(8,128)S(1)} %get-tuple-element.37.refs_0_), channel_id=1, source_target_pairs={{0,6},{1,7},{2,4},{3,5},{4,2},{5,3},{6,0},{7,1},{8,14},{9,15},{10,... | collective-permute-start | bytes 393224 | tf_op jit(solution)/shard_map/ppermute | solution.py:501
  24.8 49.4 %collective-permute-start.16 = (f32[4,2,64,1024]{3,2,1,0:T(8,128)S(1)}, f32[4,2,64,1024]{3,2,1,0:T(8,128)S(1)}, u32[]{:S(2)}, u32[]{:S(2)}) collective-permute-start(f32[4,2,64,1024]{3,2,1,0:T(8,128)S(1)} %get-tuple-element.46), channel_id=1, source_target_pairs={{0,1},{1,0},{2,3},{3,2},{4,5},{5,4},{6,7},{7,6},{8,9},{9,8},{10,11... | collective-permute-start | bytes 6291464 | tf_op jit(solution)/shard_map/ppermute | solution.py:501
  40.2 34.0 %collective-permute-start.14 = (s32[8,256,256]{2,1,0:T(8,128)S(1)}, s32[8,256,256]{2,1,0:T(8,128)S(1)}, u32[]{:S(2)}, u32[]{:S(2)}) collective-permute-start(s32[8,256,256]{2,1,0:T(8,128)S(1)} %get-tuple-element.39.refs_10_.refs_18_), channel_id=1, source_target_pairs={{0,1},{1,0},{2,3},{3,2},{4,5},{5,4},{6,7},{7,6},{8,9},{9,8},{10,11... | collective-permute-start | bytes 6291464 | tf_op jit(solution)/shard_map/ppermute | solution.py:501
  40.8 10.1 %collective-permute-start.5 = (f32[4,64,256]{2,1,0:T(8,128)S(1)}, f32[4,64,256]{2,1,0:T(8,128)S(1)}, u32[]{:S(2)}, u32[]{:S(2)}) collective-permute-start(f32[4,64,256]{2,1,0:T(8,128)S(1)} %get-tuple-element.35.refs_0_), channel_id=1, source_target_pairs={{0,6},{1,7},{2,4},{3,5},{4,2},{5,3},{6,0},{7,1},{8,14},{9,15},{10,... | collective-permute-start | bytes 786440 | tf_op jit(solution)/shard_map/ppermute | solution.py:501
  45.1 13.8 %collective-permute-start.4 = (f32[4,64,256]{2,1,0:T(8,128)S(1)}, f32[4,64,256]{2,1,0:T(8,128)S(1)}, u32[]{:S(2)}, u32[]{:S(2)}) collective-permute-start(f32[4,64,256]{2,1,0:T(8,128)S(1)} %get-tuple-element.35.refs_0_), channel_id=1, source_target_pairs={{0,4},{1,5},{2,6},{3,7},{4,0},{5,1},{6,2},{7,3},{8,12},{9,13},{10,... | collective-permute-start | bytes 786440 | tf_op jit(solution)/shard_map/ppermute | solution.py:501
  46.5 13.9 %collective-permute-start.3 = (f32[4,64,256]{2,1,0:T(8,128)S(1)}, f32[4,64,256]{2,1,0:T(8,128)S(1)}, u32[]{:S(2)}, u32[]{:S(2)}) collective-permute-start(f32[4,64,256]{2,1,0:T(8,128)S(1)} %get-tuple-element.35.refs_0_), channel_id=1, source_target_pairs={{0,2},{1,3},{2,0},{3,1},{4,6},{5,7},{6,4},{7,5},{8,10},{9,11},{10,... | collective-permute-start | bytes 786440 | tf_op jit(solution)/shard_map/ppermute | solution.py:501
  50.9 10.7 %collective-permute-start.13 = (f32[256,256]{1,0:T(8,128)S(1)}, f32[256,256]{1,0:T(8,128)S(1)}, u32[]{:S(2)}, u32[]{:S(2)}) collective-permute-start(f32[256,256]{1,0:T(8,128)S(1)} %get-tuple-element.38.refs_8_.refs_16_), channel_id=1, source_target_pairs={{0,1},{1,0},{2,3},{3,2},{4,5},{5,4},{6,7},{7,6},{8,9},{9,8},{10,11... | collective-permute-start | bytes 786440 | tf_op jit(solution)/shard_map/ppermute | solution.py:501
  58.9 10.2 %collective-permute-start.9 = (f32[4,64,256]{2,1,0:T(8,128)S(1)}, f32[4,64,256]{2,1,0:T(8,128)S(1)}, u32[]{:S(2)}, u32[]{:S(2)}) collective-permute-start(f32[4,64,256]{2,1,0:T(8,128)S(1)} %collective-permute-done.6.refs_4_), channel_id=1, source_target_pairs={{0,6},{1,7},{2,4},{3,5},{4,2},{5,3},{6,0},{7,1},{8,14},{9,15},{10,... | collective-permute-start | bytes 786440 | tf_op jit(solution)/shard_map/ppermute | solution.py:501
  60.3 13.9 %collective-permute-start.8 = (f32[4,64,256]{2,1,0:T(8,128)S(1)}, f32[4,64,256]{2,1,0:T(8,128)S(1)}, u32[]{:S(2)}, u32[]{:S(2)}) collective-permute-start(f32[4,64,256]{2,1,0:T(8,128)S(1)} %collective-permute-done.6.refs_4_), channel_id=1, source_target_pairs={{0,4},{1,5},{2,6},{3,7},{4,0},{5,1},{6,2},{7,3},{8,12},{9,13},{10,... | collective-permute-start | bytes 786440 | tf_op jit(solution)/shard_map/ppermute | solution.py:501
  61.6 12.6 %collective-permute-start.7 = (f32[4,64,256]{2,1,0:T(8,128)S(1)}, f32[4,64,256]{2,1,0:T(8,128)S(1)}, u32[]{:S(2)}, u32[]{:S(2)}) collective-permute-start(f32[4,64,256]{2,1,0:T(8,128)S(1)} %collective-permute-done.6.refs_4_), channel_id=1, source_target_pairs={{0,2},{1,3},{2,0},{3,1},{4,6},{5,7},{6,4},{7,5},{8,10},{9,11},{10,... | collective-permute-start | bytes 786440 | tf_op jit(solution)/shard_map/ppermute | solution.py:501
  96.6 7.6 %collective-permute-start.19 = (f32[64,256]{1,0:T(8,128)S(1)}, f32[64,256]{1,0:T(8,128)S(1)}, u32[]{:S(2)}, u32[]{:S(2)}) collective-permute-start(f32[64,256]{1,0:T(8,128)S(1)} %add.42.refs_0_), channel_id=1, source_target_pairs={{0,16},{8,24},{16,0},{24,8},{1,17},{9,25},{17,1},{25,9},{2,18},{10... | collective-permute-start | bytes 196616 | tf_op jit(solution)/shard_map/ppermute | solution.py:508
  108.2 8.0 %collective-permute-start.24 = (f32[72,256]{1,0:T(8,128)S(1)}, f32[72,256]{1,0:T(8,128)S(1)}, u32[]{:S(2)}, u32[]{:S(2)}) collective-permute-start(f32[72,256]{1,0:T(8,128)S(1)} %get-tuple-element.49.refs_8_), channel_id=1, source_target_pairs={{0,1},{1,0},{2,3},{3,2},{4,5},{5,4},{6,7},{7,6},{8,9},{9,8},{10,11... | collective-permute-start | bytes 221192 | tf_op jit(solution)/shard_map/ppermute | solution.py:501
  115.6 77.5 %collective-permute-start.44 = (f32[4,2,64,1024]{3,2,1,0:T(8,128)S(1)}, f32[4,2,64,1024]{3,2,1,0:T(8,128)S(1)}, u32[]{:S(2)}, u32[]{:S(2)}) collective-permute-start(f32[4,2,64,1024]{3,2,1,0:T(8,128)S(1)} %bitcast.34), channel_id=1, source_target_pairs={{0,1},{1,0},{2,3},{3,2},{4,5},{5,4},{6,7},{7,6},{8,9},{9,8},{10,11... | collective-permute-start | bytes 6291464 | tf_op jit(solution)/shard_map/ppermute | solution.py:501
  140.2 52.9 %collective-permute-start.45 = (f32[4,2,64,1024]{3,2,1,0:T(8,128)S(1)}, f32[4,2,64,1024]{3,2,1,0:T(8,128)S(1)}, u32[]{:S(2)}, u32[]{:S(2)}) collective-permute-start(f32[4,2,64,1024]{3,2,1,0:T(8,128)S(1)} %bitcast.35), channel_id=1, source_target_pairs={{0,1},{1,0},{2,3},{3,2},{4,5},{5,4},{6,7},{7,6},{8,9},{9,8},{10,11... | collective-permute-start | bytes 6291464 | tf_op jit(solution)/shard_map/ppermute | solution.py:501
  145.9 7.6 %collective-permute-start.30 = (f32[64,256]{1,0:T(8,128)S(1)}, f32[64,256]{1,0:T(8,128)S(1)}, u32[]{:S(2)}, u32[]{:S(2)}) collective-permute-start(f32[64,256]{1,0:T(8,128)S(1)} %add.43.refs_0_), channel_id=1, source_target_pairs={{0,16},{8,24},{16,0},{24,8},{1,17},{9,25},{17,1},{25,9},{2,18},{10... | collective-permute-start | bytes 196616 | tf_op jit(solution)/shard_map/ppermute | solution.py:508
  153.6 7.6 %collective-permute-start.34 = (f32[8,256]{1,0:T(8,128)S(1)}, f32[8,256]{1,0:T(8,128)S(1)}, u32[]{:S(2)}, u32[]{:S(2)}) collective-permute-start(f32[8,256]{1,0:T(8,128)S(1)} %last_dots.1), channel_id=1, source_target_pairs={{0,6},{1,7},{2,4},{3,5},{4,2},{5,3},{6,0},{7,1},{8,14},{9,15},{10,... | collective-permute-start | bytes 24584 | tf_op jit(solution)/shard_map/ppermute | solution.py:501
  161.2 8.7 %collective-permute-start.40 = (f32[4,2,64,256]{3,2,1,0:T(8,128)S(1)}, f32[4,2,64,256]{3,2,1,0:T(8,128)S(1)}, u32[]{:S(2)}, u32[]{:S(2)}) collective-permute-start(f32[4,2,64,256]{3,2,1,0:T(8,128)S(1)} %get-tuple-element.57), channel_id=1, source_target_pairs={{0,1},{1,0},{2,3},{3,2},{4,5},{5,4},{6,7},{7,6},{8,9},{9,8},{10,11... | collective-permute-start | bytes 1572872 | tf_op jit(solution)/shard_map/ppermute | solution.py:501
  166.1 8.3 %collective-permute-start.37 = (f32[2,64,256]{2,1,0:T(8,128)S(1)}, f32[2,64,256]{2,1,0:T(8,128)S(1)}, u32[]{:S(2)}, u32[]{:S(2)}) collective-permute-start(f32[2,64,256]{2,1,0:T(8,128)S(1)} %get-tuple-element.71), channel_id=1, source_target_pairs={{0,8},{8,16},{16,24},{24,0},{1,9},{9,17},{17,25},{25,1},{2,10},{10... | collective-permute-start | bytes 393224 | tf_op jit(solution)/shard_map/ppermute | solution.py:627
  166.1 11.0 %collective-permute-start.39 = (f32[2,64,256]{2,1,0:T(8,128)S(1)}, f32[2,64,256]{2,1,0:T(8,128)S(1)}, u32[]{:S(2)}, u32[]{:S(2)}) collective-permute-start(f32[2,64,256]{2,1,0:T(8,128)S(1)} %get-tuple-element.72), channel_id=1, source_target_pairs={{0,24},{8,0},{16,8},{24,16},{1,25},{9,1},{17,9},{25,17},{2,26},{10... | collective-permute-start | bytes 393224 | tf_op jit(solution)/shard_map/ppermute | solution.py:627
  169.9 15.5 %collective-permute-start.38 = (f32[2,64,256]{2,1,0:T(8,128)S(1)}, f32[2,64,256]{2,1,0:T(8,128)S(1)}, u32[]{:S(2)}, u32[]{:S(2)}) collective-permute-start(f32[2,64,256]{2,1,0:T(8,128)S(1)} %get-tuple-element.73), channel_id=1, source_target_pairs={{0,16},{8,24},{16,0},{24,8},{1,17},{9,25},{17,1},{25,9},{2,18},{10... | collective-permute-start | bytes 393224 | tf_op jit(solution)/shard_map/ppermute | solution.py:627
  174.3 11.1 %collective-permute-start.41 = (f32[2,64,256]{2,1,0:T(8,128)S(1)}, f32[2,64,256]{2,1,0:T(8,128)S(1)}, u32[]{:S(2)}, u32[]{:S(2)}) collective-permute-start(f32[2,64,256]{2,1,0:T(8,128)S(1)} %get-tuple-element.68), channel_id=1, source_target_pairs={{0,8},{8,16},{16,24},{24,0},{1,9},{9,17},{17,25},{25,1},{2,10},{10... | collective-permute-start | bytes 393224 | tf_op jit(solution)/shard_map/ppermute | solution.py:627
  177.1 8.9 %collective-permute-start.43 = (f32[2,64,256]{2,1,0:T(8,128)S(1)}, f32[2,64,256]{2,1,0:T(8,128)S(1)}, u32[]{:S(2)}, u32[]{:S(2)}) collective-permute-start(f32[2,64,256]{2,1,0:T(8,128)S(1)} %get-tuple-element.69), channel_id=1, source_target_pairs={{0,24},{8,0},{16,8},{24,16},{1,25},{9,1},{17,9},{25,17},{2,26},{10... | collective-permute-start | bytes 393224 | tf_op jit(solution)/shard_map/ppermute | solution.py:627
  185.4 7.6 %collective-permute-start.42 = (f32[2,64,256]{2,1,0:T(8,128)S(1)}, f32[2,64,256]{2,1,0:T(8,128)S(1)}, u32[]{:S(2)}, u32[]{:S(2)}) collective-permute-start(f32[2,64,256]{2,1,0:T(8,128)S(1)} %get-tuple-element.70), channel_id=1, source_target_pairs={{0,16},{8,24},{16,0},{24,8},{1,17},{9,25},{17,1},{25,9},{2,18},{10... | collective-permute-start | bytes 393224 | tf_op jit(solution)/shard_map/ppermute | solution.py:627
  (29 other events, 153.0 us)

commit v4 on v3

--- a/solution.py
+++ b/solution.py
@@ -223,8 +223,8 @@
 
 
 def apply_kernel(width, levels, nlat_blocks, first, *refs):
-    seen_refs = refs[:nlat_blocks]
-    refs = refs[nlat_blocks:]
+    seen_refs = refs[: nlat_blocks // 2]
+    refs = refs[nlat_blocks // 2 :]
     if not first:
         pay_refs = refs[:nlat_blocks]
         refs = refs[nlat_blocks:]
@@ -253,8 +253,11 @@
     def rotated(block):
         return lax.rem(block - me_mem + nblocks, nblocks)
 
+    half_blocks = nlat_blocks // 2
     for number, ref in enumerate(seen_refs):
-        seen[:, number * rows : (number + 1) * rows, :] = ref[...]
+        for side in range(2):
+            begin = (side * half_blocks + number) * rows
+            seen[:, begin : begin + rows, :] = ref[side * count : (side + 1) * count]
     if first:
         for side, ref in enumerate(value_refs):
             value[side * (nlat // 2) : (side + 1) * (nlat // 2), :] = ref[...]
@@ -541,8 +544,7 @@
 
     locals_ = direct(local)
     received = swap(other, 1)
-    seens = direct(mine)
-    seens = seens + direct(received)
+    seens = direct(jnp.concatenate([mine, received]))
     obs_sib = swap(obs, 1)
     members_sib = swap(members_sib, 1)
 
@@ -597,7 +599,7 @@
             outs.append(shape((8, LANES), F32))
         return pl.pallas_call(
             functools.partial(apply_kernel, width, levels, nlat_dev, first),
-            in_specs=[VM] * (nlat_dev * (1 if first else 2) + 12),
+            in_specs=[VM] * (nlat_dev // 2 + (0 if first else nlat_dev) + 12),
             out_specs=[VM] * len(outs),
             out_shape=outs,
             scratch_shapes=[pltpu.VMEM((half_count, nlat, slots), F32), pltpu.VMEM((nlat, slots), F32)]

time: 197 us -> 193 us (0.980)
  starting transfers between devices: 41.5 us -> 38.7 us
    ppermute x31 -> x28, starting transfers between devices: 20.1 us -> 17.3 us  [swap(): return lax.ppermute(value, 'lat', [(i, i ^ bits) for i in range(nlat_dev)])]
    ppermute x31 -> x28, waiting for transfers between devices: 29.9 us -> 29.4 us  [swap(): return lax.ppermute(value, 'lat', [(i, i ^ bits) for i in range(nlat_dev)])]
    unnamed x14 -> x15, local copies, waits for them, and re-layouts: 5.22 us -> 5.24 us
  transfers between devices with their start and end apart: 46 -> 43, of which waited for: 22 -> 21; matrix products, arithmetic and copies ran while one was open for 0% -> 0% of each run, Pallas kernels for 29% -> 29%
where the time goes in v4:
time: 193 us
  Pallas kernels  83.7 us (43%)
  waiting for transfers between devices  63.8 us (33%)
  starting transfers between devices  38.7 us (20%)
  local copies, waits for them, and re-layouts  5.31 us (3%)
    pallas_call x2, Pallas kernels, apply(): pl.pallas_call(functools.partial(apply_kernel, width, levels, nlat_dev, f...  39.5 us
    ppermute x28, waiting for transfers between devices, swap(): return lax.ppermute(value, 'lat', [(i, i ^ bits) for i in range(nlat_dev)])  29.4 us
    ppermute x6, waiting for transfers between devices, to_quarters(): lax.ppermute(image[hop], 'mem', [(i, (i + hop) % nmem) for i in range(nme...  19.1 us
    ppermute x28, starting transfers between devices, swap(): return lax.ppermute(value, 'lat', [(i, i ^ bits) for i in range(nlat_dev)])  17.3 us
    pallas_call x4, Pallas kernels, product(): pl.pallas_call(product_kernel, in_specs=[VM] * 4, out_specs=VM, out_shape...  16.1 us
    ppermute x9, waiting for transfers between devices, around_mem(): lax.ppermute(value, 'mem', [(i, (i + hop) % nmem) for i in range(nmem)])  15.3 us
    ppermute x9, starting transfers between devices, around_mem(): lax.ppermute(value, 'mem', [(i, (i + hop) % nmem) for i in range(nmem)])  13.6 us
    pallas_call x1, Pallas kernels, per_device(): pl.pallas_call(functools.partial(inverse_kernel, width, levels, lon, nlat...  10.8 us
  transfers between devices with their start and end apart: 43, of which 21 were waited for; matrix products, arithmetic and copies ran while one was open for 0% of the time, Pallas kernels for 29%

profile of v4, /device:TPU:0, one launch (start us, length us, event | category | flops | bytes accessed | tf_op | source)
XLA Modules:
  0.0 192.8 jit_solution(1778882143534873642)
XLA Ops:
  5.5 5.1 %collective-permute-start.2 = (f32[3,32,128]{2,1,0:T(8,128)S(1)}, f32[3,32,128]{2,1,0:T(8,128)S(1)}, u32[]{:S(2)}, u32[]{:S(2)}) collective-permute-start(f32[3,32,128]{2,1,0:T(8,128)S(1)} %sort_slots.1.refs_0_), channel_id=1, source_target_pairs={{0,24},{8,0},{16,8},{24,16},{1,25},{9,1},{17,9},{25,17},{2,26},{10... | collective-permute-start | bytes 147464 | tf_op jit(solution)/shard_map/ppermute | solution.py:511
  12.7 2.9 %collective-permute-done.1.refs_2_ = f32[3,32,128]{2,1,0:T(8,128)S(1)} collective-permute-done((f32[3,32,128]{2,1,0:T(8,128)S(1)}, f32[3,32,128]{2,1,0:T(8,128)S(1)}, u32[]{:S(2)}, u32[]{:S(2)}) %collective-permute-start.1) | collective-permute-done | bytes 49184 | tf_op jit(solution)/shard_map/ppermute | solution.py:511
  18.7 2.6 %members_at_slots.1 = (f32[3,64,256]{2,1,0:T(8,128)S(1)}, f32[2,64,256]{2,1,0:T(8,128)S(1)}, f32[4,64,256]{2,1,0:T(8,128)S(1)}, f32[4,64,256]{2,1,0:T(8,128)S(1)...) custom-call(f32[3,32,128]{2,1,0:T(8,128)S(1)} %sort_slots.1.refs_0_, ...), custom_call_target="tpu_custom_call" | custom-call | flops 100000000 | bytes 4194304 | tf_op jit(solution)/shard_map/members_at_slots/pallas_call | solution.py:527
  21.3 2.5 %collective-permute-start.9 = (f32[2,64,256]{2,1,0:T(8,128)S(1)}, f32[2,64,256]{2,1,0:T(8,128)S(1)}, u32[]{:S(2)}, u32[]{:S(2)}) collective-permute-start(f32[2,64,256]{2,1,0:T(8,128)S(1)} %get-tuple-element.37.refs_0_), channel_id=1, source_target_pairs={{0,6},{1,7},{2,4},{3,5},{4,2},{5,3},{6,0},{7,1},{8,14},{9,15},{10,... | collective-permute-start | bytes 393224 | tf_op jit(solution)/shard_map/ppermute | solution.py:504
  24.8 3.8 %collective-permute-done.9.refs_3_ = f32[2,64,256]{2,1,0:T(8,128)S(1)} collective-permute-done((f32[2,64,256]{2,1,0:T(8,128)S(1)}, f32[2,64,256]{2,1,0:T(8,128)S(1)}, u32[]{:S(2)}, u32[]{:S(2)}) %collective-permute-start.9) | collective-permute-done | bytes 131104 | tf_op jit(solution)/shard_map/ppermute | solution.py:504
  29.4 10.8 %inverse.1 = (s32[8,256,256]{2,1,0:T(8,128)S(1)}, f32[256,256]{1,0:T(8,128)S(1)}) custom-call(f32[2,64,256]{2,1,0:T(8,128)S(1)} %get-tuple-element.37.refs_0_, f32[2,64,256]{2,1,0:T(8,128)S(1)} %collective-permute-done.7.refs_1_, f32[2,64,256]{2,1,0:T(8,128)S(1)} %collective-permute-done.8.refs_2_, f32[2,64,256]{2,1,0:T(8,128)S(1)} %collective-permute-done.9.refs_3_), custom_call_target="tpu_custom_call" | custom-call | flops 10000000000 | bytes 2097152 | tf_op jit(solution)/shard_map/inverse/pallas_call | solution.py:577
  48.4 8.0 %lon_covariance.1 = (bf16[1024,1024]{1,0:T(8,128)(2,1)S(1)}, bf16[1024,1024]{1,0:T(8,128)(2,1)S(1)}, bf16[1024,1024]{1,0:T(8,128)(2,1)S(1)}, bf16[1024,1024]{1,0:T(8,128)(2,1)S(1)}) custom-call(f32[1024,1024]{1,0:T(8,128)S(1)} %copy-done.5), custom_call_target="tpu_custom_call" | custom-call | flops 6442450944 | bytes 12582912 | tf_op jit(solution)/shard_map/lon_covariance/pallas_call | solution.py:566
  56.4 4.2 %collective-permute-done.6.refs_3_ = f32[8,64,256]{2,1,0:T(8,128)S(1)} collective-permute-done((f32[8,64,256]{2,1,0:T(8,128)S(1)}, f32[8,64,256]{2,1,0:T(8,128)S(1)}, u32[]{:S(2)}, u32[]{:S(2)}) %collective-permute-start.6) | collective-permute-done | bytes 524320 | tf_op jit(solution)/shard_map/ppermute | solution.py:504
  60.6 10.4 %collective-permute-done.5.refs_2_ = f32[8,64,256]{2,1,0:T(8,128)S(1)} collective-permute-done((f32[8,64,256]{2,1,0:T(8,128)S(1)}, f32[8,64,256]{2,1,0:T(8,128)S(1)}, u32[]{:S(2)}, u32[]{:S(2)}) %collective-permute-start.5) | collective-permute-done | bytes 524320 | tf_op jit(solution)/shard_map/ppermute | solution.py:504
  71.0 19.7 %apply_first.1 = (f32[64,256]{1,0:T(8,128)S(1)}, f32[64,256]{1,0:T(8,128)S(1)}, f32[4,2,64,256]{3,2,1,0:T(8,128)S(1)}, f32[4,2,64,256]{3,2,1,0:T(8,128)S(1)}, bf...) custom-call(f32[8,64,256]{2,1,0:T(8,128)S(1)} %constant_dynamic-upda, ...), custom_call_target="tpu_custom_call" | custom-call | flops 9663676416 | bytes 31457280 | tf_op jit(solution)/shard_map/apply_first/pallas_call | solution.py:600
  96.3 4.6 %collective-permute-done.16.refs_2_ = f32[64,256]{1,0:T(8,128)S(1)} collective-permute-done((f32[64,256]{1,0:T(8,128)S(1)}, f32[64,256]{1,0:T(8,128)S(1)}, u32[]{:S(2)}, u32[]{:S(2)}) %collective-permute-start.16) | collective-permute-done | bytes 65568 | tf_op jit(solution)/shard_map/ppermute | solution.py:511
  108.2 4.0 %lon_product.5 = f32[512,1024]{1,0:T(8,128)S(1)} custom-call(bf16[512,1024]{1,0:T(8,128)(2,1)S(1)} %get-tuple-element.62.a_high_ref, bf16[512,1024]{1,0:T(8,128)(2,1)S(1)} %get-tuple-element.63.a_low_ref, bf16[1024,1024]{1,0:T(8,128)(2,1)S(1)} %get-tuple-element.60.b_high_ref, bf16[1024,1024]{1,0:T(8,128)(2,1)S(1)} %get-tuple-element.61.b_low_ref), custom_call_target="tpu_custom_call" | custom-call | flops 3221225472 | bytes 8388608 | tf_op jit(solution)/shard_map/lon_product/pallas_call | solution.py:461
  112.9 19.9 %apply_next.1 = (f32[64,256]{1,0:T(8,128)S(1)}, f32[64,256]{1,0:T(8,128)S(1)}, f32[4,2,64,256]{3,2,1,0:T(8,128)S(1)}, f32[4,2,64,256]{3,2,1,0:T(8,128)S(1)}, bf1...) custom-call(f32[8,64,256]{2,1,0:T(8,128)S(1)} %constant_dynamic-upda, ...), custom_call_target="tpu_custom_call" | custom-call | flops 9663676416 | bytes 31457280 | tf_op jit(solution)/shard_map/apply_next/pallas_call | solution.py:600
  132.7 4.0 %lon_product.7 = f32[512,1024]{1,0:T(8,128)S(1)} custom-call(bf16[512,1024]{1,0:T(8,128)(2,1)S(1)} %get-tuple-element.66.a_high_ref, bf16[512,1024]{1,0:T(8,128)(2,1)S(1)} %get-tuple-element.67.a_low_ref, bf16[1024,1024]{1,0:T(8,128)(2,1)S(1)} %get-tuple-element.60.b_high_ref, bf16[1024,1024]{1,0:T(8,128)(2,1)S(1)} %get-tuple-element.61.b_low_ref), custom_call_target="tpu_custom_call" | custom-call | flops 3221225472 | bytes 8388608 | tf_op jit(solution)/shard_map/lon_product/pallas_call | solution.py:461
  137.3 3.7 %collective-permute-done.25 = f32[64,256]{1,0:T(8,128)S(1)} collective-permute-done((f32[64,256]{1,0:T(8,128)S(1)}, f32[64,256]{1,0:T(8,128)S(1)}, u32[]{:S(2)}, u32[]{:S(2)}) %collective-permute-start.25) | collective-permute-done | bytes 65568 | tf_op jit(solution)/shard_map/ppermute | solution.py:504
  145.4 4.7 %collective-permute-done.27.refs_2_ = f32[64,256]{1,0:T(8,128)S(1)} collective-permute-done((f32[64,256]{1,0:T(8,128)S(1)}, f32[64,256]{1,0:T(8,128)S(1)}, u32[]{:S(2)}, u32[]{:S(2)}) %collective-permute-start.27) | collective-permute-done | bytes 65568 | tf_op jit(solution)/shard_map/ppermute | solution.py:511
  153.7 4.0 %lon_product.4 = f32[512,1024]{1,0:T(8,128)S(1)} custom-call(bf16[512,1024]{1,0:T(8,128)(2,1)S(1)} %get-tuple-element.58.a_high_ref, bf16[512,1024]{1,0:T(8,128)(2,1)S(1)} %get-tuple-element.59.a_low_ref, bf16[1024,1024]{1,0:T(8,128)(2,1)S(1)} %get-tuple-element.60.b_high_ref, bf16[1024,1024]{1,0:T(8,128)(2,1)S(1)} %get-tuple-element.61.b_low_ref), custom_call_target="tpu_custom_call" | custom-call | flops 3221225472 | bytes 8388608 | tf_op jit(solution)/shard_map/lon_product/pallas_call | solution.py:461
  158.5 4.0 %lon_product.6 = f32[512,1024]{1,0:T(8,128)S(1)} custom-call(bf16[512,1024]{1,0:T(8,128)(2,1)S(1)} %get-tuple-element.64.a_high_ref, bf16[512,1024]{1,0:T(8,128)(2,1)S(1)} %get-tuple-element.65.a_low_ref, bf16[1024,1024]{1,0:T(8,128)(2,1)S(1)} %get-tuple-element.60.b_high_ref, bf16[1024,1024]{1,0:T(8,128)(2,1)S(1)} %get-tuple-element.61.b_low_ref), custom_call_target="tpu_custom_call" | custom-call | flops 3221225472 | bytes 8388608 | tf_op jit(solution)/shard_map/lon_product/pallas_call | solution.py:461
  162.7 3.8 %collective-permute-start.36 = (f32[2,64,256]{2,1,0:T(8,128)S(1)}, f32[2,64,256]{2,1,0:T(8,128)S(1)}, u32[]{:S(2)}, u32[]{:S(2)}) collective-permute-start(f32[2,64,256]{2,1,0:T(8,128)S(1)} %get-tuple-element.72), channel_id=1, source_target_pairs={{0,24},{8,0},{16,8},{24,16},{1,25},{9,1},{17,9},{25,17},{2,26},{10... | collective-permute-start | bytes 393224 | tf_op jit(solution)/shard_map/ppermute | solution.py:629
  166.6 4.3 %collective-permute-done.34 = f32[2,64,256]{2,1,0:T(8,128)S(1)} collective-permute-done((f32[2,64,256]{2,1,0:T(8,128)S(1)}, f32[2,64,256]{2,1,0:T(8,128)S(1)}, u32[]{:S(2)}, u32[]{:S(2)}) %collective-permute-start.34) | collective-permute-done | bytes 131104 | tf_op jit(solution)/shard_map/ppermute | solution.py:629
  170.9 2.8 %collective-permute-start.38 = (f32[2,64,256]{2,1,0:T(8,128)S(1)}, f32[2,64,256]{2,1,0:T(8,128)S(1)}, u32[]{:S(2)}, u32[]{:S(2)}) collective-permute-start(f32[2,64,256]{2,1,0:T(8,128)S(1)} %get-tuple-element.68), channel_id=1, source_target_pairs={{0,8},{8,16},{16,24},{24,0},{1,9},{9,17},{17,25},{25,1},{2,10},{10... | collective-permute-start | bytes 393224 | tf_op jit(solution)/shard_map/ppermute | solution.py:629
  174.8 7.2 %collective-permute-done.35 = f32[2,64,256]{2,1,0:T(8,128)S(1)} collective-permute-done((f32[2,64,256]{2,1,0:T(8,128)S(1)}, f32[2,64,256]{2,1,0:T(8,128)S(1)}, u32[]{:S(2)}, u32[]{:S(2)}) %collective-permute-start.35) | collective-permute-done | bytes 131104 | tf_op jit(solution)/shard_map/ppermute | solution.py:629
  182.6 7.1 %collective-permute-done.39 = f32[2,64,256]{2,1,0:T(8,128)S(1)} collective-permute-done((f32[2,64,256]{2,1,0:T(8,128)S(1)}, f32[2,64,256]{2,1,0:T(8,128)S(1)}, u32[]{:S(2)}, u32[]{:S(2)}) %collective-permute-start.39) | collective-permute-done | bytes 131104 | tf_op jit(solution)/shard_map/ppermute | solution.py:629
  189.7 2.9 %final.1 = (f32[2,64,256]{2,1,0:T(8,128)}, f32[8,2,64,1024]{3,2,1,0:T(8,128)}) custom-call(f32[8,256]{1,0:T(8,128)S(1)} %add.47.dots_ref, f32[8,128]{1,0:T(8,128)S(1)} %get-tuple-element.53.refs_6_.length_ref, f32[2,64,256]{2,1,0:T(8,128)S(1)} %fusion.5.q0_ref, f32[2,64,256]{2,1,0:T(8,128)S(1)} %fusion.2.q1_ref, f32[4,2,64,1024]{3,2,1,0:T(8,128)S(1)} %bitcast.32, ...), custom_call_target="tpu_custom_call" | custom-call | tf_op jit(solution)/shard_map/final/pallas_call | solution.py:675
  (102 shorter events, 44.7 us)
Async XLA Ops:
  5.5 7.2 %collective-permute-start.2 = (f32[3,32,128]{2,1,0:T(8,128)S(1)}, f32[3,32,128]{2,1,0:T(8,128)S(1)}, u32[]{:S(2)}, u32[]{:S(2)}) collective-permute-start(f32[3,32,128]{2,1,0:T(8,128)S(1)} %sort_slots.1.refs_0_), channel_id=1, source_target_pairs={{0,24},{8,0},{16,8},{24,16},{1,25},{9,1},{17,9},{25,17},{2,26},{10... | collective-permute-start | bytes 147464 | tf_op jit(solution)/shard_map/ppermute | solution.py:511
  21.3 7.3 %collective-permute-start.9 = (f32[2,64,256]{2,1,0:T(8,128)S(1)}, f32[2,64,256]{2,1,0:T(8,128)S(1)}, u32[]{:S(2)}, u32[]{:S(2)}) collective-permute-start(f32[2,64,256]{2,1,0:T(8,128)S(1)} %get-tuple-element.37.refs_0_), channel_id=1, source_target_pairs={{0,6},{1,7},{2,4},{3,5},{4,2},{5,3},{6,0},{7,1},{8,14},{9,15},{10,... | collective-permute-start | bytes 393224 | tf_op jit(solution)/shard_map/ppermute | solution.py:504
  24.8 46.2 %collective-permute-start.13 = (f32[4,2,64,1024]{3,2,1,0:T(8,128)S(1)}, f32[4,2,64,1024]{3,2,1,0:T(8,128)S(1)}, u32[]{:S(2)}, u32[]{:S(2)}) collective-permute-start(f32[4,2,64,1024]{3,2,1,0:T(8,128)S(1)} %get-tuple-element.46), channel_id=1, source_target_pairs={{0,1},{1,0},{2,3},{3,2},{4,5},{5,4},{6,7},{7,6},{8,9},{9,8},{10,11... | collective-permute-start | bytes 6291464 | tf_op jit(solution)/shard_map/ppermute | solution.py:504
  40.2 30.8 %collective-permute-start.11 = (s32[8,256,256]{2,1,0:T(8,128)S(1)}, s32[8,256,256]{2,1,0:T(8,128)S(1)}, u32[]{:S(2)}, u32[]{:S(2)}) collective-permute-start(s32[8,256,256]{2,1,0:T(8,128)S(1)} %get-tuple-element.39.refs_6_.refs_14_), channel_id=1, source_target_pairs={{0,1},{1,0},{2,3},{3,2},{4,5},{5,4},{6,7},{7,6},{8,9},{9,8},{10,11... | collective-permute-start | bytes 6291464 | tf_op jit(solution)/shard_map/ppermute | solution.py:504
  40.8 6.7 %collective-permute-start.10 = (f32[256,256]{1,0:T(8,128)S(1)}, f32[256,256]{1,0:T(8,128)S(1)}, u32[]{:S(2)}, u32[]{:S(2)}) collective-permute-start(f32[256,256]{1,0:T(8,128)S(1)} %get-tuple-element.38.refs_4_.refs_12_), channel_id=1, source_target_pairs={{0,1},{1,0},{2,3},{3,2},{4,5},{5,4},{6,7},{7,6},{8,9},{9,8},{10,11... | collective-permute-start | bytes 786440 | tf_op jit(solution)/shard_map/ppermute | solution.py:504
  44.8 15.8 %collective-permute-start.6 = (f32[8,64,256]{2,1,0:T(8,128)S(1)}, f32[8,64,256]{2,1,0:T(8,128)S(1)}, u32[]{:S(2)}, u32[]{:S(2)}) collective-permute-start(f32[8,64,256]{2,1,0:T(8,128)S(1)} %constant_dynamic-update-slice_fusion.refs_0_), channel_id=1, source_target_pairs={{0,6},{1,7},{2,4},{3,5},{4,2},{5,3},{6,0},{7,1},{8,14},{9,15},{10,... | collective-permute-start | bytes 1572872 | tf_op jit(solution)/shard_map/ppermute | solution.py:504
  46.3 24.7 %collective-permute-start.5 = (f32[8,64,256]{2,1,0:T(8,128)S(1)}, f32[8,64,256]{2,1,0:T(8,128)S(1)}, u32[]{:S(2)}, u32[]{:S(2)}) collective-permute-start(f32[8,64,256]{2,1,0:T(8,128)S(1)} %constant_dynamic-update-slice_fusion.refs_0_), channel_id=1, source_target_pairs={{0,4},{1,5},{2,6},{3,7},{4,0},{5,1},{6,2},{7,3},{8,12},{9,13},{10,... | collective-permute-start | bytes 1572872 | tf_op jit(solution)/shard_map/ppermute | solution.py:504
  47.5 23.5 %collective-permute-start.4 = (f32[8,64,256]{2,1,0:T(8,128)S(1)}, f32[8,64,256]{2,1,0:T(8,128)S(1)}, u32[]{:S(2)}, u32[]{:S(2)}) collective-permute-start(f32[8,64,256]{2,1,0:T(8,128)S(1)} %constant_dynamic-update-slice_fusion.refs_0_), channel_id=1, source_target_pairs={{0,2},{1,3},{2,0},{3,1},{4,6},{5,7},{6,4},{7,5},{8,10},{9,11},{10,... | collective-permute-start | bytes 1572872 | tf_op jit(solution)/shard_map/ppermute | solution.py:504
  93.3 7.6 %collective-permute-start.16 = (f32[64,256]{1,0:T(8,128)S(1)}, f32[64,256]{1,0:T(8,128)S(1)}, u32[]{:S(2)}, u32[]{:S(2)}) collective-permute-start(f32[64,256]{1,0:T(8,128)S(1)} %add.42.refs_0_), channel_id=1, source_target_pairs={{0,16},{8,24},{16,0},{24,8},{1,17},{9,25},{17,1},{25,9},{2,18},{10... | collective-permute-start | bytes 196616 | tf_op jit(solution)/shard_map/ppermute | solution.py:511
  93.7 7.2 %collective-permute-start.15 = (f32[64,256]{1,0:T(8,128)S(1)}, f32[64,256]{1,0:T(8,128)S(1)}, u32[]{:S(2)}, u32[]{:S(2)}) collective-permute-start(f32[64,256]{1,0:T(8,128)S(1)} %add.42.refs_0_), channel_id=1, source_target_pairs={{0,8},{8,16},{16,24},{24,0},{1,9},{9,17},{17,25},{25,1},{2,10},{10... | collective-permute-start | bytes 196616 | tf_op jit(solution)/shard_map/ppermute | solution.py:511
  104.9 7.9 %collective-permute-start.21 = (f32[72,256]{1,0:T(8,128)S(1)}, f32[72,256]{1,0:T(8,128)S(1)}, u32[]{:S(2)}, u32[]{:S(2)}) collective-permute-start(f32[72,256]{1,0:T(8,128)S(1)} %get-tuple-element.49.refs_4_), channel_id=1, source_target_pairs={{0,1},{1,0},{2,3},{3,2},{4,5},{5,4},{6,7},{7,6},{8,9},{9,8},{10,11... | collective-permute-start | bytes 221192 | tf_op jit(solution)/shard_map/ppermute | solution.py:504
  106.7 6.1 %collective-permute-start.24 = (f32[72,256]{1,0:T(8,128)S(1)}, f32[72,256]{1,0:T(8,128)S(1)}, u32[]{:S(2)}, u32[]{:S(2)}) collective-permute-start(f32[72,256]{1,0:T(8,128)S(1)} %collective-permute-done.20.refs_7_), channel_id=1, source_target_pairs={{0,1},{1,0},{2,3},{3,2},{4,5},{5,4},{6,7},{7,6},{8,9},{9,8},{10,11... | collective-permute-start | bytes 221192 | tf_op jit(solution)/shard_map/ppermute | solution.py:504
  112.3 77.4 %collective-permute-start.41 = (f32[4,2,64,1024]{3,2,1,0:T(8,128)S(1)}, f32[4,2,64,1024]{3,2,1,0:T(8,128)S(1)}, u32[]{:S(2)}, u32[]{:S(2)}) collective-permute-start(f32[4,2,64,1024]{3,2,1,0:T(8,128)S(1)} %bitcast.34), channel_id=1, source_target_pairs={{0,1},{1,0},{2,3},{3,2},{4,5},{5,4},{6,7},{7,6},{8,9},{9,8},{10,11... | collective-permute-start | bytes 6291464 | tf_op jit(solution)/shard_map/ppermute | solution.py:504
  136.8 52.9 %collective-permute-start.42 = (f32[4,2,64,1024]{3,2,1,0:T(8,128)S(1)}, f32[4,2,64,1024]{3,2,1,0:T(8,128)S(1)}, u32[]{:S(2)}, u32[]{:S(2)}) collective-permute-start(f32[4,2,64,1024]{3,2,1,0:T(8,128)S(1)} %bitcast.35), channel_id=1, source_target_pairs={{0,1},{1,0},{2,3},{3,2},{4,5},{5,4},{6,7},{7,6},{8,9},{9,8},{10,11... | collective-permute-start | bytes 6291464 | tf_op jit(solution)/shard_map/ppermute | solution.py:504
  142.5 7.6 %collective-permute-start.27 = (f32[64,256]{1,0:T(8,128)S(1)}, f32[64,256]{1,0:T(8,128)S(1)}, u32[]{:S(2)}, u32[]{:S(2)}) collective-permute-start(f32[64,256]{1,0:T(8,128)S(1)} %add.43.refs_0_), channel_id=1, source_target_pairs={{0,16},{8,24},{16,0},{24,8},{1,17},{9,25},{17,1},{25,9},{2,18},{10... | collective-permute-start | bytes 196616 | tf_op jit(solution)/shard_map/ppermute | solution.py:511
  143.0 7.1 %collective-permute-start.26 = (f32[64,256]{1,0:T(8,128)S(1)}, f32[64,256]{1,0:T(8,128)S(1)}, u32[]{:S(2)}, u32[]{:S(2)}) collective-permute-start(f32[64,256]{1,0:T(8,128)S(1)} %add.43.refs_0_), channel_id=1, source_target_pairs={{0,8},{8,16},{16,24},{24,0},{1,9},{9,17},{17,25},{25,1},{2,10},{10... | collective-permute-start | bytes 196616 | tf_op jit(solution)/shard_map/ppermute | solution.py:511
  150.2 7.6 %collective-permute-start.31 = (f32[8,256]{1,0:T(8,128)S(1)}, f32[8,256]{1,0:T(8,128)S(1)}, u32[]{:S(2)}, u32[]{:S(2)}) collective-permute-start(f32[8,256]{1,0:T(8,128)S(1)} %last_dots.1), channel_id=1, source_target_pairs={{0,6},{1,7},{2,4},{3,5},{4,2},{5,3},{6,0},{7,1},{8,14},{9,15},{10,... | collective-permute-start | bytes 24584 | tf_op jit(solution)/shard_map/ppermute | solution.py:504
  157.8 8.7 %collective-permute-start.37 = (f32[4,2,64,256]{3,2,1,0:T(8,128)S(1)}, f32[4,2,64,256]{3,2,1,0:T(8,128)S(1)}, u32[]{:S(2)}, u32[]{:S(2)}) collective-permute-start(f32[4,2,64,256]{3,2,1,0:T(8,128)S(1)} %get-tuple-element.57), channel_id=1, source_target_pairs={{0,1},{1,0},{2,3},{3,2},{4,5},{5,4},{6,7},{7,6},{8,9},{9,8},{10,11... | collective-permute-start | bytes 1572872 | tf_op jit(solution)/shard_map/ppermute | solution.py:504
  162.7 8.3 %collective-permute-start.34 = (f32[2,64,256]{2,1,0:T(8,128)S(1)}, f32[2,64,256]{2,1,0:T(8,128)S(1)}, u32[]{:S(2)}, u32[]{:S(2)}) collective-permute-start(f32[2,64,256]{2,1,0:T(8,128)S(1)} %get-tuple-element.71), channel_id=1, source_target_pairs={{0,8},{8,16},{16,24},{24,0},{1,9},{9,17},{17,25},{25,1},{2,10},{10... | collective-permute-start | bytes 393224 | tf_op jit(solution)/shard_map/ppermute | solution.py:629
  162.7 11.0 %collective-permute-start.36 = (f32[2,64,256]{2,1,0:T(8,128)S(1)}, f32[2,64,256]{2,1,0:T(8,128)S(1)}, u32[]{:S(2)}, u32[]{:S(2)}) collective-permute-start(f32[2,64,256]{2,1,0:T(8,128)S(1)} %get-tuple-element.72), channel_id=1, source_target_pairs={{0,24},{8,0},{16,8},{24,16},{1,25},{9,1},{17,9},{25,17},{2,26},{10... | collective-permute-start | bytes 393224 | tf_op jit(solution)/shard_map/ppermute | solution.py:629
  166.5 15.5 %collective-permute-start.35 = (f32[2,64,256]{2,1,0:T(8,128)S(1)}, f32[2,64,256]{2,1,0:T(8,128)S(1)}, u32[]{:S(2)}, u32[]{:S(2)}) collective-permute-start(f32[2,64,256]{2,1,0:T(8,128)S(1)} %get-tuple-element.73), channel_id=1, source_target_pairs={{0,16},{8,24},{16,0},{24,8},{1,17},{9,25},{17,1},{25,9},{2,18},{10... | collective-permute-start | bytes 393224 | tf_op jit(solution)/shard_map/ppermute | solution.py:629
  170.9 11.1 %collective-permute-start.38 = (f32[2,64,256]{2,1,0:T(8,128)S(1)}, f32[2,64,256]{2,1,0:T(8,128)S(1)}, u32[]{:S(2)}, u32[]{:S(2)}) collective-permute-start(f32[2,64,256]{2,1,0:T(8,128)S(1)} %get-tuple-element.68), channel_id=1, source_target_pairs={{0,8},{8,16},{16,24},{24,0},{1,9},{9,17},{17,25},{25,1},{2,10},{10... | collective-permute-start | bytes 393224 | tf_op jit(solution)/shard_map/ppermute | solution.py:629
  173.7 8.9 %collective-permute-start.40 = (f32[2,64,256]{2,1,0:T(8,128)S(1)}, f32[2,64,256]{2,1,0:T(8,128)S(1)}, u32[]{:S(2)}, u32[]{:S(2)}) collective-permute-start(f32[2,64,256]{2,1,0:T(8,128)S(1)} %get-tuple-element.69), channel_id=1, source_target_pairs={{0,24},{8,0},{16,8},{24,16},{1,25},{9,1},{17,9},{25,17},{2,26},{10... | collective-permute-start | bytes 393224 | tf_op jit(solution)/shard_map/ppermute | solution.py:629
  182.0 7.6 %collective-permute-start.39 = (f32[2,64,256]{2,1,0:T(8,128)S(1)}, f32[2,64,256]{2,1,0:T(8,128)S(1)}, u32[]{:S(2)}, u32[]{:S(2)}) collective-permute-start(f32[2,64,256]{2,1,0:T(8,128)S(1)} %get-tuple-element.70), channel_id=1, source_target_pairs={{0,16},{8,24},{16,0},{24,8},{1,17},{9,25},{17,1},{25,9},{2,18},{10... | collective-permute-start | bytes 393224 | tf_op jit(solution)/shard_map/ppermute | solution.py:629
  (26 other events, 117.8 us)

commit v5 on v3

--- a/solution.py
+++ b/solution.py
@@ -496,12 +496,22 @@
     shape = jax.ShapeDtypeStruct
     chips = list(range(0, nlat_dev, 2))
     order = chips + [bits + 1 for bits in chips]
+    steps = [2**k for k in range(1, (nlat_dev - 1).bit_length())]
 
     def swap(value, bits):
         return lax.ppermute(value, "lat", [(i, i ^ bits) for i in range(nlat_dev)])
 
     def direct(value):
         return [value] + [swap(value, bits) for bits in chips[1:]]
+
+    def relayed(value, hops):
+        blocks = {0: value}
+        for hop in hops:
+            arrived = {}
+            for bits, block in blocks.items():
+                arrived[bits ^ hop] = swap(block, hop)
+            blocks.update(arrived)
+        return [blocks[bits] for bits in chips]
 
     def around_mem(value):
         return [value] + [
@@ -541,8 +551,7 @@
 
     locals_ = direct(local)
     received = swap(other, 1)
-    seens = direct(mine)
-    seens = seens + direct(received)
+    seens = relayed(mine, steps) + relayed(received, steps[::-1])
     obs_sib = swap(obs, 1)
     members_sib = swap(members_sib, 1)
 

time: 197 us -> 194 us (0.985)
  waiting for transfers between devices: 64.2 us -> 61.3 us
    ppermute x31, waiting for transfers between devices: 29.9 us -> 26.8 us  [swap(): return lax.ppermute(value, 'lat', [(i, i ^ bits) for i in range(nlat_dev)])]
where the time goes in v5:
time: 194 us; the launch traced here: 193 us
  Pallas kernels  83.9 us (43%)
  waiting for transfers between devices  61.3 us (32%)
  starting transfers between devices  41.5 us (21%)
  local copies, waits for them, and re-layouts  5.27 us (3%)
    pallas_call x2, Pallas kernels, apply(): pl.pallas_call(functools.partial(apply_kernel, width, levels, nlat_dev, f...  39.7 us
    ppermute x31, waiting for transfers between devices, swap(): return lax.ppermute(value, 'lat', [(i, i ^ bits) for i in range(nlat_dev)])  26.8 us
    ppermute x31, starting transfers between devices, swap(): return lax.ppermute(value, 'lat', [(i, i ^ bits) for i in range(nlat_dev)])  19.8 us
    ppermute x6, waiting for transfers between devices, to_quarters(): lax.ppermute(image[hop], 'mem', [(i, (i + hop) % nmem) for i in range(nme...  19.1 us
    pallas_call x4, Pallas kernels, product(): pl.pallas_call(product_kernel, in_specs=[VM] * 4, out_specs=VM, out_shape...  16 us
    ppermute x9, waiting for transfers between devices, around_mem(): lax.ppermute(value, 'mem', [(i, (i + hop) % nmem) for i in range(nmem)])  15.4 us
    ppermute x9, starting transfers between devices, around_mem(): lax.ppermute(value, 'mem', [(i, (i + hop) % nmem) for i in range(nmem)])  14 us
    pallas_call x1, Pallas kernels, per_device(): pl.pallas_call(functools.partial(inverse_kernel, width, levels, lon, nlat...  10.8 us
  transfers between devices with their start and end apart: 46, of which 22 were waited for; matrix products, arithmetic and copies ran while one was open for 0% of the time, Pallas kernels for 29%

profile of v5, /device:TPU:0, one launch (start us, length us, event | category | flops | bytes accessed | tf_op | source)
XLA Modules:
  0.0 193.3 jit_solution(4407915447023404486)
XLA Ops:
  5.5 5.1 %collective-permute-start.2 = (f32[3,32,128]{2,1,0:T(8,128)S(1)}, f32[3,32,128]{2,1,0:T(8,128)S(1)}, u32[]{:S(2)}, u32[]{:S(2)}) collective-permute-start(f32[3,32,128]{2,1,0:T(8,128)S(1)} %sort_slots.1.refs_0_), channel_id=1, source_target_pairs={{0,24},{8,0},{16,8},{24,16},{1,25},{9,1},{17,9},{25,17},{2,26},{10... | collective-permute-start | bytes 147464 | tf_op jit(solution)/shard_map/ppermute | solution.py:518
  12.7 2.9 %collective-permute-done.1.refs_2_ = f32[3,32,128]{2,1,0:T(8,128)S(1)} collective-permute-done((f32[3,32,128]{2,1,0:T(8,128)S(1)}, f32[3,32,128]{2,1,0:T(8,128)S(1)}, u32[]{:S(2)}, u32[]{:S(2)}) %collective-permute-start.1) | collective-permute-done | bytes 49184 | tf_op jit(solution)/shard_map/ppermute | solution.py:518
  24.8 3.8 %collective-permute-done.12.refs_3_ = f32[2,64,256]{2,1,0:T(8,128)S(1)} collective-permute-done((f32[2,64,256]{2,1,0:T(8,128)S(1)}, f32[2,64,256]{2,1,0:T(8,128)S(1)}, u32[]{:S(2)}, u32[]{:S(2)}) %collective-permute-start.12) | collective-permute-done | bytes 131104 | tf_op jit(solution)/shard_map/ppermute | solution.py:502
  29.4 10.8 %inverse.1 = (s32[8,256,256]{2,1,0:T(8,128)S(1)}, f32[256,256]{1,0:T(8,128)S(1)}) custom-call(f32[2,64,256]{2,1,0:T(8,128)S(1)} %get-tuple-element.37.refs_0_, f32[2,64,256]{2,1,0:T(8,128)S(1)} %collective-permute-done.10.refs_1_, f32[2,64,256]{2,1,0:T(8,128)S(1)} %collective-permute-done.11.refs_2_, f32[2,64,256]{2,1,0:T(8,128)S(1)} %collective-permute-done.12.refs_3_), custom_call_target="tpu_custom_call" | custom-call | flops 10000000000 | bytes 2097152 | tf_op jit(solution)/shard_map/inverse/pallas_call | solution.py:584
  42.2 2.9 %collective-permute-done.15.refs_15_.refs_23_ = f32[3,64,256]{2,1,0:T(8,128)S(1)} collective-permute-done((f32[3,64,256]{2,1,0:T(8,128)S(1)}, f32[3,64,256]{2,1,0:T(8,128)S(1)}, u32[]{:S(2)}, u32[]{:S(2)}) %collective-permute-start.15) | collective-permute-done | bytes 196640 | tf_op jit(solution)/shard_map/ppermute | solution.py:502
  46.2 2.9 %collective-permute-done.4.refs_2_ = f32[4,64,256]{2,1,0:T(8,128)S(1)} collective-permute-done((f32[4,64,256]{2,1,0:T(8,128)S(1)}, f32[4,64,256]{2,1,0:T(8,128)S(1)}, u32[]{:S(2)}, u32[]{:S(2)}) %collective-permute-start.4) | collective-permute-done | bytes 262176 | tf_op jit(solution)/shard_map/ppermute | solution.py:502
  50.5 8.0 %lon_covariance.1 = (bf16[1024,1024]{1,0:T(8,128)(2,1)S(1)}, bf16[1024,1024]{1,0:T(8,128)(2,1)S(1)}, bf16[1024,1024]{1,0:T(8,128)(2,1)S(1)}, bf16[1024,1024]{1,0:T(8,128)(2,1)S(1)}) custom-call(f32[1024,1024]{1,0:T(8,128)S(1)} %copy-done.5), custom_call_target="tpu_custom_call" | custom-call | flops 6442450944 | bytes 12582912 | tf_op jit(solution)/shard_map/lon_covariance/pallas_call | solution.py:573
  62.7 5.0 %collective-permute-done.7.refs_5_ = f32[4,64,256]{2,1,0:T(8,128)S(1)} collective-permute-done((f32[4,64,256]{2,1,0:T(8,128)S(1)}, f32[4,64,256]{2,1,0:T(8,128)S(1)}, u32[]{:S(2)}, u32[]{:S(2)}) %collective-permute-start.7) | collective-permute-done | bytes 262176 | tf_op jit(solution)/shard_map/ppermute | solution.py:502
  67.8 3.6 %collective-permute-done.9.refs_7_ = f32[4,64,256]{2,1,0:T(8,128)S(1)} collective-permute-done((f32[4,64,256]{2,1,0:T(8,128)S(1)}, f32[4,64,256]{2,1,0:T(8,128)S(1)}, u32[]{:S(2)}, u32[]{:S(2)}) %collective-permute-start.9) | collective-permute-done | bytes 262176 | tf_op jit(solution)/shard_map/ppermute | solution.py:502
  71.4 19.7 %apply_first.1 = (f32[64,256]{1,0:T(8,128)S(1)}, f32[64,256]{1,0:T(8,128)S(1)}, f32[4,2,64,256]{3,2,1,0:T(8,128)S(1)}, f32[4,2,64,256]{3,2,1,0:T(8,128)S(1)}, bf...) custom-call(f32[4,64,256]{2,1,0:T(8,128)S(1)} %get-tuple-element.35., ...), custom_call_target="tpu_custom_call" | custom-call | flops 9663676416 | bytes 31457280 | tf_op jit(solution)/shard_map/apply_first/pallas_call | solution.py:607
  96.7 4.5 %collective-permute-done.19.refs_2_ = f32[64,256]{1,0:T(8,128)S(1)} collective-permute-done((f32[64,256]{1,0:T(8,128)S(1)}, f32[64,256]{1,0:T(8,128)S(1)}, u32[]{:S(2)}, u32[]{:S(2)}) %collective-permute-start.19) | collective-permute-done | bytes 65568 | tf_op jit(solution)/shard_map/ppermute | solution.py:518
  108.4 4.0 %lon_product.5 = f32[512,1024]{1,0:T(8,128)S(1)} custom-call(bf16[512,1024]{1,0:T(8,128)(2,1)S(1)} %get-tuple-element.62.a_high_ref, bf16[512,1024]{1,0:T(8,128)(2,1)S(1)} %get-tuple-element.63.a_low_ref, bf16[1024,1024]{1,0:T(8,128)(2,1)S(1)} %get-tuple-element.60.b_high_ref, bf16[1024,1024]{1,0:T(8,128)(2,1)S(1)} %get-tuple-element.61.b_low_ref), custom_call_target="tpu_custom_call" | custom-call | flops 3221225472 | bytes 8388608 | tf_op jit(solution)/shard_map/lon_product/pallas_call | solution.py:458
  112.8 20.0 %apply_next.1 = (f32[64,256]{1,0:T(8,128)S(1)}, f32[64,256]{1,0:T(8,128)S(1)}, f32[4,2,64,256]{3,2,1,0:T(8,128)S(1)}, f32[4,2,64,256]{3,2,1,0:T(8,128)S(1)}, bf1...) custom-call(f32[4,64,256]{2,1,0:T(8,128)S(1)} %get-tuple-element.35., ...), custom_call_target="tpu_custom_call" | custom-call | flops 9663676416 | bytes 31457280 | tf_op jit(solution)/shard_map/apply_next/pallas_call | solution.py:607
  132.8 4.0 %lon_product.7 = f32[512,1024]{1,0:T(8,128)S(1)} custom-call(bf16[512,1024]{1,0:T(8,128)(2,1)S(1)} %get-tuple-element.66.a_high_ref, bf16[512,1024]{1,0:T(8,128)(2,1)S(1)} %get-tuple-element.67.a_low_ref, bf16[1024,1024]{1,0:T(8,128)(2,1)S(1)} %get-tuple-element.60.b_high_ref, bf16[1024,1024]{1,0:T(8,128)(2,1)S(1)} %get-tuple-element.61.b_low_ref), custom_call_target="tpu_custom_call" | custom-call | flops 3221225472 | bytes 8388608 | tf_op jit(solution)/shard_map/lon_product/pallas_call | solution.py:458
  137.4 3.7 %collective-permute-done.28 = f32[64,256]{1,0:T(8,128)S(1)} collective-permute-done((f32[64,256]{1,0:T(8,128)S(1)}, f32[64,256]{1,0:T(8,128)S(1)}, u32[]{:S(2)}, u32[]{:S(2)}) %collective-permute-start.28) | collective-permute-done | bytes 65568 | tf_op jit(solution)/shard_map/ppermute | solution.py:502
  145.4 5.2 %collective-permute-done.30.refs_2_ = f32[64,256]{1,0:T(8,128)S(1)} collective-permute-done((f32[64,256]{1,0:T(8,128)S(1)}, f32[64,256]{1,0:T(8,128)S(1)}, u32[]{:S(2)}, u32[]{:S(2)}) %collective-permute-start.30) | collective-permute-done | bytes 65568 | tf_op jit(solution)/shard_map/ppermute | solution.py:518
  154.2 4.0 %lon_product.4 = f32[512,1024]{1,0:T(8,128)S(1)} custom-call(bf16[512,1024]{1,0:T(8,128)(2,1)S(1)} %get-tuple-element.58.a_high_ref, bf16[512,1024]{1,0:T(8,128)(2,1)S(1)} %get-tuple-element.59.a_low_ref, bf16[1024,1024]{1,0:T(8,128)(2,1)S(1)} %get-tuple-element.60.b_high_ref, bf16[1024,1024]{1,0:T(8,128)(2,1)S(1)} %get-tuple-element.61.b_low_ref), custom_call_target="tpu_custom_call" | custom-call | flops 3221225472 | bytes 8388608 | tf_op jit(solution)/shard_map/lon_product/pallas_call | solution.py:458
  159.0 4.0 %lon_product.6 = f32[512,1024]{1,0:T(8,128)S(1)} custom-call(bf16[512,1024]{1,0:T(8,128)(2,1)S(1)} %get-tuple-element.64.a_high_ref, bf16[512,1024]{1,0:T(8,128)(2,1)S(1)} %get-tuple-element.65.a_low_ref, bf16[1024,1024]{1,0:T(8,128)(2,1)S(1)} %get-tuple-element.60.b_high_ref, bf16[1024,1024]{1,0:T(8,128)(2,1)S(1)} %get-tuple-element.61.b_low_ref), custom_call_target="tpu_custom_call" | custom-call | flops 3221225472 | bytes 8388608 | tf_op jit(solution)/shard_map/lon_product/pallas_call | solution.py:458
  163.2 3.8 %collective-permute-start.39 = (f32[2,64,256]{2,1,0:T(8,128)S(1)}, f32[2,64,256]{2,1,0:T(8,128)S(1)}, u32[]{:S(2)}, u32[]{:S(2)}) collective-permute-start(f32[2,64,256]{2,1,0:T(8,128)S(1)} %get-tuple-element.72), channel_id=1, source_target_pairs={{0,24},{8,0},{16,8},{24,16},{1,25},{9,1},{17,9},{25,17},{2,26},{10... | collective-permute-start | bytes 393224 | tf_op jit(solution)/shard_map/ppermute | solution.py:636
  167.1 4.3 %collective-permute-done.37 = f32[2,64,256]{2,1,0:T(8,128)S(1)} collective-permute-done((f32[2,64,256]{2,1,0:T(8,128)S(1)}, f32[2,64,256]{2,1,0:T(8,128)S(1)}, u32[]{:S(2)}, u32[]{:S(2)}) %collective-permute-start.37) | collective-permute-done | bytes 131104 | tf_op jit(solution)/shard_map/ppermute | solution.py:636
  171.4 2.7 %collective-permute-start.41 = (f32[2,64,256]{2,1,0:T(8,128)S(1)}, f32[2,64,256]{2,1,0:T(8,128)S(1)}, u32[]{:S(2)}, u32[]{:S(2)}) collective-permute-start(f32[2,64,256]{2,1,0:T(8,128)S(1)} %get-tuple-element.68), channel_id=1, source_target_pairs={{0,8},{8,16},{16,24},{24,0},{1,9},{9,17},{17,25},{25,1},{2,10},{10... | collective-permute-start | bytes 393224 | tf_op jit(solution)/shard_map/ppermute | solution.py:636
  175.3 7.2 %collective-permute-done.38 = f32[2,64,256]{2,1,0:T(8,128)S(1)} collective-permute-done((f32[2,64,256]{2,1,0:T(8,128)S(1)}, f32[2,64,256]{2,1,0:T(8,128)S(1)}, u32[]{:S(2)}, u32[]{:S(2)}) %collective-permute-start.38) | collective-permute-done | bytes 131104 | tf_op jit(solution)/shard_map/ppermute | solution.py:636
  183.1 7.1 %collective-permute-done.42 = f32[2,64,256]{2,1,0:T(8,128)S(1)} collective-permute-done((f32[2,64,256]{2,1,0:T(8,128)S(1)}, f32[2,64,256]{2,1,0:T(8,128)S(1)}, u32[]{:S(2)}, u32[]{:S(2)}) %collective-permute-start.42) | collective-permute-done | bytes 131104 | tf_op jit(solution)/shard_map/ppermute | solution.py:636
  190.2 2.9 %final.1 = (f32[2,64,256]{2,1,0:T(8,128)}, f32[8,2,64,1024]{3,2,1,0:T(8,128)}) custom-call(f32[8,256]{1,0:T(8,128)S(1)} %add.47.dots_ref, f32[8,128]{1,0:T(8,128)S(1)} %get-tuple-element.53.refs_6_.length_ref, f32[2,64,256]{2,1,0:T(8,128)S(1)} %fusion.5.q0_ref, f32[2,64,256]{2,1,0:T(8,128)S(1)} %fusion.2.q1_ref, f32[4,2,64,1024]{3,2,1,0:T(8,128)S(1)} %bitcast.32, ...), custom_call_target="tpu_custom_call" | custom-call | tf_op jit(solution)/shard_map/final/pallas_call | solution.py:682
  (106 shorter events, 49.9 us)
Async XLA Ops:
  21.3 7.3 %collective-permute-start.12 = (f32[2,64,256]{2,1,0:T(8,128)S(1)}, f32[2,64,256]{2,1,0:T(8,128)S(1)}, u32[]{:S(2)}, u32[]{:S(2)}) collective-permute-start(f32[2,64,256]{2,1,0:T(8,128)S(1)} %get-tuple-element.37.refs_0_), channel_id=1, source_target_pairs={{0,6},{1,7},{2,4},{3,5},{4,2},{5,3},{6,0},{7,1},{8,14},{9,15},{10,... | collective-permute-start | bytes 393224 | tf_op jit(solution)/shard_map/ppermute | solution.py:502
  24.8 46.5 %collective-permute-start.16 = (f32[4,2,64,1024]{3,2,1,0:T(8,128)S(1)}, f32[4,2,64,1024]{3,2,1,0:T(8,128)S(1)}, u32[]{:S(2)}, u32[]{:S(2)}) collective-permute-start(f32[4,2,64,1024]{3,2,1,0:T(8,128)S(1)} %get-tuple-element.46), channel_id=1, source_target_pairs={{0,1},{1,0},{2,3},{3,2},{4,5},{5,4},{6,7},{7,6},{8,9},{9,8},{10,11... | collective-permute-start | bytes 6291464 | tf_op jit(solution)/shard_map/ppermute | solution.py:502
  40.2 31.2 %collective-permute-start.14 = (s32[8,256,256]{2,1,0:T(8,128)S(1)}, s32[8,256,256]{2,1,0:T(8,128)S(1)}, u32[]{:S(2)}, u32[]{:S(2)}) collective-permute-start(s32[8,256,256]{2,1,0:T(8,128)S(1)} %get-tuple-element.39.refs_10_.refs_18_), channel_id=1, source_target_pairs={{0,1},{1,0},{2,3},{3,2},{4,5},{5,4},{6,7},{7,6},{8,9},{9,8},{10,11... | collective-permute-start | bytes 6291464 | tf_op jit(solution)/shard_map/ppermute | solution.py:502
  40.8 8.3 %collective-permute-start.4 = (f32[4,64,256]{2,1,0:T(8,128)S(1)}, f32[4,64,256]{2,1,0:T(8,128)S(1)}, u32[]{:S(2)}, u32[]{:S(2)}) collective-permute-start(f32[4,64,256]{2,1,0:T(8,128)S(1)} %get-tuple-element.35.refs_0_), channel_id=1, source_target_pairs={{0,4},{1,5},{2,6},{3,7},{4,0},{5,1},{6,2},{7,3},{8,12},{9,13},{10,... | collective-permute-start | bytes 786440 | tf_op jit(solution)/shard_map/ppermute | solution.py:502
  45.1 13.4 %collective-permute-start.3 = (f32[4,64,256]{2,1,0:T(8,128)S(1)}, f32[4,64,256]{2,1,0:T(8,128)S(1)}, u32[]{:S(2)}, u32[]{:S(2)}) collective-permute-start(f32[4,64,256]{2,1,0:T(8,128)S(1)} %get-tuple-element.35.refs_0_), channel_id=1, source_target_pairs={{0,2},{1,3},{2,0},{3,1},{4,6},{5,7},{6,4},{7,5},{8,10},{9,11},{10,... | collective-permute-start | bytes 786440 | tf_op jit(solution)/shard_map/ppermute | solution.py:502
  46.2 12.9 %collective-permute-start.13 = (f32[256,256]{1,0:T(8,128)S(1)}, f32[256,256]{1,0:T(8,128)S(1)}, u32[]{:S(2)}, u32[]{:S(2)}) collective-permute-start(f32[256,256]{1,0:T(8,128)S(1)} %get-tuple-element.38.refs_8_.refs_16_), channel_id=1, source_target_pairs={{0,1},{1,0},{2,3},{3,2},{4,5},{5,4},{6,7},{7,6},{8,9},{9,8},{10,11... | collective-permute-start | bytes 786440 | tf_op jit(solution)/shard_map/ppermute | solution.py:502
  49.1 11.2 %collective-permute-start.8 = (f32[4,64,256]{2,1,0:T(8,128)S(1)}, f32[4,64,256]{2,1,0:T(8,128)S(1)}, u32[]{:S(2)}, u32[]{:S(2)}) collective-permute-start(f32[4,64,256]{2,1,0:T(8,128)S(1)} %collective-permute-done.6.refs_4_), channel_id=1, source_target_pairs={{0,4},{1,5},{2,6},{3,7},{4,0},{5,1},{6,2},{7,3},{8,12},{9,13},{10,... | collective-permute-start | bytes 786440 | tf_op jit(solution)/shard_map/ppermute | solution.py:502
  58.5 9.2 %collective-permute-start.7 = (f32[4,64,256]{2,1,0:T(8,128)S(1)}, f32[4,64,256]{2,1,0:T(8,128)S(1)}, u32[]{:S(2)}, u32[]{:S(2)}) collective-permute-start(f32[4,64,256]{2,1,0:T(8,128)S(1)} %collective-permute-done.6.refs_4_), channel_id=1, source_target_pairs={{0,2},{1,3},{2,0},{3,1},{4,6},{5,7},{6,4},{7,5},{8,10},{9,11},{10,... | collective-permute-start | bytes 786440 | tf_op jit(solution)/shard_map/ppermute | solution.py:502
  59.1 8.6 %collective-permute-start.5 = (f32[4,64,256]{2,1,0:T(8,128)S(1)}, f32[4,64,256]{2,1,0:T(8,128)S(1)}, u32[]{:S(2)}, u32[]{:S(2)}) collective-permute-start(f32[4,64,256]{2,1,0:T(8,128)S(1)} %collective-permute-done.3.refs_1_), channel_id=1, source_target_pairs={{0,4},{1,5},{2,6},{3,7},{4,0},{5,1},{6,2},{7,3},{8,12},{9,13},{10,... | collective-permute-start | bytes 786440 | tf_op jit(solution)/shard_map/ppermute | solution.py:502
  60.3 11.0 %collective-permute-start.9 = (f32[4,64,256]{2,1,0:T(8,128)S(1)}, f32[4,64,256]{2,1,0:T(8,128)S(1)}, u32[]{:S(2)}, u32[]{:S(2)}) collective-permute-start(f32[4,64,256]{2,1,0:T(8,128)S(1)} %collective-permute-done.8.refs_6_), channel_id=1, source_target_pairs={{0,2},{1,3},{2,0},{3,1},{4,6},{5,7},{6,4},{7,5},{8,10},{9,11},{10,... | collective-permute-start | bytes 786440 | tf_op jit(solution)/shard_map/ppermute | solution.py:502
  93.7 7.6 %collective-permute-start.19 = (f32[64,256]{1,0:T(8,128)S(1)}, f32[64,256]{1,0:T(8,128)S(1)}, u32[]{:S(2)}, u32[]{:S(2)}) collective-permute-start(f32[64,256]{1,0:T(8,128)S(1)} %add.42.refs_0_), channel_id=1, source_target_pairs={{0,16},{8,24},{16,0},{24,8},{1,17},{9,25},{17,1},{25,9},{2,18},{10... | collective-permute-start | bytes 196616 | tf_op jit(solution)/shard_map/ppermute | solution.py:518
  105.3 7.5 %collective-permute-start.24 = (f32[72,256]{1,0:T(8,128)S(1)}, f32[72,256]{1,0:T(8,128)S(1)}, u32[]{:S(2)}, u32[]{:S(2)}) collective-permute-start(f32[72,256]{1,0:T(8,128)S(1)} %get-tuple-element.49.refs_8_), channel_id=1, source_target_pairs={{0,1},{1,0},{2,3},{3,2},{4,5},{5,4},{6,7},{7,6},{8,9},{9,8},{10,11... | collective-permute-start | bytes 221192 | tf_op jit(solution)/shard_map/ppermute | solution.py:502
  112.4 77.8 %collective-permute-start.44 = (f32[4,2,64,1024]{3,2,1,0:T(8,128)S(1)}, f32[4,2,64,1024]{3,2,1,0:T(8,128)S(1)}, u32[]{:S(2)}, u32[]{:S(2)}) collective-permute-start(f32[4,2,64,1024]{3,2,1,0:T(8,128)S(1)} %bitcast.34), channel_id=1, source_target_pairs={{0,1},{1,0},{2,3},{3,2},{4,5},{5,4},{6,7},{7,6},{8,9},{9,8},{10,11... | collective-permute-start | bytes 6291464 | tf_op jit(solution)/shard_map/ppermute | solution.py:502
  136.8 53.4 %collective-permute-start.45 = (f32[4,2,64,1024]{3,2,1,0:T(8,128)S(1)}, f32[4,2,64,1024]{3,2,1,0:T(8,128)S(1)}, u32[]{:S(2)}, u32[]{:S(2)}) collective-permute-start(f32[4,2,64,1024]{3,2,1,0:T(8,128)S(1)} %bitcast.35), channel_id=1, source_target_pairs={{0,1},{1,0},{2,3},{3,2},{4,5},{5,4},{6,7},{7,6},{8,9},{9,8},{10,11... | collective-permute-start | bytes 6291464 | tf_op jit(solution)/shard_map/ppermute | solution.py:502
  142.8 7.8 %collective-permute-start.30 = (f32[64,256]{1,0:T(8,128)S(1)}, f32[64,256]{1,0:T(8,128)S(1)}, u32[]{:S(2)}, u32[]{:S(2)}) collective-permute-start(f32[64,256]{1,0:T(8,128)S(1)} %add.43.refs_0_), channel_id=1, source_target_pairs={{0,16},{8,24},{16,0},{24,8},{1,17},{9,25},{17,1},{25,9},{2,18},{10... | collective-permute-start | bytes 196616 | tf_op jit(solution)/shard_map/ppermute | solution.py:518
  143.3 7.2 %collective-permute-start.29 = (f32[64,256]{1,0:T(8,128)S(1)}, f32[64,256]{1,0:T(8,128)S(1)}, u32[]{:S(2)}, u32[]{:S(2)}) collective-permute-start(f32[64,256]{1,0:T(8,128)S(1)} %add.43.refs_0_), channel_id=1, source_target_pairs={{0,8},{8,16},{16,24},{24,0},{1,9},{9,17},{17,25},{25,1},{2,10},{10... | collective-permute-start | bytes 196616 | tf_op jit(solution)/shard_map/ppermute | solution.py:518
  150.7 7.6 %collective-permute-start.34 = (f32[8,256]{1,0:T(8,128)S(1)}, f32[8,256]{1,0:T(8,128)S(1)}, u32[]{:S(2)}, u32[]{:S(2)}) collective-permute-start(f32[8,256]{1,0:T(8,128)S(1)} %last_dots.1), channel_id=1, source_target_pairs={{0,6},{1,7},{2,4},{3,5},{4,2},{5,3},{6,0},{7,1},{8,14},{9,15},{10,... | collective-permute-start | bytes 24584 | tf_op jit(solution)/shard_map/ppermute | solution.py:502
  158.3 8.7 %collective-permute-start.40 = (f32[4,2,64,256]{3,2,1,0:T(8,128)S(1)}, f32[4,2,64,256]{3,2,1,0:T(8,128)S(1)}, u32[]{:S(2)}, u32[]{:S(2)}) collective-permute-start(f32[4,2,64,256]{3,2,1,0:T(8,128)S(1)} %get-tuple-element.57), channel_id=1, source_target_pairs={{0,1},{1,0},{2,3},{3,2},{4,5},{5,4},{6,7},{7,6},{8,9},{9,8},{10,11... | collective-permute-start | bytes 1572872 | tf_op jit(solution)/shard_map/ppermute | solution.py:502
  163.1 8.3 %collective-permute-start.37 = (f32[2,64,256]{2,1,0:T(8,128)S(1)}, f32[2,64,256]{2,1,0:T(8,128)S(1)}, u32[]{:S(2)}, u32[]{:S(2)}) collective-permute-start(f32[2,64,256]{2,1,0:T(8,128)S(1)} %get-tuple-element.71), channel_id=1, source_target_pairs={{0,8},{8,16},{16,24},{24,0},{1,9},{9,17},{17,25},{25,1},{2,10},{10... | collective-permute-start | bytes 393224 | tf_op jit(solution)/shard_map/ppermute | solution.py:636
  163.2 10.9 %collective-permute-start.39 = (f32[2,64,256]{2,1,0:T(8,128)S(1)}, f32[2,64,256]{2,1,0:T(8,128)S(1)}, u32[]{:S(2)}, u32[]{:S(2)}) collective-permute-start(f32[2,64,256]{2,1,0:T(8,128)S(1)} %get-tuple-element.72), channel_id=1, source_target_pairs={{0,24},{8,0},{16,8},{24,16},{1,25},{9,1},{17,9},{25,17},{2,26},{10... | collective-permute-start | bytes 393224 | tf_op jit(solution)/shard_map/ppermute | solution.py:636
  167.0 15.5 %collective-permute-start.38 = (f32[2,64,256]{2,1,0:T(8,128)S(1)}, f32[2,64,256]{2,1,0:T(8,128)S(1)}, u32[]{:S(2)}, u32[]{:S(2)}) collective-permute-start(f32[2,64,256]{2,1,0:T(8,128)S(1)} %get-tuple-element.73), channel_id=1, source_target_pairs={{0,16},{8,24},{16,0},{24,8},{1,17},{9,25},{17,1},{25,9},{2,18},{10... | collective-permute-start | bytes 393224 | tf_op jit(solution)/shard_map/ppermute | solution.py:636
  171.4 11.1 %collective-permute-start.41 = (f32[2,64,256]{2,1,0:T(8,128)S(1)}, f32[2,64,256]{2,1,0:T(8,128)S(1)}, u32[]{:S(2)}, u32[]{:S(2)}) collective-permute-start(f32[2,64,256]{2,1,0:T(8,128)S(1)} %get-tuple-element.68), channel_id=1, source_target_pairs={{0,8},{8,16},{16,24},{24,0},{1,9},{9,17},{17,25},{25,1},{2,10},{10... | collective-permute-start | bytes 393224 | tf_op jit(solution)/shard_map/ppermute | solution.py:636
  174.2 8.9 %collective-permute-start.43 = (f32[2,64,256]{2,1,0:T(8,128)S(1)}, f32[2,64,256]{2,1,0:T(8,128)S(1)}, u32[]{:S(2)}, u32[]{:S(2)}) collective-permute-start(f32[2,64,256]{2,1,0:T(8,128)S(1)} %get-tuple-element.69), channel_id=1, source_target_pairs={{0,24},{8,0},{16,8},{24,16},{1,25},{9,1},{17,9},{25,17},{2,26},{10... | collective-permute-start | bytes 393224 | tf_op jit(solution)/shard_map/ppermute | solution.py:636
  182.5 7.6 %collective-permute-start.42 = (f32[2,64,256]{2,1,0:T(8,128)S(1)}, f32[2,64,256]{2,1,0:T(8,128)S(1)}, u32[]{:S(2)}, u32[]{:S(2)}) collective-permute-start(f32[2,64,256]{2,1,0:T(8,128)S(1)} %get-tuple-element.70), channel_id=1, source_target_pairs={{0,16},{8,24},{16,0},{24,8},{1,17},{9,25},{17,1},{25,9},{2,18},{10... | collective-permute-start | bytes 393224 | tf_op jit(solution)/shard_map/ppermute | solution.py:636
  (29 other events, 155.7 us)
